TPU v7x, 32 devices: a whole 2x2x4 slice. The times are simulated.
32 devices in a mesh: dp: 2 (over core), wide: 4 (over y, x), narrow: 4 (over z).
Axes of the slice: x: 2, y: 2, z: 4, core: 2. Of those that a mesh axis runs over, the one named last changes fastest.
Arguments:
- block_input: float32 [1600, 4096], P('wide', ('dp', 'narrow')), as said below
- block_cotangent: float32 [1600, 4096], P('wide', ('dp', 'narrow')), may hold values from -6 to 6
- seq_start: int32 [32, 128], P(('dp', 'wide', 'narrow')), may hold values from 0 to 127, as said below
- ln1_gain: float32 [1600], P('wide'), may hold values from 0.5 to 1.5
- ln1_shift: float32 [1600], P('wide'), may hold values from -2 to 2
- w_qkv: float32 [1600, 3, 1600], P('wide', None, 'narrow'), may hold values from -0.15625 to 0.15625
- b_qv: float32 [2, 1600], P(None, 'narrow'), may hold values from -3 to 3
- w_out: float32 [1600, 1600], P('wide', 'narrow'), may hold values from -0.4375 to 0.4375
- b_out: float32 [1600], P('wide'), may hold values from -2 to 2
- ln2_gain: float32 [1600], P('wide'), may hold values from 0.5 to 1.5
- ln2_shift: float32 [1600], P('wide'), may hold values from -2 to 2
- w_fc: float32 [1600, 6400], P('wide', 'narrow'), may hold values from -0.15625 to 0.15625
- b_fc: float32 [6400], P('narrow'), may hold values from -3 to 3
- w_proj: float32 [1600, 6400], P('wide', 'narrow'), may hold values from -0.078125 to 0.078125
- b_proj: float32 [1600], P('wide'), may hold values from -2 to 2
Outputs:
- block_output: float32 [1600, 4096], P('wide', ('dp', 'narrow'))
- input_grad: float32 [1600, 4096], P('wide', ('dp', 'narrow'))
- grad_ln1_gain: float32 [1600], P('wide')
- grad_ln1_shift: float32 [1600], P('wide')
- grad_w_qkv: float32 [1600, 3, 1600], P('wide', None, 'narrow')
- grad_b_qv: float32 [2, 1600], P(None, 'narrow')
- grad_w_out: float32 [1600, 1600], P('wide', 'narrow')
- grad_b_out: float32 [1600], P('wide')
- grad_ln2_gain: float32 [1600], P('wide')
- grad_ln2_shift: float32 [1600], P('wide')
- grad_w_fc: float32 [1600, 6400], P('wide', 'narrow')
- grad_b_fc: float32 [6400], P('narrow')
- grad_w_proj: float32 [1600, 6400], P('wide', 'narrow')
- grad_b_proj: float32 [1600], P('wide')
Inputs may be any that keep to these rules, and one draw needn't show every extreme that they name: `block_input`: token activations of order one, with scales that differ from token to token. `seq_start`: along each row the values never fall; each equals the token's own position at the first token of its sequence and the start of its sequence after it. Block 0 holds one sequence of 128 tokens; some block ends with a sequence of one token.
All inputs are finite; a program needn't handle non-finite values.
Results may differ from a plain program's by a relative error of at most 0.011.
Values may be sent and summed in bfloat16 or wider, within the bound.
A program may use at most 320 MiB of HBM per device.

v0:
```python
import math

import jax
import jax.numpy as jnp
from jax import lax
from jax.sharding import PartitionSpec as P

HEADS = 25
HEAD = 64


EPS = 1e-05
GELU_C = math.sqrt(2.0 / math.pi)


def gelu_value(pre_act):
    inner = GELU_C * (pre_act + 0.044715 * pre_act * pre_act * pre_act)
    return 0.5 * pre_act * (1.0 + jnp.tanh(inner))


def gelu_slope(pre_act):
    tanh_part = jnp.tanh(GELU_C * (pre_act + 0.044715 * pre_act * pre_act * pre_act))
    return 0.5 * (1.0 + tanh_part) + 0.5 * pre_act * (1.0 - tanh_part * tanh_part) * GELU_C * (
        1.0 + 3.0 * 0.044715 * pre_act * pre_act
    )


def row_totals(first_term, second_term):
    return lax.psum(
        (jnp.sum(first_term, axis=1, keepdims=True), jnp.sum(second_term, axis=1, keepdims=True)),
        "wide",
    )


def norm_forward(inputs, gain_shard, shift_shard):
    full_width = inputs.shape[1] * lax.axis_size("wide")
    total_sum, square_sum = row_totals(inputs, inputs * inputs)
    mean_row = total_sum / full_width
    inv_std = lax.rsqrt(square_sum / full_width - mean_row * mean_row + EPS)
    normed = (inputs - mean_row) * inv_std
    return (normed, inv_std, (normed * gain_shard + shift_shard).astype(jnp.bfloat16))


def norm_backward(row_grads, normed, inv_std, gain_shard):
    full_width = row_grads.shape[1] * lax.axis_size("wide")
    scaled = row_grads * gain_shard
    first_sum, second_sum = row_totals(scaled, scaled * normed)
    return inv_std * (scaled - first_sum / full_width - normed * (second_sum / full_width))


def gather_narrow(values):
    return lax.all_gather(values, "narrow", axis=0, tiled=True)


def sum_narrow(partial_value):
    return lax.psum_scatter(partial_value, "narrow", scatter_dimension=0, tiled=True)


def sum_wide(gathered, weight_bf, transposed):

    def partial_rows():
        if transposed:
            return lax.dot_general(
                gathered, weight_bf, (((1,), (1,)), ((), ())), preferred_element_type=jnp.float32
            )
        return jnp.dot(gathered, weight_bf, preferred_element_type=jnp.float32)

    return lax.psum_scatter(partial_rows(), "wide", scatter_dimension=0, tiled=True)


def project_wide(activations, weight_bf):
    return sum_narrow(
        jnp.dot(
            lax.all_gather(activations, "wide", axis=0, tiled=True),
            weight_bf,
            preferred_element_type=jnp.float32,
        )
    )


def fold_wide(grad_rows, inputs_all, weight_bf):
    block_rows = lax.all_gather(grad_rows, "wide", axis=0, tiled=True)
    weight_grad = lax.dot_general(
        inputs_all, block_rows, (((0,), (0,)), ((), ())), preferred_element_type=jnp.float32
    )
    back_rows = lax.dot_general(
        block_rows, weight_bf, (((1,), (1,)), ((), ())), preferred_element_type=jnp.float32
    )
    weight_grad, partial_value = (weight_grad, back_rows)
    return (weight_grad, sum_narrow(partial_value))


def weight_grad_block(activations, grads_all):
    return lax.dot_general(
        lax.all_gather(activations, "wide", axis=0, tiled=True),
        grads_all,
        (((0,), (0,)), ((), ())),
        preferred_element_type=jnp.float32,
    )


def to_heads(values):
    return lax.all_to_all(values, "narrow", split_axis=0, concat_axis=2, tiled=True)


def from_heads(values):
    return lax.all_to_all(values, "narrow", split_axis=2, concat_axis=0, tiled=True)


def block_mask(starts):
    position = jnp.arange(starts.shape[0])
    return (position[None, :] <= position[:, None]) & (starts[:, None] == starts[None, :])


def split_heads(values):
    return values.reshape(values.shape[0], HEADS, HEAD)


def attend_forward(heads_all, allowed):
    score_scale = 1.0 / math.sqrt(HEAD)
    queries = split_heads(heads_all[:, 0])
    keys_part = split_heads(heads_all[:, 1])
    values_part = split_heads(heads_all[:, 2])
    scores = (
        jnp.einsum("ihd,jhd->hij", queries, keys_part, preferred_element_type=jnp.float32)
        * score_scale
    )
    log_total = jnp.log(jnp.sum(jnp.where(allowed, jnp.exp(scores), 0.0), axis=2, keepdims=True))
    attn_probs = jnp.where(allowed, jnp.exp(scores - log_total), 0.0).astype(jnp.bfloat16)
    attended = jnp.einsum(
        "hij,jhd->ihd", attn_probs, values_part, preferred_element_type=jnp.float32
    )
    return (attended.reshape(heads_all.shape[0], HEADS * HEAD).astype(jnp.bfloat16), log_total)


def attend_backward(heads_all, allowed, log_total, attended_cot):
    score_scale = 1.0 / math.sqrt(HEAD)
    queries = split_heads(heads_all[:, 0])
    keys_part = split_heads(heads_all[:, 1])
    values_part = split_heads(heads_all[:, 2])
    scores = (
        jnp.einsum("ihd,jhd->hij", queries, keys_part, preferred_element_type=jnp.float32)
        * score_scale
    )
    probs_full = jnp.where(allowed, jnp.exp(scores - log_total), 0.0)
    cot_heads = split_heads(attended_cot)
    dprobs = jnp.einsum("ihd,jhd->hij", cot_heads, values_part, preferred_element_type=jnp.float32)
    row_delta = jnp.sum(probs_full * dprobs, axis=2, keepdims=True)
    score_cot = (probs_full * (dprobs - row_delta) * score_scale).astype(jnp.bfloat16)
    query_grad = jnp.einsum(
        "hij,jhd->ihd", score_cot, keys_part, preferred_element_type=jnp.float32
    )
    key_grad = jnp.einsum("hij,ihd->jhd", score_cot, queries, preferred_element_type=jnp.float32)
    value_grad = jnp.einsum(
        "hij,ihd->jhd",
        probs_full.astype(jnp.bfloat16),
        cot_heads,
        preferred_element_type=jnp.float32,
    )
    stacked = jnp.stack([query_grad, key_grad, value_grad], axis=1)
    return stacked.reshape(heads_all.shape[0], 3, HEADS * HEAD)


def local(
    block_input,
    block_cotangent,
    seq_start,
    ln1_gain,
    ln1_shift,
    w_qkv,
    b_qv,
    w_out,
    b_out,
    ln2_gain,
    ln2_shift,
    w_fc,
    b_fc,
    w_proj,
    b_proj,
):
    narrow_count = lax.axis_size("narrow")
    narrow_index = lax.axis_index("narrow")
    part_width = w_qkv.shape[2]
    hidden_width = w_fc.shape[1]
    rows_input = block_input.T
    rows_cot = block_cotangent.T
    wq_bf = w_qkv.astype(jnp.bfloat16).reshape(w_qkv.shape[0], 3 * part_width)
    wo_bf = w_out.T.astype(jnp.bfloat16)
    wf_bf = w_fc.astype(jnp.bfloat16)
    wp_bf = w_proj.T.astype(jnp.bfloat16)
    bias_three = jnp.stack([b_qv[0], jnp.zeros_like(b_qv[0]), b_qv[1]])
    normed_one, inv_one, norm_one = norm_forward(rows_input, ln1_gain, ln1_shift)
    norm_one_all = gather_narrow(norm_one)
    qkv_rows = sum_wide(norm_one_all, wq_bf, False)
    grid_rows = qkv_rows.shape[0]
    qkv_grid = (qkv_rows.reshape(grid_rows, 3, part_width) + bias_three).astype(jnp.bfloat16)
    heads_all = to_heads(qkv_grid)
    block_rows = heads_all.shape[0]
    allowed = block_mask(seq_start[0])
    attended, log_total = attend_forward(heads_all, allowed)
    attended_grid = from_heads(attended.reshape(block_rows, 1, HEADS * HEAD)).reshape(
        grid_rows, part_width
    )
    residual = rows_input + project_wide(attended_grid, wo_bf) + b_out
    normed_two, inv_two, norm_two = norm_forward(residual, ln2_gain, ln2_shift)
    norm_two_all = gather_narrow(norm_two)
    pre_act = sum_wide(norm_two_all, wf_bf, False) + b_fc
    hidden = gelu_value(pre_act).astype(jnp.bfloat16)
    output_rows = residual + project_wide(hidden, wp_bf) + b_proj
    cot_rows = rows_cot.astype(jnp.bfloat16)
    cot_all = gather_narrow(cot_rows)
    grad_w_proj = weight_grad_block(hidden, cot_all)
    pre_grad = sum_wide(cot_all, wp_bf, True) * gelu_slope(pre_act)
    pre_cot = pre_grad.astype(jnp.bfloat16)
    grad_w_fc, norm_two_grad = fold_wide(pre_cot, norm_two_all, wf_bf)
    resid_grad = rows_cot + norm_backward(norm_two_grad, normed_two, inv_two, ln2_gain)
    resid_cot = resid_grad.astype(jnp.bfloat16)
    resid_all = gather_narrow(resid_cot)
    grad_w_out = weight_grad_block(attended_grid, resid_all)
    attended_cot = sum_wide(resid_all, wo_bf, True).astype(jnp.bfloat16)
    cot_heads = to_heads(attended_cot.reshape(grid_rows, 1, part_width)).reshape(
        block_rows, HEADS * HEAD
    )
    qkv_grad = attend_backward(heads_all, allowed, log_total, cot_heads)
    qkv_cot = from_heads(qkv_grad.astype(jnp.bfloat16))
    grad_w_qkv, norm_one_grad = fold_wide(
        qkv_cot.reshape(grid_rows, 3 * part_width), norm_one_all, wq_bf
    )
    grad_input_rows = resid_grad + norm_backward(norm_one_grad, normed_one, inv_one, ln1_gain)
    qkv_sums = jnp.sum(qkv_grad, axis=0)
    bias_qv_full = jnp.stack([qkv_sums[0], qkv_sums[2]])
    fc_full = jnp.zeros((narrow_count * hidden_width,), jnp.float32)
    fc_full = lax.dynamic_update_slice_in_dim(
        fc_full, jnp.sum(pre_grad, axis=0), narrow_index * hidden_width, 0
    )
    bias_qv_sum, fc_sum = lax.psum((bias_qv_full, fc_full), ("dp", "wide", "narrow"))
    grad_b_qv = lax.dynamic_slice_in_dim(bias_qv_sum, narrow_index * part_width, part_width, 1)
    grad_b_fc = lax.dynamic_slice_in_dim(fc_sum, narrow_index * hidden_width, hidden_width, 0)
    row_terms = (
        jnp.sum(norm_one_grad * normed_one, axis=0),
        jnp.sum(norm_one_grad, axis=0),
        jnp.sum(resid_grad, axis=0),
        jnp.sum(norm_two_grad * normed_two, axis=0),
        jnp.sum(norm_two_grad, axis=0),
        jnp.sum(rows_cot, axis=0),
    )
    gain_one_grad, shift_one_grad, out_bias_grad, gain_two_grad, shift_two_grad, proj_bias_grad = (
        lax.psum(
            (row_terms[0], row_terms[1], row_terms[2], row_terms[3], row_terms[4], row_terms[5]),
            ("dp", "narrow"),
        )
    )
    qkv_total, out_total, fc_total, proj_total = lax.psum(
        (grad_w_qkv.reshape(w_qkv.shape), grad_w_out.T, grad_w_fc, grad_w_proj.T), "dp"
    )
    return (
        output_rows.T,
        grad_input_rows.T,
        gain_one_grad,
        shift_one_grad,
        qkv_total,
        grad_b_qv,
        out_total,
        out_bias_grad,
        gain_two_grad,
        shift_two_grad,
        fc_total,
        grad_b_fc,
        proj_total,
        proj_bias_grad,
    )


def solution(mesh):
    return jax.shard_map(
        local,
        mesh=mesh,
        in_specs=(
            P("wide", ("dp", "narrow")),
            P("wide", ("dp", "narrow")),
            P(("dp", "wide", "narrow"), None),
            P("wide"),
            P("wide"),
            P("wide", None, "narrow"),
            P(None, "narrow"),
            P("wide", "narrow"),
            P("wide"),
            P("wide"),
            P("wide"),
            P("wide", "narrow"),
            P("narrow"),
            P("wide", "narrow"),
            P("wide"),
        ),
        out_specs=(
            P("wide", ("dp", "narrow")),
            P("wide", ("dp", "narrow")),
            P("wide"),
            P("wide"),
            P("wide", None, "narrow"),
            P(None, "narrow"),
            P("wide", "narrow"),
            P("wide"),
            P("wide"),
            P("wide"),
            P("wide", "narrow"),
            P("narrow"),
            P("wide", "narrow"),
            P("wide"),
        ),
        check_vma=False,
    )
```

profile of v0, /device:TPU:17, one launch (start us, length us, event | category | flops | bytes accessed | tf_op | source)
XLA Modules:
  0.0 1332.8 jit_solution(5024976810314251157)
XLA Ops:
  21.5 35.4 %all-gather.9.cloned.1.call-done = bf16[2048,400]{0,1:T(8,128)(2,1)} async-done(((bf16[512,400]{0,1:T(8,128)(2,1)}), bf16[2048,400]{0,1:T(8,128)(2,1)}) %all-gather.9.cloned.1.call-update) | async-done | bytes 1638416 | tf_op jit(solution)/shard_map/all_gather | solution.py:52
  64.3 97.5 %reduce-scatter.9.cloned.1.call-done = f32[512,1200]{0,1:T(8,128)} async-done(((f32[2048,1200]{0,1:T(8,128)}), f32[512,1200]{0,1:T(8,128)}) %reduce-scatter.9.cloned.1.call-update) | async-done | bytes 2457616 | tf_op jit(solution)/shard_map/reduce_scatter | solution.py:68
  172.0 44.1 %all-to-all-done = bf16[512,3,400]{2,1,0:T(4,128)(2,1)S(1)} async-done(((bf16[512,3,400]{2,1,0:T(4,128)(2,1)}), bf16[512,3,400]{2,1,0:T(4,128)(2,1)S(1)}, u32[]{:S(2)}, u32[]{:S(2)}) %all-to-all-start) | async-done | bytes 1228832 | tf_op jit(solution)/shard_map/all_to_all | solution.py:103
  229.2 9.1 reduce.2
  238.4 15.1 %all_to_all.63 = bf16[4,2,25600]{2,1,0:T(2,128)(2,1)S(1)} all-to-all(bf16[4,2,25600]{2,1,0:T(2,128)(2,1)S(1)} %reshape.90), channel_id=1, replica_groups=mesh['dp'=2,'wide'=4,'narrow'=4] {'narrow'}, dimensions={0} | all-to-all | bytes 819200 | tf_op jit(solution)/shard_map/all_to_all | solution.py:107
  255.0 31.7 %all-gather.11.cloned.1.call-done = bf16[2048,400]{0,1:T(8,128)(2,1)} async-done(((bf16[512,400]{0,1:T(8,128)(2,1)}), bf16[2048,400]{0,1:T(8,128)(2,1)}) %all-gather.11.cloned.1.call-update) | async-done | bytes 1638416 | tf_op jit(solution)/shard_map/all_gather | solution.py:74
  292.8 60.7 %reduce-scatter.11.cloned.1.call-done = f32[512,400]{0,1:T(8,128)} async-done(((f32[2048,400]{0,1:T(8,128)}), f32[512,400]{0,1:T(8,128)}) %reduce-scatter.11.cloned.1.call-update) | async-done | bytes 819216 | tf_op jit(solution)/shard_map/reduce_scatter | solution.py:56
  363.9 28.5 %all-gather.17.cloned.1.call-done = bf16[2048,400]{0,1:T(8,128)(2,1)} async-done(((bf16[512,400]{0,1:T(8,128)(2,1)}), bf16[2048,400]{0,1:T(8,128)(2,1)}) %all-gather.17.cloned.1.call-update) | async-done | bytes 1638416 | tf_op jit(solution)/shard_map/all_gather | solution.py:52
  392.4 10.5 fusion.34
  403.0 28.4 %all-gather.13.cloned.1.call-done = bf16[2048,400]{0,1:T(8,128)(2,1)} async-done(((bf16[512,400]{0,1:T(8,128)(2,1)}), bf16[2048,400]{0,1:T(8,128)(2,1)}) %all-gather.13.cloned.1.call-update) | async-done | bytes 1638416 | tf_op jit(solution)/shard_map/all_gather | solution.py:52
  431.4 10.8 fusion.40
  442.3 117.1 %reduce-scatter.17.cloned.1.call-done = f32[512,1600]{0,1:T(8,128)} async-done(((f32[2048,1600]{0,1:T(8,128)}), f32[512,1600]{0,1:T(8,128)}) %reduce-scatter.17.cloned.1.call-update) | async-done | bytes 3276816 | tf_op jit(solution)/shard_map/reduce_scatter | solution.py:68
  559.4 128.0 %reduce-scatter.13.cloned.1.call-done = f32[512,1600]{0,1:T(8,128)} async-done(((f32[2048,1600]{0,1:T(8,128)}), f32[512,1600]{0,1:T(8,128)}) %reduce-scatter.13.cloned.1.call-update) | async-done | bytes 3276816 | tf_op jit(solution)/shard_map/reduce_scatter | solution.py:68
  694.0 71.6 %all-gather.19.cloned.1.call-done = bf16[2048,1600]{0,1:T(8,128)(2,1)} async-done(((bf16[512,1600]{0,1:T(8,128)(2,1)}), bf16[2048,1600]{0,1:T(8,128)(2,1)}) %all-gather.19.cloned.1.call-update) | async-done | bytes 6553616 | tf_op jit(solution)/shard_map/all_gather | solution.py:82
  774.3 65.6 %all-gather.15.cloned.1.call-done = bf16[2048,1600]{0,1:T(8,128)(2,1)} async-done(((bf16[512,1600]{0,1:T(8,128)(2,1)}), bf16[2048,1600]{0,1:T(8,128)(2,1)}) %all-gather.15.cloned.1.call-update) | async-done | bytes 6553616 | tf_op jit(solution)/shard_map/all_gather | solution.py:74
  839.9 8.5 fusion.36
  848.5 56.3 %reduce-scatter.19.cloned.1.call-done = f32[512,400]{0,1:T(8,128)} async-done(((f32[2048,400]{0,1:T(8,128)}), f32[512,400]{0,1:T(8,128)}) %reduce-scatter.19.cloned.1.call-update) | async-done | bytes 819216 | tf_op jit(solution)/shard_map/reduce_scatter | solution.py:56
  914.2 55.3 %reduce-scatter.15.cloned.1.call-done = f32[512,400]{0,1:T(8,128)} async-done(((f32[2048,400]{0,1:T(8,128)}), f32[512,400]{0,1:T(8,128)}) %reduce-scatter.15.cloned.1.call-update) | async-done | bytes 819216 | tf_op jit(solution)/shard_map/reduce_scatter | solution.py:56
  973.8 37.0 %all-gather.21.cloned.1.call-done = bf16[2048,400]{0,1:T(8,128)(2,1)} async-done(((bf16[512,400]{0,1:T(8,128)(2,1)}), bf16[2048,400]{0,1:T(8,128)(2,1)}) %all-gather.21.cloned.1.call-update) | async-done | bytes 1638416 | tf_op jit(solution)/shard_map/all_gather | solution.py:52
  1015.0 45.1 %reduce-scatter.21.cloned.1.call-done = f32[512,400]{0,1:T(8,128)} async-done(((f32[2048,400]{0,1:T(8,128)}), f32[512,400]{0,1:T(8,128)}) %reduce-scatter.21.cloned.1.call-update) | async-done | bytes 819216 | tf_op jit(solution)/shard_map/reduce_scatter | solution.py:68
  1096.8 42.4 %all_to_all.64 = bf16[128,3,1600]{0,1,2:T(4,128)(2,1)S(1)} all-to-all(bf16[128,3,1600]{0,1,2:T(4,128)(2,1)S(1)} %fusion.9), channel_id=1, replica_groups=mesh['dp'=2,'wide'=4,'narrow'=4] {'narrow'}, dimensions={2} | all-to-all | bytes 2457600 | tf_op jit(solution)/shard_map/all_to_all | solution.py:107
  1141.6 58.8 %all-gather.23.cloned.1.call-done = bf16[2048,1200]{0,1:T(8,128)(2,1)} async-done(((bf16[512,1200]{0,1:T(8,128)(2,1)}), bf16[2048,1200]{0,1:T(8,128)(2,1)}) %all-gather.23.cloned.1.call-update) | async-done | bytes 4915216 | tf_op jit(solution)/shard_map/all_gather | solution.py:82
  1235.2 42.1 %all-reduce = (f32[2,1600]{1,0:T(2,128)S(1)}, f32[6400]{0:T(1024)S(1)}) all-reduce(f32[2,1600]{1,0:T(2,128)S(1)} %pad_maximum_fusion.1, f32[6400]{0:T(1024)S(1)} %dynamic_update_slice.3), channel_id=1, replica_groups=mesh['dp'=2,'wide'=4,'narrow'=4] {'dp','wide','narrow'}, use_global_device_ids=true, to_apply=%region_32.33 | all-reduce | flops 9600 | bytes 76800 | tf_op jit(solution)/shard_map/psum | solution.py:236
  1288.1 28.4 %all-reduce.1 = (f32[400]{0:T(512)}, f32[400]{0:T(512)}, f32[400]{0:T(512)}, f32[400]{0:T(512)}, f32[400]{0:T(512)}, /*index=5*/f32[400]{0:T(512)}) all-reduce(f32[400]{0:T(512)S(1)} %get-tuple-element.114, f32[400]{0:T(512)S(1)} %get-tuple-element.119, ...), channel_id=1, replica_groups=mesh['dp'=2,'wide'=4,'narrow'=4] {'dp','narrow'}, use_global_device_ids=true, to_apply=%region_27.28 | all-reduce | flops 2400 | bytes 19200 | tf_op jit(solution)/shard_map/psum | solution.py:248
  (185 shorter events, 190.2 us)
Async XLA Ops:
  7.2 49.6 %all-gather.9.cloned.1.call-start = ((), (), s32[]{:S(2)}) async-start(), calls=%async_computation.12 | async-start | bytes 2048000 | tf_op jit(solution)/shard_map/all_gather | solution.py:52
  18.7 143.1 %reduce-scatter.9.cloned.1.call-start = ((), (), s32[]{:S(2)}) async-start(), calls=%async_computation.13 | async-start | bytes 12288000 | tf_op jit(solution)/shard_map/reduce_scatter | solution.py:68
  166.6 49.5 %all-to-all-start = ((bf16[512,3,400]{2,1,0:T(4,128)(2,1)}), bf16[512,3,400]{2,1,0:T(4,128)(2,1)S(1)}, u32[]{:S(2)}, u32[]{:S(2)}) async-start(bf16[512,3,400]{2,1,0:T(4,128)(2,1)} %copy.135), calls=%async_computation.1 | async-start | bytes 4194304 | tf_op jit(solution)/shard_map/all_to_all | solution.py:103
  171.3 115.3 %all-gather.11.cloned.1.call-start = ((), (), s32[]{:S(2)}) async-start(), calls=%async_computation.14 | async-start | bytes 2048000 | tf_op jit(solution)/shard_map/all_gather | solution.py:74
  254.9 98.6 %reduce-scatter.11.cloned.1.call-start = ((), (), s32[]{:S(2)}) async-start(), calls=%async_computation.15 | async-start | bytes 4096000 | tf_op jit(solution)/shard_map/reduce_scatter | solution.py:56
  290.8 62.7 %copy-start.28 = (f32[400]{0:T(512)S(1)}, f32[400]{0:T(512)}, u32[]{:S(2)}) copy-start(f32[400]{0:T(512)} %param.23) | copy-start | bytes 4804
  290.8 101.6 %all-gather.17.cloned.1.call-start = ((), (), s32[]{:S(2)}) async-start(), calls=%async_computation.20 | async-start | bytes 2048000 | tf_op jit(solution)/shard_map/all_gather | solution.py:52
  292.7 70.0 %copy-start.19 = (f32[400]{0:T(512)S(1)}, f32[400]{0:T(512)}, u32[]{:S(2)}) copy-start(f32[400]{0:T(512)} %param.24) | copy-start | bytes 4804
  292.7 70.0 %copy-start.25 = (f32[400]{0:T(512)S(1)}, f32[400]{0:T(512)}, u32[]{:S(2)}) copy-start(f32[400]{0:T(512)} %param.25) | copy-start | bytes 4804
  292.8 138.6 %all-gather.13.cloned.1.call-start = ((), (), s32[]{:S(2)}) async-start(), calls=%async_computation.16 | async-start | bytes 2048000 | tf_op jit(solution)/shard_map/all_gather | solution.py:52
  363.7 195.7 %reduce-scatter.17.cloned.1.call-start = ((), (), s32[]{:S(2)}) async-start(), calls=%async_computation.21 | async-start | bytes 16384000 | tf_op jit(solution)/shard_map/reduce_scatter | solution.py:68
  402.9 284.5 %reduce-scatter.13.cloned.1.call-start = ((), (), s32[]{:S(2)}) async-start(), calls=%async_computation.17 | async-start | bytes 16384000 | tf_op jit(solution)/shard_map/reduce_scatter | solution.py:68
  442.2 245.3 %copy-start.21 = (f32[1600]{0:T(1024)S(1)}, f32[1600]{0:T(1024)}, u32[]{:S(2)}) copy-start(f32[1600]{0:T(1024)} %param.27) | copy-start | bytes 19204
  442.2 323.4 %all-gather.19.cloned.1.call-start = ((), (), s32[]{:S(2)}) async-start(), calls=%async_computation.22 | async-start | bytes 8192000 | tf_op jit(solution)/shard_map/all_gather | solution.py:82
  693.4 146.6 %all-gather.15.cloned.1.call-start = ((), (), s32[]{:S(2)}) async-start(), calls=%async_computation.18 | async-start | bytes 8192000 | tf_op jit(solution)/shard_map/all_gather | solution.py:74
  694.0 210.9 %reduce-scatter.19.cloned.1.call-start = ((), (), s32[]{:S(2)}) async-start(), calls=%async_computation.23 | async-start | bytes 4096000 | tf_op jit(solution)/shard_map/reduce_scatter | solution.py:56
  774.1 195.4 %reduce-scatter.15.cloned.1.call-start = ((), (), s32[]{:S(2)}) async-start(), calls=%async_computation.19 | async-start | bytes 4096000 | tf_op jit(solution)/shard_map/reduce_scatter | solution.py:56
  848.5 121.0 %copy-start.26 = (f32[400]{0:T(512)S(1)}, f32[400]{0:T(512)}, u32[]{:S(2)}) copy-start(f32[400]{0:T(512)} %param.29) | copy-start | bytes 4804
  848.5 162.3 %all-gather.21.cloned.1.call-start = ((), (), s32[]{:S(2)}) async-start(), calls=%async_computation.24 | async-start | bytes 2048000 | tf_op jit(solution)/shard_map/all_gather | solution.py:52
  973.8 86.3 %reduce-scatter.21.cloned.1.call-start = ((), (), s32[]{:S(2)}) async-start(), calls=%async_computation.25 | async-start | bytes 4096000 | tf_op jit(solution)/shard_map/reduce_scatter | solution.py:68
  1065.9 11.9 all-to-all-start.2
  1070.5 129.8 %all-gather.23.cloned.1.call-start = ((), (), s32[]{:S(2)}) async-start(), calls=%async_computation.26 | async-start | bytes 6144000 | tf_op jit(solution)/shard_map/all_gather | solution.py:82
  1141.1 137.4 %reduce-scatter.23.cloned.1.call-start = ((), (), s32[]{:S(2)}) async-start(), calls=%async_computation.27 | async-start | bytes 4096000 | tf_op jit(solution)/shard_map/reduce_scatter | solution.py:56
  1207.1 110.5 %all-reduce.9.cloned.1.call-start = ((), (), s32[]{:S(2)}) async-start(), calls=%async_computation.28 | async-start | bytes 17203200 | tf_op jit(solution)/shard_map/psum | solution.py:253
  (28 other events, 296.6 us)
Sparse Core Ops, SparseCore 0:
  18.8 37.9 all-gather.8
  63.7 98.0 reduce-scatter.8
  255.0 31.5 all-gather.10
  290.9 62.5 reduce-scatter.10
  355.5 36.8 all-gather.16
  394.4 36.9 all-gather.12
  434.5 124.8 reduce-scatter.16
  562.6 124.8 reduce-scatter.12
  693.5 72.0 all-gather.18
  767.8 72.0 all-gather.14
  842.3 62.5 reduce-scatter.18
  907.0 62.4 reduce-scatter.14
  973.9 36.8 all-gather.20
  1015.1 44.9 reduce-scatter.20
  1141.2 59.0 all-gather.22
  1207.2 63.4 reduce-scatter.22
  1274.6 39.2 all-reduce.8
where the time goes:
time: 1340 us; the launch traced here: 1330 us
  waiting for transfers between devices  967 us (72%)
  blocking collectives  159 us (12%)
  matrix products  97.9 us (7%)
  other arithmetic  45 us (3%)
  local copies, waits for them, and re-layouts  37.6 us (3%)
  between operations  14.6 us (1%)
    reduce_scatter x4, waiting for transfers between devices, sum_wide(): lax.psum_scatter(partial_rows(), 'wide', scatter_dimension=0, tiled=True)  388 us
    reduce_scatter x4, waiting for transfers between devices, sum_narrow(): lax.psum_scatter(partial_value, 'narrow', scatter_dimension=0, tiled=True)  172 us
    all_gather x2, waiting for transfers between devices, fold_wide(): block_rows = lax.all_gather(grad_rows, 'wide', axis=0, tiled=True)  130 us
    all_gather x4, waiting for transfers between devices, gather_narrow(): return lax.all_gather(values, 'narrow', axis=0, tiled=True)  129 us
    all_gather x2, waiting for transfers between devices, project_wide(): lax.all_gather(activations, 'wide', axis=0, tiled=True)  97.3 us
    all_to_all x2, blocking collectives, from_heads(): lax.all_to_all(values, 'narrow', split_axis=2, concat_axis=0, tiled=True)  57.5 us
    all_to_all x2, waiting for transfers between devices, to_heads(): lax.all_to_all(values, 'narrow', split_axis=0, concat_axis=2, tiled=True)  49.3 us
    psum x1, blocking collectives, local(): lax.psum((bias_qv_full, fc_full), ('dp', 'wide', 'narrow'))  42.1 us
  transfers between devices with their start and end apart: 19, of which 17 were waited for; matrix products, arithmetic and copies ran while one was open for 6% of the time, Pallas kernels for 0%

commit v1 on v0

v1 whole, which is shorter than its diff:
```python
import math

import jax
import jax.numpy as jnp
from jax import lax
from jax.sharding import PartitionSpec as P

HEADS = 25
HEAD = 64

EPS = 1e-05
GELU_C = math.sqrt(2.0 / math.pi)
BF = jnp.bfloat16
F32 = jnp.float32
ZC = ("narrow", "dp")


def gelu_value(pre_act):
    inner = GELU_C * (pre_act + 0.044715 * pre_act * pre_act * pre_act)
    return 0.5 * pre_act * (1.0 + jnp.tanh(inner))


def gelu_slope(pre_act):
    tanh_part = jnp.tanh(GELU_C * (pre_act + 0.044715 * pre_act * pre_act * pre_act))
    return 0.5 * (1.0 + tanh_part) + 0.5 * pre_act * (1.0 - tanh_part * tanh_part) * GELU_C * (
        1.0 + 3.0 * 0.044715 * pre_act * pre_act
    )


def dot(a, b, ca, cb):
    return lax.dot_general(a, b, (((ca,), (cb,)), ((), ())), preferred_element_type=F32)


def row_totals(first_term, second_term):
    return lax.psum(
        (jnp.sum(first_term, axis=1, keepdims=True), jnp.sum(second_term, axis=1, keepdims=True)),
        "wide",
    )


def norm_forward(inputs, gain_shard, shift_shard):
    full_width = inputs.shape[1] * lax.axis_size("wide")
    total_sum, square_sum = row_totals(inputs, inputs * inputs)
    mean_row = total_sum / full_width
    inv_std = lax.rsqrt(square_sum / full_width - mean_row * mean_row + EPS)
    normed = (inputs - mean_row) * inv_std
    return (normed, inv_std, (normed * gain_shard + shift_shard).astype(BF))


def norm_backward(row_grads, normed, inv_std, gain_shard):
    full_width = row_grads.shape[1] * lax.axis_size("wide")
    scaled = row_grads * gain_shard
    first_sum, second_sum = row_totals(scaled, scaled * normed)
    return inv_std * (scaled - first_sum / full_width - normed * (second_sum / full_width))


def gather_features(values):
    return lax.all_gather(values, "wide", axis=1, tiled=True)


def gather_tokens(values):
    return lax.all_gather(values, "wide", axis=0, tiled=True)


def sum_features(partial_value):
    return lax.psum_scatter(partial_value.astype(BF), "wide", scatter_dimension=1, tiled=True).astype(F32)


def sum_tokens(partial_value):
    return lax.psum_scatter(partial_value.astype(BF), "wide", scatter_dimension=0, tiled=True).astype(F32)


def block_mask(starts):
    position = jnp.arange(starts.shape[0])
    return (position[None, :] <= position[:, None]) & (starts[:, None] == starts[None, :])


def split_heads(values):
    return values.reshape(values.shape[0], HEADS, HEAD)


def attend_forward(heads_all, allowed):
    score_scale = 1.0 / math.sqrt(HEAD)
    queries = split_heads(heads_all[:, 0])
    keys_part = split_heads(heads_all[:, 1])
    values_part = split_heads(heads_all[:, 2])
    scores = jnp.einsum("ihd,jhd->hij", queries, keys_part, preferred_element_type=F32) * score_scale
    log_total = jnp.log(jnp.sum(jnp.where(allowed, jnp.exp(scores), 0.0), axis=2, keepdims=True))
    attn_probs = jnp.where(allowed, jnp.exp(scores - log_total), 0.0).astype(BF)
    attended = jnp.einsum("hij,jhd->ihd", attn_probs, values_part, preferred_element_type=F32)
    return (attended.reshape(heads_all.shape[0], HEADS * HEAD).astype(BF), log_total)


def attend_backward(heads_all, allowed, log_total, attended_cot):
    score_scale = 1.0 / math.sqrt(HEAD)
    queries = split_heads(heads_all[:, 0])
    keys_part = split_heads(heads_all[:, 1])
    values_part = split_heads(heads_all[:, 2])
    scores = jnp.einsum("ihd,jhd->hij", queries, keys_part, preferred_element_type=F32) * score_scale
    probs_full = jnp.where(allowed, jnp.exp(scores - log_total), 0.0)
    cot_heads = split_heads(attended_cot)
    dprobs = jnp.einsum("ihd,jhd->hij", cot_heads, values_part, preferred_element_type=F32)
    row_delta = jnp.sum(probs_full * dprobs, axis=2, keepdims=True)
    score_cot = (probs_full * (dprobs - row_delta) * score_scale).astype(BF)
    query_grad = jnp.einsum("hij,jhd->ihd", score_cot, keys_part, preferred_element_type=F32)
    key_grad = jnp.einsum("hij,ihd->jhd", score_cot, queries, preferred_element_type=F32)
    value_grad = jnp.einsum("hij,ihd->jhd", probs_full.astype(BF), cot_heads, preferred_element_type=F32)
    stacked = jnp.stack([query_grad, key_grad, value_grad], axis=1)
    return stacked.reshape(heads_all.shape[0], 3, HEADS * HEAD)


def own_half(values, axis):
    half = values.shape[axis] // lax.axis_size("dp")
    return lax.dynamic_slice_in_dim(values, lax.axis_index("dp") * half, half, axis)


def local(
    block_input,
    block_cotangent,
    seq_start,
    ln1_gain,
    ln1_shift,
    w_qkv,
    b_qv,
    w_out,
    b_out,
    ln2_gain,
    ln2_shift,
    w_fc,
    b_fc,
    w_proj,
    b_proj,
):
    cores, wide, narrow = lax.axis_size("dp"), lax.axis_size("wide"), lax.axis_size("narrow")
    w_index, n_index = lax.axis_index("wide"), lax.axis_index("narrow")
    feats, part = w_qkv.shape[0], w_qkv.shape[2]
    width = feats * wide
    hid = w_fc.shape[1]
    piece = hid // wide
    half = piece // cores

    perm = []
    for w in range(wide):
        for n in range(narrow):
            block = n * wide + w
            perm.append((block, w * narrow + n))
    starts = lax.ppermute(seq_start, ("wide", "narrow"), perm)[0]
    allowed = block_mask(starts)

    wq_mine = own_half(w_qkv.astype(BF).reshape(feats, 3 * part), 0)
    wq_all = lax.all_gather(wq_mine, ZC, axis=0)
    wq_all = wq_all.reshape(narrow, feats, 3, part).transpose(1, 2, 0, 3).reshape(feats, 3 * width)
    wo_mine = own_half(w_out.T.astype(BF), 0)
    wo_all = lax.all_gather(wo_mine, ZC, axis=0, tiled=True)

    def split_units(by_units):
        pieces = by_units.reshape(wide, cores, half, feats)
        mine = lax.dynamic_index_in_dim(pieces, lax.axis_index("dp"), 1, keepdims=False)
        mixed = lax.all_to_all(mine, "wide", split_axis=0, concat_axis=0, tiled=True)
        mixed = mixed.transpose(1, 0, 2).reshape(half, width)
        return lax.all_gather(mixed, ZC, axis=0, tiled=True)

    wf_all = split_units(w_fc.astype(BF).T)
    wp_all = split_units(w_proj.astype(BF).T)
    b_fc_mine = lax.all_gather(
        lax.dynamic_slice_in_dim(b_fc, w_index * piece, piece, 0), "narrow", axis=0, tiled=True
    )

    rows_input = block_input.T
    rows_cot = block_cotangent.T
    normed_one, inv_one, norm_one = norm_forward(rows_input, ln1_gain, ln1_shift)
    bias_q, bias_v = lax.all_gather(b_qv, "narrow", axis=1, tiled=True)
    bias_three = jnp.stack([bias_q, jnp.zeros_like(bias_q), bias_v])
    qkv_rows = sum_tokens(dot(norm_one, wq_all, 1, 0))
    heads_all = (qkv_rows.reshape(-1, 3, width) + bias_three).astype(BF)
    attended, log_total = attend_forward(heads_all, allowed)
    attended_all = gather_tokens(attended)
    residual = rows_input + dot(attended_all, wo_all, 1, 0) + b_out
    normed_two, inv_two, norm_two = norm_forward(residual, ln2_gain, ln2_shift)
    norm_two_all = gather_features(norm_two)
    pre_act = dot(norm_two_all, wf_all, 1, 1) + b_fc_mine
    hidden = gelu_value(pre_act).astype(BF)
    output_rows = residual + sum_features(dot(hidden, wp_all, 1, 0)) + b_proj

    cot_all = gather_features(rows_cot.astype(BF))
    pre_grad = dot(cot_all, wp_all, 1, 1) * gelu_slope(pre_act)
    pre_cot = pre_grad.astype(BF)
    norm_two_grad = sum_features(dot(pre_cot, wf_all, 1, 0))

    def reduce_units(grad_units):
        total = lax.psum_scatter(grad_units.astype(BF), ZC, scatter_dimension=0, tiled=True)
        mixed = lax.all_to_all(
            total.reshape(half, wide, feats), "wide", split_axis=1, concat_axis=0, tiled=True
        )
        mixed = mixed.reshape(wide, half, feats)
        both = lax.all_gather(mixed, "dp", axis=1)
        return both.reshape(hid, feats).T.astype(F32)

    grad_w_proj = reduce_units(dot(hidden, cot_all, 0, 0))
    grad_w_fc = reduce_units(dot(pre_cot, norm_two_all, 0, 0))
    resid_grad = rows_cot + norm_backward(norm_two_grad, normed_two, inv_two, ln2_gain)
    resid_cot = resid_grad.astype(BF)
    attended_cot = sum_tokens(dot(resid_cot, wo_all, 1, 1)).astype(BF)
    qkv_grad = attend_backward(heads_all, allowed, log_total, attended_cot)
    qkv_cot_all = gather_tokens(qkv_grad.astype(BF).reshape(-1, 3 * width))
    norm_one_grad = dot(qkv_cot_all, wq_all, 1, 1)

    wo_grad = dot(attended_all, resid_cot, 0, 0)
    wo_grad = lax.psum_scatter(wo_grad.astype(BF), ZC, scatter_dimension=0, tiled=True)
    grad_w_out = lax.all_gather(wo_grad, "dp", axis=0, tiled=True).T.astype(F32)
    wq_grad = dot(norm_one, qkv_cot_all, 0, 0).astype(BF).reshape(feats, 3, narrow, part)
    wq_grad = wq_grad.transpose(2, 0, 1, 3).reshape(narrow * feats, 3 * part)
    wq_grad = lax.psum_scatter(wq_grad, ZC, scatter_dimension=0, tiled=True)
    grad_w_qkv = lax.all_gather(wq_grad, "dp", axis=0, tiled=True).reshape(feats, 3, part).astype(F32)

    grad_input_rows = resid_grad + norm_backward(norm_one_grad, normed_one, inv_one, ln1_gain)

    qkv_sums = jnp.sum(qkv_grad, axis=0)
    fc_sums = jnp.sum(pre_grad, axis=0).reshape(narrow, 1, piece)
    fc_full = jnp.zeros((narrow, wide, piece), F32)
    fc_full = lax.dynamic_update_slice_in_dim(fc_full, fc_sums, w_index, 1)
    bias_qv_sum, fc_sum = lax.psum(
        (jnp.stack([qkv_sums[0], qkv_sums[2]]), fc_full.reshape(narrow * hid)), ("dp", "wide", "narrow")
    )
    grad_b_qv = lax.dynamic_slice_in_dim(bias_qv_sum, n_index * part, part, 1)
    grad_b_fc = lax.dynamic_slice_in_dim(fc_sum, n_index * hid, hid, 0)
    row_terms = (
        jnp.sum(norm_one_grad * normed_one, axis=0),
        jnp.sum(norm_one_grad, axis=0),
        jnp.sum(resid_grad, axis=0),
        jnp.sum(norm_two_grad * normed_two, axis=0),
        jnp.sum(norm_two_grad, axis=0),
        jnp.sum(rows_cot, axis=0),
    )
    gain_one, shift_one, out_bias, gain_two, shift_two, proj_bias = lax.psum(row_terms, ("dp", "narrow"))
    return (
        output_rows.T,
        grad_input_rows.T,
        gain_one,
        shift_one,
        grad_w_qkv,
        grad_b_qv,
        grad_w_out,
        out_bias,
        gain_two,
        shift_two,
        grad_w_fc,
        grad_b_fc,
        grad_w_proj,
        proj_bias,
    )


def solution(mesh):
    return jax.shard_map(
        local,
        mesh=mesh,
        in_specs=(
            P("wide", ("dp", "narrow")),
            P("wide", ("dp", "narrow")),
            P(("dp", "wide", "narrow"), None),
            P("wide"),
            P("wide"),
            P("wide", None, "narrow"),
            P(None, "narrow"),
            P("wide", "narrow"),
            P("wide"),
            P("wide"),
            P("wide"),
            P("wide", "narrow"),
            P("narrow"),
            P("wide", "narrow"),
            P("wide"),
        ),
        out_specs=(
            P("wide", ("dp", "narrow")),
            P("wide", ("dp", "narrow")),
            P("wide"),
            P("wide"),
            P("wide", None, "narrow"),
            P(None, "narrow"),
            P("wide", "narrow"),
            P("wide"),
            P("wide"),
            P("wide"),
            P("wide", "narrow"),
            P("narrow"),
            P("wide", "narrow"),
            P("wide"),
        ),
        check_vma=False,
    )
```

time: 1340 us -> 928 us (0.69)
  waiting for transfers between devices: 967 us -> 415 us
  local copies, waits for them, and re-layouts: 37.6 us -> 171 us
  blocking collectives: 159 us -> 187 us
  other arithmetic: 45 us -> 22.7 us
    reduce_scatter x8 -> x4, waiting for transfers between devices: 560 us -> 49.5 us  [the longest x2 49.5 us: sum_features(): lax.psum_scatter(partial_value.astype(BF), 'wide', scatter_dimension=1, t...]
    unnamed x17 -> x22, waiting for transfers between devices: 0.8 us -> 139 us
    all_gather x8 -> x10, waiting for transfers between devices: 357 us -> 226 us  [the longest x2 73.1 us: split_units(): return lax.all_gather(mixed, ZC, axis=0, tiled=True)]
    reshape x0 -> x15, local copies, waits for them, and re-layouts: none -> 82.1 us  [the longest x2 27.1 us: local(): dot(norm_one, qkv_cot_all, 0, 0).astype(BF).reshape(feats, 3, narrow, part)]
    all_to_all x2 -> x0, waiting for transfers between devices: 49.3 us -> none  [to_heads(): lax.all_to_all(values, 'narrow', split_axis=0, concat_axis=2, tiled=True)]
    dynamic_slice x2 -> x7, local copies, waits for them, and re-layouts: 1.35 us -> 19.6 us  [the longest x3 15.1 us: split_units(): lax.dynamic_index_in_dim(pieces, lax.axis_index('dp'), 1, keepdims=False)]
    all_gather x0 -> x3, blocking collectives: none -> 15.3 us  [the longest x1 9.48 us: local(): bias_q, bias_v = lax.all_gather(b_qv, 'narrow', axis=1, tiled=True)]
    transpose x0 -> x3, local copies, waits for them, and re-layouts: none -> 13.5 us  [the longest x1 12.6 us: local(): wq_all.reshape(narrow, feats, 3, part).transpose(1, 2, 0, 3)]
  transfers between devices with their start and end apart: 19 -> 19, of which waited for: 17 -> 13; matrix products, arithmetic and copies ran while one was open for 6% -> 21% of each run, Pallas kernels for 0% -> 0%
where the time goes in v1:
time: 928 us; the launch traced here: 914 us
  waiting for transfers between devices  415 us (45%)
  blocking collectives  187 us (20%)
  local copies, waits for them, and re-layouts  171 us (18%)
  matrix products  96 us (10%)
  other arithmetic  22.7 us (2%)
  between operations  15.8 us (2%)
    unnamed x22, waiting for transfers between devices  139 us
    dot_general x12, matrix products, dot(): lax.dot_general(a, b, (((ca,), (cb,)), ((), ())), preferred_element_type=...  77.2 us
    all_gather x2, waiting for transfers between devices, split_units(): return lax.all_gather(mixed, ZC, axis=0, tiled=True)  73.1 us
    all_gather x2, waiting for transfers between devices, gather_features(): return lax.all_gather(values, 'wide', axis=1, tiled=True)  59 us
    all_gather x2, waiting for transfers between devices, gather_tokens(): return lax.all_gather(values, 'wide', axis=0, tiled=True)  55.9 us
    reduce_scatter x2, waiting for transfers between devices, sum_features(): lax.psum_scatter(partial_value.astype(BF), 'wide', scatter_dimension=1, t...  49.5 us
    psum x1, blocking collectives, local(): lax.psum((jnp.stack([qkv_sums[0], qkv_sums[2]]), fc_full.reshape(narrow *...  41.2 us
    all_gather x1, waiting for transfers between devices, local(): wq_all = lax.all_gather(wq_mine, ZC, axis=0)  38.4 us
  transfers between devices with their start and end apart: 19, of which 13 were waited for; matrix products, arithmetic and copies ran while one was open for 21% of the time, Pallas kernels for 0%

profile of v1, /device:TPU:17, one launch (start us, length us, event | category | flops | bytes accessed | tf_op | source)
XLA Modules:
  0.0 913.8 jit_solution(4123981955321819578)
XLA Ops:
  21.4 38.4 %all-gather.29.cloned.1.call-done = bf16[1600,1200]{1,0:T(8,128)(2,1)} async-done(((bf16[200,1200]{1,0:T(8,128)(2,1)}), bf16[1600,1200]{1,0:T(8,128)(2,1)}) %all-gather.29.cloned.1.call-update) | async-done | bytes 3840016 | tf_op jit(solution)/shard_map/all_gather | solution.py:151
  66.5 14.6 %reshape.114 = bf16[4,400,3,400]{1,0,3,2:T(4,128)(2,1)} reshape(bf16[1600,1200]{0,1:T(8,128)(2,1)} %copy.116) | data formatting | bytes 7680000 | tf_op jit(solution)/shard_map/reshape | solution.py:152
  81.2 12.6 %copy.117 = bf16[400,3,4,400]{3,2,1,0:T(4,128)(2,1)} copy(bf16[400,3,4,400]{0,2,3,1:T(4,128)(2,1)} %bitcast.146) | data formatting | bytes 7680000 | tf_op jit(solution)/shard_map/transpose | solution.py:152
  135.0 43.0 %reduce-scatter.25.cloned.1.call-done = bf16[128,4800]{1,0:T(8,128)(2,1)} async-done(((bf16[512,4800]{1,0:T(8,128)(2,1)}), bf16[128,4800]{1,0:T(8,128)(2,1)}) %reduce-scatter.25.cloned.1.call-update) | async-done | bytes 1228816
  208.6 16.1 %all_to_all.40 = bf16[4,200,400]{2,1,0:T(8,128)(2,1)S(1)} all-to-all(bf16[4,200,400]{2,1,0:T(8,128)(2,1)S(1)} %bitcast.157), channel_id=1, replica_groups=mesh['dp'=2,'wide'=4,'narrow'=4] {'wide'}, dimensions={0} | all-to-all | bytes 1280000 | tf_op jit(solution)/shard_map/all_to_all | solution.py:159
  226.8 16.3 %all-gather.15.cloned.1.call-done = bf16[512,1600]{0,1:T(8,128)(2,1)} async-done(((bf16[128,1600]{0,1:T(8,128)(2,1)}), bf16[512,1600]{0,1:T(8,128)(2,1)}) %all-gather.15.cloned.1.call-update) | async-done | bytes 1638416 | tf_op jit(solution)/shard_map/all_gather | solution.py:62
  260.1 12.6 %all_to_all.41 = bf16[4,200,400]{2,1,0:T(8,128)(2,1)S(1)} all-to-all(bf16[4,200,400]{2,1,0:T(8,128)(2,1)} %bitcast.159), channel_id=1, replica_groups=mesh['dp'=2,'wide'=4,'narrow'=4] {'wide'}, dimensions={0} | all-to-all | bytes 1280000 | tf_op jit(solution)/shard_map/all_to_all | solution.py:159
  276.9 9.9 %all-reduce = f32[1600]{0:T(1024)S(1)} all-reduce(f32[1600]{0:T(1024)S(1)} %dynamic-slice_dynamic-update-slice_fusion), channel_id=1, replica_groups=mesh['dp'=2,'wide'=4,'narrow'=4] {'narrow'}, use_global_device_ids=true, to_apply=%add | all-reduce | flops 1600 | bytes 12800
  286.8 14.8 %all-gather.21.cloned.1.call-done = bf16[1600,1600]{1,0:T(8,128)(2,1)} async-done(((bf16[200,1600]{1,0:T(8,128)(2,1)}), bf16[1600,1600]{1,0:T(8,128)(2,1)}) %all-gather.21.cloned.1.call-update) | async-done | bytes 5120016 | tf_op jit(solution)/shard_map/all_gather | solution.py:161
  301.6 33.2 %all-gather.19.cloned.1.call-done = bf16[512,1600]{0,1:T(8,128)(2,1)} async-done(((bf16[512,400]{0,1:T(8,128)(2,1)}), bf16[512,1600]{0,1:T(8,128)(2,1)}) %all-gather.19.cloned.1.call-update) | async-done | bytes 1638416 | tf_op jit(solution)/shard_map/all_gather | solution.py:58
  342.8 25.9 %all-gather.25.cloned.1.call-done = bf16[512,1600]{0,1:T(8,128)(2,1)} async-done(((bf16[512,400]{0,1:T(8,128)(2,1)}), bf16[512,1600]{0,1:T(8,128)(2,1)}) %all-gather.25.cloned.1.call-update) | async-done | bytes 1638416 | tf_op jit(solution)/shard_map/all_gather | solution.py:58
  368.6 58.2 %all-gather.23.cloned.1.call-done = bf16[1600,1600]{1,0:T(8,128)(2,1)} async-done(((bf16[200,1600]{1,0:T(8,128)(2,1)}), bf16[1600,1600]{1,0:T(8,128)(2,1)}) %all-gather.23.cloned.1.call-update) | async-done | bytes 5120016 | tf_op jit(solution)/shard_map/all_gather | solution.py:161
  452.9 22.8 %reduce-scatter.21.cloned.1.call-done = bf16[512,400]{0,1:T(8,128)(2,1)} async-done(((bf16[512,1600]{0,1:T(8,128)(2,1)}), bf16[512,400]{0,1:T(8,128)(2,1)}) %reduce-scatter.21.cloned.1.call-update) | async-done | bytes 409616 | tf_op jit(solution)/shard_map/reduce_scatter | solution.py:66
  484.1 26.6 %reduce-scatter.19.cloned.1.call-done = bf16[512,400]{0,1:T(8,128)(2,1)} async-done(((bf16[512,1600]{0,1:T(8,128)(2,1)}), bf16[512,400]{0,1:T(8,128)(2,1)}) %reduce-scatter.19.cloned.1.call-update) | async-done | bytes 409616 | tf_op jit(solution)/shard_map/reduce_scatter | solution.py:66
  538.8 10.9 %reduce-scatter.27.cloned.1.call-done = bf16[128,1600]{1,0:T(8,128)(2,1)} async-done(((bf16[512,1600]{1,0:T(8,128)(2,1)}), bf16[128,1600]{1,0:T(8,128)(2,1)}) %reduce-scatter.27.cloned.1.call-update) | async-done | bytes 409616
  567.9 43.8 %reduce-scatter.31.cloned.1.call-done = bf16[200,1600]{1,0:T(8,128)(2,1)} async-done(((bf16[1600,1600]{1,0:T(8,128)(2,1)}), bf16[200,1600]{1,0:T(8,128)(2,1)}) %reduce-scatter.31.cloned.1.call-update) | async-done | bytes 640016
  616.8 14.3 %all_to_all.42 = bf16[200,4,400]{2,0,1:T(8,128)(2,1)S(1)} all-to-all(bf16[200,4,400]{2,0,1:T(8,128)(2,1)S(1)} %copy.131), channel_id=1, replica_groups=mesh['dp'=2,'wide'=4,'narrow'=4] {'wide'}, dimensions={1} | all-to-all | bytes 1280000 | tf_op jit(solution)/shard_map/all_to_all | solution.py:192
  632.5 41.5 %reduce-scatter.33.cloned.1.call-done = bf16[200,1600]{1,0:T(8,128)(2,1)} async-done(((bf16[1600,1600]{1,0:T(8,128)(2,1)}), bf16[200,1600]{1,0:T(8,128)(2,1)}) %reduce-scatter.33.cloned.1.call-update) | async-done | bytes 640016
  679.2 19.5 %all_to_all.43 = bf16[200,4,400]{2,0,1:T(8,128)(2,1)S(1)} all-to-all(bf16[200,4,400]{2,0,1:T(8,128)(2,1)S(1)} %copy.135), channel_id=1, replica_groups=mesh['dp'=2,'wide'=4,'narrow'=4] {'wide'}, dimensions={1} | all-to-all | bytes 1280000 | tf_op jit(solution)/shard_map/all_to_all | solution.py:192
  700.3 39.7 %all-gather.27.cloned.1.call-done = bf16[512,4800]{0,1:T(8,128)(2,1)} async-done(((bf16[128,4800]{0,1:T(8,128)(2,1)}), bf16[512,4800]{0,1:T(8,128)(2,1)}) %all-gather.27.cloned.1.call-update) | async-done | bytes 4915216 | tf_op jit(solution)/shard_map/all_gather | solution.py:62
  746.5 14.2 %reshape.123 = bf16[400,3,4,400]{3,2,1,0:T(4,128)(2,1)} reshape(bf16[400,4800]{1,0:T(8,128)(2,1)} %convolution_convert_fusion.3) | data formatting | bytes 7680000 | tf_op jit(solution)/shard_map/reshape | solution.py:211
  760.6 12.9 %copy.128 = bf16[400,3,4,400]{0,2,3,1:T(4,128)(2,1)} copy(bf16[400,3,4,400]{3,2,1,0:T(4,128)(2,1)} %reshape.123) | data formatting | bytes 7680000 | tf_op jit(solution)/shard_map/reshape | solution.py:211
  797.6 41.2 %all-reduce.3 = (f32[2,1600]{1,0:T(2,128)S(1)}, f32[6400]{0:T(1024)S(1)}) all-reduce(f32[2,1600]{1,0:T(2,128)S(1)} %pad_maximum_fusion.2, f32[6400]{0:T(1024)S(1)} %reshape.127), channel_id=1, replica_groups=mesh['dp'=2,'wide'=4,'narrow'=4] {'dp','wide','narrow'}, use_global_device_ids=true, to_apply=%region_28.29 | all-reduce | flops 9600 | bytes 76800 | tf_op jit(solution)/shard_map/psum | solution.py:222
  870.1 29.4 %all-reduce.4 = (f32[400]{0:T(512)}, f32[400]{0:T(512)}, f32[400]{0:T(512)}, f32[400]{0:T(512)}, f32[400]{0:T(512)}, /*index=5*/f32[400]{0:T(512)}) all-reduce(f32[400]{0:T(512)S(1)} %get-tuple-element.98, f32[400]{0:T(512)S(1)} %get-tuple-element.103, ...), channel_id=1, replica_groups=mesh['dp'=2,'wide'=4,'narrow'=4] {'dp','narrow'}, use_global_device_ids=true, to_apply=%region_23.24 | all-reduce | flops 2400 | bytes 19200 | tf_op jit(solution)/shard_map/psum | solution.py:235
  (194 shorter events, 285.5 us)
Async XLA Ops:
  7.2 116.9 %copy-start = (f32[400,400]{1,0:T(8,128)S(1)}, f32[400,400]{1,0:T(8,128)}, u32[]{:S(2)}) copy-start(f32[400,400]{1,0:T(8,128)} %param.22) | copy-start | bytes 1920004
  7.2 52.6 %all-gather.29.cloned.1.call-start = ((), (), s32[]{:S(2)}) async-start(), calls=%async_computation.22 | async-start | bytes 4608000 | tf_op jit(solution)/shard_map/all_gather | solution.py:151
  13.3 164.7 %reduce-scatter.25.cloned.1.call-start = ((), (), s32[]{:S(2)}) async-start(), calls=%async_computation.25 | async-start | bytes 6225920
  119.2 107.6 %all-gather.17.cloned.1.call-start = ((), (), s32[]{:S(2)}) async-start(), calls=%async_computation.13 | async-start | bytes 1843200 | tf_op jit(solution)/shard_map/all_gather | solution.py:154
  119.8 15.0 %collective-permute-start = (s32[1,128]{1,0:T(1,128)S(1)}, s32[1,128]{1,0:T(1,128)S(1)}, u32[]{:S(2)}, u32[]{:S(2)}) collective-permute-start(s32[1,128]{1,0:T(1,128)S(1)} %copy-done.22), channel_id=1, source_target_pairs={{0,0},{4,1},{8,2},{12,3},{1,4},{5,5},{9,6},{13,7},{2,8},{6,9},{10,... | collective-permute-start | bytes 1544 | tf_op jit(solution)/shard_map/ppermute | solution.py:147
  125.0 118.1 %all-gather.15.cloned.1.call-start = ((), (), s32[]{:S(2)}) async-start(), calls=%async_computation.12 | async-start | bytes 2048000 | tf_op jit(solution)/shard_map/all_gather | solution.py:62
  186.2 115.4 %all-gather.21.cloned.1.call-start = ((), (), s32[]{:S(2)}) async-start(), calls=%async_computation.15 | async-start | bytes 5990400 | tf_op jit(solution)/shard_map/all_gather | solution.py:161
  226.7 26.2 %copy-start.12 = (f32[400]{0:T(512)S(1)}, f32[400]{0:T(512)}, u32[]{:S(2)}) copy-start(f32[400]{0:T(512)} %param.24) | copy-start | bytes 4804
  226.8 108.0 %all-gather.19.cloned.1.call-start = ((), (), s32[]{:S(2)}) async-start(), calls=%async_computation.14 | async-start | bytes 2048000 | tf_op jit(solution)/shard_map/all_gather | solution.py:58
  254.0 114.7 %all-gather.25.cloned.1.call-start = ((), (), s32[]{:S(2)}) async-start(), calls=%async_computation.18 | async-start | bytes 2048000 | tf_op jit(solution)/shard_map/all_gather | solution.py:58
  256.1 170.8 %all-gather.23.cloned.1.call-start = ((), (), s32[]{:S(2)}) async-start(), calls=%async_computation.16 | async-start | bytes 5990400 | tf_op jit(solution)/shard_map/all_gather | solution.py:161
  274.7 201.0 %reduce-scatter.21.cloned.1.call-start = ((), (), s32[]{:S(2)}) async-start(), calls=%async_computation.19 | async-start | bytes 2048000 | tf_op jit(solution)/shard_map/reduce_scatter | solution.py:66
  444.6 66.2 %reduce-scatter.19.cloned.1.call-start = ((), (), s32[]{:S(2)}) async-start(), calls=%async_computation.17 | async-start | bytes 2048000 | tf_op jit(solution)/shard_map/reduce_scatter | solution.py:66
  452.8 57.9 %copy-start.3 = (f32[400,512]{1,0:T(8,128)S(1)}, f32[400,512]{1,0:T(8,128)}, u32[]{:S(2)}) copy-start(f32[400,512]{1,0:T(8,128)} %param.16) | copy-start | bytes 2457604
  452.8 57.9 %copy-start.15 = (f32[400]{0:T(512)S(1)}, f32[400]{0:T(512)}, u32[]{:S(2)}) copy-start(f32[400]{0:T(512)} %param.29) | copy-start | bytes 4804
  452.9 96.8 %reduce-scatter.27.cloned.1.call-start = ((), (), s32[]{:S(2)}) async-start(), calls=%async_computation.26 | async-start | bytes 2129920
  517.6 94.1 %reduce-scatter.31.cloned.1.call-start = ((), (), s32[]{:S(2)}) async-start(), calls=%async_computation.28 | async-start | bytes 5990400
  526.0 148.1 %reduce-scatter.33.cloned.1.call-start = ((), (), s32[]{:S(2)}) async-start(), calls=%async_computation.29 | async-start | bytes 5990400
  535.6 204.4 %all-gather.27.cloned.1.call-start = ((), (), s32[]{:S(2)}) async-start(), calls=%async_computation.20 | async-start | bytes 6144000 | tf_op jit(solution)/shard_map/all_gather | solution.py:62
  563.9 226.8 %reduce-scatter.23.cloned.1.call-start = ((), (), s32[]{:S(2)}) async-start(), calls=%async_computation.21 | async-start | bytes 1843200 | tf_op jit(solution)/shard_map/reduce_scatter | solution.py:209
  567.8 272.4 %all-gather.31.cloned.1.call-start = ((), (), s32[]{:S(2)}) async-start(), calls=%async_computation.23 | async-start | bytes 2457600 | tf_op jit(solution)/shard_map/all_gather | solution.py:196
  632.4 216.3 %all-gather.33.cloned.1.call-start = ((), (), s32[]{:S(2)}) async-start(), calls=%async_computation.24 | async-start | bytes 2457600 | tf_op jit(solution)/shard_map/all_gather | solution.py:196
  700.0 200.7 %reduce-scatter.29.cloned.1.call-start = ((), (), s32[]{:S(2)}) async-start(), calls=%async_computation.27 | async-start | bytes 4608000 | tf_op jit(solution)/shard_map/reduce_scatter | solution.py:213
  857.1 42.4 %copy-start.5 = (f32[512,400]{0,1:T(8,128)S(1)}, f32[512,400]{0,1:T(8,128)}, u32[]{:S(2)}) copy-start(f32[512,400]{0,1:T(8,128)} %copy-done.4) | copy-start | bytes 2457604
  (20 other events, 113.9 us)
Sparse Core Ops, SparseCore 0:
  13.4 46.3 all-gather.28
  119.3 58.5 reduce-scatter.24
  180.1 25.3 all-gather.16
  207.8 35.2 all-gather.14
  245.2 56.4 all-gather.20
  303.9 30.8 all-gather.18
  337.2 31.3 all-gather.24
  370.8 55.9 all-gather.22
  444.7 30.9 reduce-scatter.20
  479.2 31.5 reduce-scatter.18
  517.7 31.9 reduce-scatter.26
  551.9 59.7 reduce-scatter.30
  614.0 60.0 reduce-scatter.32
  676.3 63.6 all-gather.26
  742.7 29.4 reduce-scatter.22
  774.1 14.1 all-gather.30
  789.7 11.0 all-gather.32
  803.0 49.2 reduce-scatter.28

commit v2 on v1

--- a/solution.py
+++ b/solution.py
@@ -12,7 +12,6 @@
 GELU_C = math.sqrt(2.0 / math.pi)
 BF = jnp.bfloat16
 F32 = jnp.float32
-ZC = ("narrow", "dp")
 
 
 def gelu_value(pre_act):
@@ -54,20 +53,28 @@
     return inv_std * (scaled - first_sum / full_width - normed * (second_sum / full_width))
 
 
-def gather_features(values):
-    return lax.all_gather(values, "wide", axis=1, tiled=True)
-
-
 def gather_tokens(values):
     return lax.all_gather(values, "wide", axis=0, tiled=True)
 
 
-def sum_features(partial_value):
-    return lax.psum_scatter(partial_value.astype(BF), "wide", scatter_dimension=1, tiled=True).astype(F32)
+def gather_narrow(values):
+    return lax.all_gather(values, "narrow", axis=0, tiled=True)
 
 
 def sum_tokens(partial_value):
     return lax.psum_scatter(partial_value.astype(BF), "wide", scatter_dimension=0, tiled=True).astype(F32)
+
+
+def sum_narrow(partial_value):
+    return lax.psum_scatter(partial_value.astype(BF), "narrow", scatter_dimension=0, tiled=True).astype(F32)
+
+
+def to_tokens(values):
+    return lax.all_to_all(values, "wide", split_axis=0, concat_axis=1, tiled=True)
+
+
+def to_features(values):
+    return lax.all_to_all(values, "wide", split_axis=1, concat_axis=0, tiled=True)
 
 
 def block_mask(starts):
@@ -136,8 +143,6 @@
     feats, part = w_qkv.shape[0], w_qkv.shape[2]
     width = feats * wide
     hid = w_fc.shape[1]
-    piece = hid // wide
-    half = piece // cores
 
     perm = []
     for w in range(wide):
@@ -148,91 +153,108 @@
     allowed = block_mask(starts)
 
     wq_mine = own_half(w_qkv.astype(BF).reshape(feats, 3 * part), 0)
-    wq_all = lax.all_gather(wq_mine, ZC, axis=0)
-    wq_all = wq_all.reshape(narrow, feats, 3, part).transpose(1, 2, 0, 3).reshape(feats, 3 * width)
-    wo_mine = own_half(w_out.T.astype(BF), 0)
-    wo_all = lax.all_gather(wo_mine, ZC, axis=0, tiled=True)
-
-    def split_units(by_units):
-        pieces = by_units.reshape(wide, cores, half, feats)
-        mine = lax.dynamic_index_in_dim(pieces, lax.axis_index("dp"), 1, keepdims=False)
-        mixed = lax.all_to_all(mine, "wide", split_axis=0, concat_axis=0, tiled=True)
-        mixed = mixed.transpose(1, 0, 2).reshape(half, width)
-        return lax.all_gather(mixed, ZC, axis=0, tiled=True)
-
-    wf_all = split_units(w_fc.astype(BF).T)
-    wp_all = split_units(w_proj.astype(BF).T)
-    b_fc_mine = lax.all_gather(
-        lax.dynamic_slice_in_dim(b_fc, w_index * piece, piece, 0), "narrow", axis=0, tiled=True
+    wq_all = lax.all_gather(wq_mine, ("narrow", "dp"), axis=0, tiled=True)
+    wq_all = wq_all.reshape(narrow, feats, 3 * part)
+    wo_mine = lax.all_gather(own_half(w_out.astype(BF), 0), "narrow", axis=1, tiled=True)
+    wo_all = lax.all_gather(wo_mine, ("wide", "dp"), axis=0, tiled=True)
+    wf_all = lax.all_gather(own_half(w_fc.astype(BF), 0), ("wide", "dp"), axis=0, tiled=True)
+    wp_all = lax.all_gather(own_half(w_proj.astype(BF), 0), ("wide", "dp"), axis=0, tiled=True)
+    b_out_full, gain_two_full, shift_two_full = lax.all_gather(
+        jnp.stack([b_out, ln2_gain, ln2_shift]), "wide", axis=1, tiled=True
+    )
+    bias_qv = lax.all_gather(b_qv, "narrow", axis=0).reshape(narrow, 1, 2, part)
+    bias_three = jnp.concatenate(
+        [bias_qv[:, :, 0], jnp.zeros((narrow, 1, part), F32), bias_qv[:, :, 1]], axis=2
     )
 
     rows_input = block_input.T
     rows_cot = block_cotangent.T
+    x_tok = to_tokens(rows_input)
+    dy_tok = to_tokens(rows_cot)
+    cot_all = gather_narrow(dy_tok.astype(BF))
+
     normed_one, inv_one, norm_one = norm_forward(rows_input, ln1_gain, ln1_shift)
-    bias_q, bias_v = lax.all_gather(b_qv, "narrow", axis=1, tiled=True)
-    bias_three = jnp.stack([bias_q, jnp.zeros_like(bias_q), bias_v])
-    qkv_rows = sum_tokens(dot(norm_one, wq_all, 1, 0))
-    heads_all = (qkv_rows.reshape(-1, 3, width) + bias_three).astype(BF)
+    qkv_part = jnp.einsum("tk,nkc->tnc", norm_one, wq_all, preferred_element_type=F32)
+    qkv_rows = sum_tokens(qkv_part.transpose(0, 1, 2)).transpose(1, 0, 2)
+    qkv_rows = (qkv_rows + bias_three).astype(BF)
+    heads_all = qkv_rows.reshape(narrow, -1, 3, part).transpose(1, 2, 0, 3).reshape(-1, 3, width)
     attended, log_total = attend_forward(heads_all, allowed)
-    attended_all = gather_tokens(attended)
-    residual = rows_input + dot(attended_all, wo_all, 1, 0) + b_out
-    normed_two, inv_two, norm_two = norm_forward(residual, ln2_gain, ln2_shift)
-    norm_two_all = gather_features(norm_two)
-    pre_act = dot(norm_two_all, wf_all, 1, 1) + b_fc_mine
+    residual = x_tok + dot(attended, wo_all, 1, 1) + b_out_full
+    mean_two = jnp.mean(residual, axis=1, keepdims=True)
+    inv_two = lax.rsqrt(jnp.mean(residual * residual, axis=1, keepdims=True) - mean_two * mean_two + EPS)
+    normed_two = (residual - mean_two) * inv_two
+    norm_two = (normed_two * gain_two_full + shift_two_full).astype(BF)
+    norm_two_all = gather_narrow(norm_two)
+    pre_act = dot(norm_two_all, wf_all, 1, 0) + b_fc
     hidden = gelu_value(pre_act).astype(BF)
-    output_rows = residual + sum_features(dot(hidden, wp_all, 1, 0)) + b_proj
-
-    cot_all = gather_features(rows_cot.astype(BF))
-    pre_grad = dot(cot_all, wp_all, 1, 1) * gelu_slope(pre_act)
+    out_tok = residual + sum_narrow(dot(hidden, wp_all, 1, 1))
+    output_rows = to_features(out_tok) + b_proj
+
+    pre_grad = dot(cot_all, wp_all, 1, 0) * gelu_slope(pre_act)
     pre_cot = pre_grad.astype(BF)
-    norm_two_grad = sum_features(dot(pre_cot, wf_all, 1, 0))
-
-    def reduce_units(grad_units):
-        total = lax.psum_scatter(grad_units.astype(BF), ZC, scatter_dimension=0, tiled=True)
-        mixed = lax.all_to_all(
-            total.reshape(half, wide, feats), "wide", split_axis=1, concat_axis=0, tiled=True
-        )
-        mixed = mixed.reshape(wide, half, feats)
-        both = lax.all_gather(mixed, "dp", axis=1)
-        return both.reshape(hid, feats).T.astype(F32)
-
-    grad_w_proj = reduce_units(dot(hidden, cot_all, 0, 0))
-    grad_w_fc = reduce_units(dot(pre_cot, norm_two_all, 0, 0))
-    resid_grad = rows_cot + norm_backward(norm_two_grad, normed_two, inv_two, ln2_gain)
+    norm_two_grad = sum_narrow(dot(pre_cot, wf_all, 1, 1))
+
+    def reduce_wide(grad):
+        total = lax.psum_scatter(grad.astype(BF), ("wide", "dp"), scatter_dimension=0, tiled=True)
+        return total
+
+    def share(total):
+        return lax.all_gather(total, "dp", axis=0, tiled=True).astype(F32)
+
+    grad_w_proj = share(reduce_wide(dot(cot_all, hidden, 0, 0)))
+    grad_w_fc = share(reduce_wide(dot(norm_two_all, pre_cot, 0, 0)))
+
+    scaled = norm_two_grad * gain_two_full
+    mean_scaled = jnp.mean(scaled, axis=1, keepdims=True)
+    mean_cross = jnp.mean(scaled * normed_two, axis=1, keepdims=True)
+    resid_grad = dy_tok + inv_two * (scaled - mean_scaled - normed_two * mean_cross)
     resid_cot = resid_grad.astype(BF)
-    attended_cot = sum_tokens(dot(resid_cot, wo_all, 1, 1)).astype(BF)
+    attended_cot = dot(resid_cot, wo_all, 1, 0).astype(BF)
+    wo_grad = reduce_wide(dot(resid_cot, attended, 0, 0))
+    wo_grad = lax.psum_scatter(wo_grad, "narrow", scatter_dimension=1, tiled=True)
+    grad_w_out = share(wo_grad)
+
     qkv_grad = attend_backward(heads_all, allowed, log_total, attended_cot)
-    qkv_cot_all = gather_tokens(qkv_grad.astype(BF).reshape(-1, 3 * width))
-    norm_one_grad = dot(qkv_cot_all, wq_all, 1, 1)
-
-    wo_grad = dot(attended_all, resid_cot, 0, 0)
-    wo_grad = lax.psum_scatter(wo_grad.astype(BF), ZC, scatter_dimension=0, tiled=True)
-    grad_w_out = lax.all_gather(wo_grad, "dp", axis=0, tiled=True).T.astype(F32)
-    wq_grad = dot(norm_one, qkv_cot_all, 0, 0).astype(BF).reshape(feats, 3, narrow, part)
-    wq_grad = wq_grad.transpose(2, 0, 1, 3).reshape(narrow * feats, 3 * part)
-    wq_grad = lax.psum_scatter(wq_grad, ZC, scatter_dimension=0, tiled=True)
-    grad_w_qkv = lax.all_gather(wq_grad, "dp", axis=0, tiled=True).reshape(feats, 3, part).astype(F32)
-
-    grad_input_rows = resid_grad + norm_backward(norm_one_grad, normed_one, inv_one, ln1_gain)
+    qkv_cot = qkv_grad.astype(BF).reshape(-1, 3, narrow, part).transpose(0, 2, 1, 3)
+    qkv_cot_all = gather_tokens(qkv_cot.reshape(-1, narrow, 3 * part))
+    norm_one_grad = jnp.einsum("tnc,nkc->tk", qkv_cot_all, wq_all, preferred_element_type=F32)
+    wq_grad = jnp.einsum("tk,tnc->nkc", norm_one, qkv_cot_all, preferred_element_type=F32).astype(BF)
+    wq_grad = lax.psum_scatter(
+        wq_grad.reshape(narrow * feats, 3 * part), ("narrow", "dp"), scatter_dimension=0, tiled=True
+    )
+    grad_w_qkv = share(wq_grad).reshape(feats, 3, part)
+
+    resid_back = to_features(resid_grad)
+    grad_input_rows = resid_back + norm_backward(norm_one_grad, normed_one, inv_one, ln1_gain)
 
     qkv_sums = jnp.sum(qkv_grad, axis=0)
-    fc_sums = jnp.sum(pre_grad, axis=0).reshape(narrow, 1, piece)
-    fc_full = jnp.zeros((narrow, wide, piece), F32)
-    fc_full = lax.dynamic_update_slice_in_dim(fc_full, fc_sums, w_index, 1)
-    bias_qv_sum, fc_sum = lax.psum(
-        (jnp.stack([qkv_sums[0], qkv_sums[2]]), fc_full.reshape(narrow * hid)), ("dp", "wide", "narrow")
-    )
-    grad_b_qv = lax.dynamic_slice_in_dim(bias_qv_sum, n_index * part, part, 1)
+    fc_full = lax.dynamic_update_slice_in_dim(
+        jnp.zeros((narrow * hid,), F32), jnp.sum(pre_grad, axis=0), n_index * hid, 0
+    )
+    token_terms = jnp.stack(
+        [
+            qkv_sums[0],
+            qkv_sums[2],
+            jnp.sum(resid_grad, axis=0),
+            jnp.sum(norm_two_grad * normed_two, axis=0),
+            jnp.sum(norm_two_grad, axis=0),
+        ]
+    )
+    feature_terms = jnp.stack(
+        [
+            jnp.sum(norm_one_grad * normed_one, axis=0),
+            jnp.sum(norm_one_grad, axis=0),
+            jnp.sum(rows_cot, axis=0),
+        ]
+    )
+    feature_full = lax.dynamic_update_slice_in_dim(
+        jnp.zeros((3, width), F32), feature_terms, w_index * feats, 1
+    )
+    token_sum, feature_sum, fc_sum = lax.psum((token_terms, feature_full, fc_full), ("dp", "wide", "narrow"))
+    grad_b_qv = lax.dynamic_slice_in_dim(token_sum[:2], n_index * part, part, 1)
+    out_bias, gain_two, shift_two = lax.dynamic_slice_in_dim(token_sum[2:], w_index * feats, feats, 1)
+    gain_one, shift_one, proj_bias = lax.dynamic_slice_in_dim(feature_sum, w_index * feats, feats, 1)
     grad_b_fc = lax.dynamic_slice_in_dim(fc_sum, n_index * hid, hid, 0)
-    row_terms = (
-        jnp.sum(norm_one_grad * normed_one, axis=0),
-        jnp.sum(norm_one_grad, axis=0),
-        jnp.sum(resid_grad, axis=0),
-        jnp.sum(norm_two_grad * normed_two, axis=0),
-        jnp.sum(norm_two_grad, axis=0),
-        jnp.sum(rows_cot, axis=0),
-    )
-    gain_one, shift_one, out_bias, gain_two, shift_two, proj_bias = lax.psum(row_terms, ("dp", "narrow"))
     return (
         output_rows.T,
         grad_input_rows.T,

time: 928 us -> 824 us (0.89)
  local copies, waits for them, and re-layouts: 171 us -> 59.9 us
  blocking collectives: 187 us -> 93.3 us
  waiting for transfers between devices: 415 us -> 498 us
  starting transfers between devices: 5.81 us -> 17.6 us
    unnamed x22 -> x25, waiting for transfers between devices: 139 us -> 250 us
    reshape x15 -> x0, local copies, waits for them, and re-layouts: 82.1 us -> none  [the longest x2 27.1 us: local(): dot(norm_one, qkv_cot_all, 0, 0).astype(BF).reshape(feats, 3, narrow, part)]
    psum x2 -> x0, blocking collectives: 70.7 us -> none  [the longest x1 41.2 us: local(): lax.psum((jnp.stack([qkv_sums[0], qkv_sums[2]]), fc_full.reshape(narrow *...]
    psum x0 -> x1, waiting for transfers between devices: none -> 60 us  [local(): lax.psum((token_terms, feature_full, fc_full), ('dp', 'wide', 'narrow'))]
    all_gather x2 -> x1, waiting for transfers between devices: 55.9 us -> 0.01 us  [gather_tokens(): return lax.all_gather(values, 'wide', axis=0, tiled=True)]
    reduce_scatter x4 -> x1, waiting for transfers between devices: 49.5 us -> 0.01 us  [local(): lax.psum_scatter(wq_grad.reshape(narrow * feats, 3 * part), ('narrow', 'd...]
    all_to_all x4 -> x1, blocking collectives: 62.5 us -> 20 us  [to_tokens(): lax.all_to_all(values, 'wide', split_axis=0, concat_axis=1, tiled=True)]
    all_gather x3 -> x5, blocking collectives: 15.3 us -> 56.7 us  [the longest x1 22.2 us: local(): lax.all_gather(jnp.stack([b_out, ln2_gain, ln2_shift]), 'wide', axis=1, t...]
  transfers between devices with their start and end apart: 19 -> 22, of which waited for: 13 -> 13; matrix products, arithmetic and copies ran while one was open for 21% -> 17% of each run, Pallas kernels for 0% -> 0%
where the time goes in v2:
time: 824 us; the launch traced here: 814 us
  waiting for transfers between devices  498 us (60%)
  matrix products  104 us (13%)
  blocking collectives  93.3 us (11%)
  local copies, waits for them, and re-layouts  59.9 us (7%)
  other arithmetic  23.3 us (3%)
  starting transfers between devices  17.6 us (2%)
  between operations  17.4 us (2%)
    unnamed x25, waiting for transfers between devices  250 us
    all_gather x2, waiting for transfers between devices, gather_narrow(): return lax.all_gather(values, 'narrow', axis=0, tiled=True)  70.7 us
    dot_general x9, matrix products, dot(): lax.dot_general(a, b, (((ca,), (cb,)), ((), ())), preferred_element_type=...  62.2 us
    psum x1, waiting for transfers between devices, local(): lax.psum((token_terms, feature_full, fc_full), ('dp', 'wide', 'narrow'))  60 us
    all_gather x1, waiting for transfers between devices, local(): lax.all_gather(own_half(w_proj.astype(BF), 0), ('wide', 'dp'), axis=0, ti...  43 us
    all_gather x1, waiting for transfers between devices, local(): wq_all = lax.all_gather(wq_mine, ('narrow', 'dp'), axis=0, tiled=True)  38.4 us
    unnamed x72, local copies, waits for them, and re-layouts  33.6 us
    all_gather x1, blocking collectives, local(): lax.all_gather(jnp.stack([b_out, ln2_gain, ln2_shift]), 'wide', axis=1, t...  22.2 us
  transfers between devices with their start and end apart: 22, of which 13 were waited for; matrix products, arithmetic and copies ran while one was open for 17% of the time, Pallas kernels for 0%

profile of v2, /device:TPU:17, one launch (start us, length us, event | category | flops | bytes accessed | tf_op | source)
XLA Modules:
  0.0 814.0 jit_solution(4616256458298618883)
XLA Ops:
  18.2 7.9 all-reduce.5
  26.2 38.4 %all-gather.13.cloned.1.call-done = bf16[1600,1200]{1,0:T(8,128)(2,1)} async-done(((bf16[200,1200]{1,0:T(8,128)(2,1)}), bf16[1600,1200]{1,0:T(8,128)(2,1)}) %all-gather.13.cloned.1.call-update) | async-done | bytes 3840016 | tf_op jit(solution)/shard_map/all_gather | solution.py:156
  64.5 8.2 %convolution_convert_fusion.3 = bf16[512,4,1200]{0,2,1:T(8,128)(2,1)} fusion(bf16[4,400,1200]{2,1,0:T(8,128)(2,1)} %bitcast.247, f32[400,512]{1,0:T(8,128)S(1)} %copy-done.2, f32[400]{0:T(512)S(1)} %copy-done.25, f32[400]{0:T(512)S(1)} %copy-done.23, f32[512]{0:T(512)S(1)} %bitcast.228, f32[512]{0:T(512)S(1)} %bitcast.224), kind=kOutput, calls=%fused_computation.6 | convolution fusion | flops 1969561600 | bytes 9581696 | tf_op jit(solution)/shard_map/tk,nkc->tnc/dot_general | solution.py:177
  72.7 7.5 copy.132
  83.8 16.9 %all_gather.48 = bf16[200,1600]{0,1:T(8,128)(2,1)} all-gather(bf16[200,400]{0,1:T(8,128)(2,1)} %copy.136), channel_id=1, replica_groups=mesh['dp'=2,'wide'=4,'narrow'=4] {'narrow'}, dimensions={1}, use_global_device_ids=true | all-gather | bytes 800000 | tf_op jit(solution)/shard_map/all_gather | solution.py:158
  113.8 22.2 %all-gather.2 = f32[4,400,3]{1,2,0:T(4,128)S(1)} all-gather(f32[1,400,3]{1,2,0:T(4,128)S(1)} %maximum_bitcast_fusion.1), channel_id=1, replica_groups=mesh['dp'=2,'wide'=4,'narrow'=4] {'wide'}, dimensions={0}, use_global_device_ids=true | all-gather | bytes 24000 | tf_op jit(solution)/shard_map/all_gather | solution.py:162
  136.1 10.8 %all-gather.1 = f32[4,2,400]{2,1,0:T(2,128)S(1)} all-gather(f32[1,2,400]{2,1,0:T(2,128)S(1)} %bitcast.232), channel_id=2, replica_groups=mesh['dp'=2,'wide'=4,'narrow'=4] {'narrow'}, dimensions={0}, use_global_device_ids=true | all-gather | bytes 16000 | tf_op jit(solution)/shard_map/all_gather | solution.py:165
  167.6 20.0 %all_to_all.76 = f32[4,128,400]{1,2,0:T(8,128)S(1)} all-to-all(f32[4,128,400]{1,2,0:T(8,128)S(1)} %copy_bitcast_fusion), channel_id=1, replica_groups=mesh['dp'=2,'wide'=4,'narrow'=4] {'wide'}, dimensions={0} | all-to-all | bytes 1638400 | tf_op jit(solution)/shard_map/all_to_all | solution.py:73
  191.3 21.3 %all-gather.19.cloned.1.call-done = bf16[1600,1600]{1,0:T(8,128)(2,1)} async-done(((bf16[200,1600]{1,0:T(8,128)(2,1)}), bf16[1600,1600]{1,0:T(8,128)(2,1)}) %all-gather.19.cloned.1.call-update) | async-done | bytes 5120016 | tf_op jit(solution)/shard_map/all_gather | solution.py:160
  212.6 39.6 %all-gather.17.cloned.1.call-done = bf16[512,1600]{0,1:T(8,128)(2,1)} async-done(((bf16[128,1600]{0,1:T(8,128)(2,1)}), bf16[512,1600]{0,1:T(8,128)(2,1)}) %all-gather.17.cloned.1.call-update) | async-done | bytes 1638416 | tf_op jit(solution)/shard_map/all_gather | solution.py:61
  252.2 7.9 convolution_add_fusion
  260.1 31.1 %all-gather.23.cloned.1.call-done = bf16[512,1600]{0,1:T(8,128)(2,1)} async-done(((bf16[128,1600]{0,1:T(8,128)(2,1)}), bf16[512,1600]{0,1:T(8,128)(2,1)}) %all-gather.23.cloned.1.call-update) | async-done | bytes 1638416 | tf_op jit(solution)/shard_map/all_gather | solution.py:61
  291.2 43.0 %all-gather.21.cloned.1.call-done = bf16[1600,1600]{1,0:T(8,128)(2,1)} async-done(((bf16[200,1600]{1,0:T(8,128)(2,1)}), bf16[1600,1600]{1,0:T(8,128)(2,1)}) %all-gather.21.cloned.1.call-update) | async-done | bytes 5120016 | tf_op jit(solution)/shard_map/all_gather | solution.py:161
  334.2 9.2 %fusion.89 = (f32[1600]{0:T(1024)S(1)}, bf16[512,1600]{0,1:T(8,128)(2,1)S(1)}) fusion(f32[512,1600]{0,1:T(8,128)} %convolution_add_fusion, bf16[1600,1600]{1,0:T(8,128)(2,1)} %all-gather.21.cloned.1.call-done, bf16[512,1600]{0,1:T(8,128)(2,1)} %all-gather.23.cloned.1.call-done), kind=kOutput, calls=%fused_computation.128 | convolution fusion | flops 2637822464 | bytes 11680000 | tf_op jit(solution)/shard_map/dot_general | solution.py:30
  355.1 8.0 convolution_convert_fusion.6
  366.7 8.6 %fusion.2 = bf16[1600,1600]{0,1:T(8,128)(2,1)} fusion(bf16[512,1600]{0,1:T(8,128)(2,1)} %all-gather.23.cloned.1.call-done, f32[512,1600]{0,1:T(8,128)} %convolution_add_fusion), kind=kOutput, calls=%fused_computation.5 | convolution fusion | flops 2631372800 | bytes 10035200 | tf_op jit(solution)/shard_map/dot_general | solution.py:30
  375.4 7.5 convolution_convert_fusion.1
  392.1 37.9 %reduce-scatter.25.cloned.1.call-done = bf16[128,1600]{1,0:T(8,128)(2,1)} async-done(((bf16[512,1600]{1,0:T(8,128)(2,1)}), bf16[128,1600]{1,0:T(8,128)(2,1)}) %reduce-scatter.25.cloned.1.call-update) | async-done | bytes 409616
  464.0 90.0 %all-reduce.9.cloned.1.call-done = bf16[1600,1600]{0,1:T(8,128)(2,1)} async-done(((bf16[1600,1600]{0,1:T(8,128)(2,1)}), bf16[1600,1600]{0,1:T(8,128)(2,1)}) %all-reduce.9.cloned.1.call-update) | async-done | bytes 5120016
  560.9 59.0 %reduce-scatter.35.cloned.1.call-done = bf16[200,1600]{1,0:T(8,128)(2,1)} async-done(((bf16[1600,1600]{1,0:T(8,128)(2,1)}), bf16[200,1600]{1,0:T(8,128)(2,1)}) %reduce-scatter.35.cloned.1.call-update) | async-done | bytes 640016
  628.0 58.2 %reduce-scatter.33.cloned.1.call-done = bf16[200,1600]{1,0:T(8,128)(2,1)} async-done(((bf16[1600,1600]{1,0:T(8,128)(2,1)}), bf16[200,1600]{1,0:T(8,128)(2,1)}) %reduce-scatter.33.cloned.1.call-update) | async-done | bytes 640016
  701.8 7.7 all-to-all-done.1
  717.0 8.8 %all-reduce.4 = (f32[512,1]{0,1:T(1,128)S(1)}, f32[512,1]{0,1:T(1,128)S(1)}) all-reduce(f32[512,1]{0,1:T(1,128)S(1)} %bitcast.245, f32[512,1]{0,1:T(1,128)S(1)} %bitcast.246), channel_id=1, replica_groups=mesh['dp'=2,'wide'=4,'narrow'=4] {'wide'}, use_global_device_ids=true, to_apply=%region_16.17 | all-reduce | flops 1024 | bytes 8192 | tf_op jit(solution)/shard_map/psum | solution.py:34
  727.0 60.0 %all-reduce.11.cloned.1.call-done = (f32[3,1600]{1,0:T(4,128)}, f32[5,1600]{1,0:T(8,128)}, f32[6400]{0:T(1024)}) async-done(((f32[3,1600]{1,0:T(4,128)}, f32[5,1600]{1,0:T(8,128)}, f32[6400]{0:T(1024)}), (f32[3,1600]{1,0:T(4,128)}, f32[5,1600]{1,0:T(8,128)}, f32[6400]{0:T(1024)})) %all-reduce.11.cloned.1.call-update) | async-done | bytes 76816 | tf_op jit(solution)/shard_map/psum | solution.py:253
  (196 shorter events, 167.1 us)
Async XLA Ops:
  8.0 95.0 %copy-start = (f32[400,1600]{1,0:T(8,128)S(1)}, f32[400,1600]{1,0:T(8,128)}, u32[]{:S(2)}) copy-start(f32[400,1600]{1,0:T(8,128)} %param.26) | copy-start | bytes 7680004
  8.0 56.5 %all-gather.13.cloned.1.call-start = ((), (), s32[]{:S(2)}) async-start(), calls=%async_computation.11 | async-start | bytes 4608000 | tf_op jit(solution)/shard_map/all_gather | solution.py:156
  18.0 129.2 %reduce-scatter.23.cloned.1.call-start = ((), (), s32[]{:S(2)}) async-start(), calls=%async_computation.20 | async-start | bytes 6225920
  80.3 81.7 %all-gather.15.cloned.1.call-start = ((), (), s32[]{:S(2)}) async-start(), calls=%async_computation.12 | async-start | bytes 5990400 | tf_op jit(solution)/shard_map/all_gather | solution.py:159
  103.0 109.6 %all-gather.19.cloned.1.call-start = ((), (), s32[]{:S(2)}) async-start(), calls=%async_computation.14 | async-start | bytes 5990400 | tf_op jit(solution)/shard_map/all_gather | solution.py:160
  104.0 43.1 %collective-permute-start = (s32[1,128]{1,0:T(1,128)S(1)}, s32[1,128]{1,0:T(1,128)S(1)}, u32[]{:S(2)}, u32[]{:S(2)}) collective-permute-start(s32[1,128]{1,0:T(1,128)S(1)} %copy-done.26), channel_id=1, source_target_pairs={{0,0},{4,1},{8,2},{12,3},{1,4},{5,5},{9,6},{13,7},{2,8},{6,9},{10,... | collective-permute-start | bytes 1544 | tf_op jit(solution)/shard_map/ppermute | solution.py:152
  109.5 45.4 %all-to-all-start = ((f32[4,128,400]{1,2,0:T(8,128)}), f32[4,128,400]{1,2,0:T(8,128)}, u32[]{:S(2)}, u32[]{:S(2)}) async-start(f32[4,128,400]{1,2,0:T(8,128)} %copy_bitcast_fusion.1), calls=%async_computation | async-start | bytes 1638400 | tf_op jit(solution)/shard_map/all_to_all | solution.py:73
  113.7 138.5 %all-gather.17.cloned.1.call-start = ((), (), s32[]{:S(2)}) async-start(), calls=%async_computation.13 | async-start | bytes 2048000 | tf_op jit(solution)/shard_map/all_gather | solution.py:61
  167.5 123.7 %all-gather.23.cloned.1.call-start = ((), (), s32[]{:S(2)}) async-start(), calls=%async_computation.16 | async-start | bytes 2048000 | tf_op jit(solution)/shard_map/all_gather | solution.py:61
  188.5 145.7 %all-gather.21.cloned.1.call-start = ((), (), s32[]{:S(2)}) async-start(), calls=%async_computation.15 | async-start | bytes 5990400 | tf_op jit(solution)/shard_map/all_gather | solution.py:161
  190.8 200.0 %reduce-scatter.27.cloned.1.call-start = ((), (), s32[]{:S(2)}) async-start(), calls=%async_computation.22 | async-start | bytes 2129920
  354.9 75.0 %reduce-scatter.25.cloned.1.call-start = ((), (), s32[]{:S(2)}) async-start(), calls=%async_computation.21 | async-start | bytes 2129920
  366.7 187.4 %all-reduce.9.cloned.1.call-start = ((), (), s32[]{:S(2)}) async-start(), calls=%async_computation.25 | async-start | bytes 10649600
  375.4 244.5 %reduce-scatter.35.cloned.1.call-start = ((), (), s32[]{:S(2)}) async-start(), calls=%async_computation.27 | async-start | bytes 5990400
  382.9 238.0 %all-gather.25.cloned.1.call-start = ((), (), s32[]{:S(2)}) async-start(), calls=%async_computation.17 | async-start | bytes 6144000 | tf_op jit(solution)/shard_map/all_gather | solution.py:57
  457.0 229.2 %reduce-scatter.33.cloned.1.call-start = ((), (), s32[]{:S(2)}) async-start(), calls=%async_computation.26 | async-start | bytes 5990400
  462.2 236.6 %all-gather.29.cloned.1.call-start = ((), (), s32[]{:S(2)}) async-start(), calls=%async_computation.19 | async-start | bytes 1996800 | tf_op jit(solution)/shard_map/all_gather | solution.py:202
  464.0 92.9 %copy-start.4 = (f32[400,512]{1,0:T(8,128)S(1)}, f32[400,512]{1,0:T(8,128)}, u32[]{:S(2)}) copy-start(f32[400,512]{1,0:T(8,128)} %param.16) | copy-start | bytes 2457604
  556.9 157.1 %all-gather.27.cloned.1.call-start = ((), (), s32[]{:S(2)}) async-start(), calls=%async_computation.18 | async-start | bytes 1996800 | tf_op jit(solution)/shard_map/all_gather | solution.py:202
  619.9 167.0 %all-reduce.11.cloned.1.call-start = ((), (), s32[]{:S(2)}) async-start(), calls=%async_computation.28 | async-start | bytes 217088 | tf_op jit(solution)/shard_map/psum | solution.py:253
  628.0 164.8 %reduce-scatter.31.cloned.1.call-start = ((), (), s32[]{:S(2)}) async-start(), calls=%async_computation.24 | async-start | bytes 1024000
  688.5 110.5 %reduce-scatter.29.cloned.1.call-start = ((), (), s32[]{:S(2)}) async-start(), calls=%async_computation.23 | async-start | bytes 4608000 | tf_op jit(solution)/shard_map/reduce_scatter | solution.py:222
  695.2 14.2 %all-to-all-start.1 = ((f32[128,4,400]{0,2,1:T(8,128)}), f32[128,4,400]{0,2,1:T(8,128)S(1)}, u32[]{:S(2)}, u32[]{:S(2)}) async-start(f32[128,4,400]{0,2,1:T(8,128)} %bitcast.30), calls=%async_computation.1 | async-start | bytes 1638400 | tf_op jit(solution)/shard_map/all_to_all | solution.py:77
  709.5 16.3 %all-to-all-start.3 = ((f32[128,4,400]{0,2,1:T(8,128)}), f32[128,4,400]{0,2,1:T(8,128)S(1)}, u32[]{:S(2)}, u32[]{:S(2)}) async-start(f32[128,4,400]{0,2,1:T(8,128)} %bitcast.38), calls=%async_computation.3 | async-start | bytes 1638400 | tf_op jit(solution)/shard_map/all_to_all | solution.py:77
  (27 other events, 346.2 us)
Sparse Core Ops, SparseCore 0:
  18.1 46.3 all-gather.12
  80.4 66.6 reduce-scatter.22
  457.2 58.8 all-gather.24
  557.0 10.3 all-gather.28
  620.0 10.3 all-gather.26
  636.3 150.6 all-reduce.10
Sparse Core Ops, SparseCore 1:
  103.1 58.8 all-gather.14
  164.3 48.3 all-gather.18
  214.6 37.5 all-gather.16
  254.3 36.8 all-gather.22
  293.7 40.4 all-gather.20
  355.0 35.8 reduce-scatter.26
  393.6 36.3 reduce-scatter.24
  433.1 120.9 all-reduce.8
  557.4 62.5 reduce-scatter.34
  623.3 62.8 reduce-scatter.32
  689.0 22.4 reduce-scatter.30
  713.7 49.0 reduce-scatter.28

commit v3 on v2

--- a/solution.py
+++ b/solution.py
@@ -3,6 +3,8 @@
 import jax
 import jax.numpy as jnp
 from jax import lax
+from jax.experimental import pallas as pl
+from jax.experimental.pallas import tpu as pltpu
 from jax.sharding import PartitionSpec as P
 
 HEADS = 25
@@ -114,6 +116,404 @@
     value_grad = jnp.einsum("hij,ihd->jhd", probs_full.astype(BF), cot_heads, preferred_element_type=F32)
     stacked = jnp.stack([query_grad, key_grad, value_grad], axis=1)
     return stacked.reshape(heads_all.shape[0], 3, HEADS * HEAD)
+
+
+MESH = pl.DeviceIdType.MESH
+VMEM_LIMIT = 60 * 1024 * 1024
+
+
+def params(collective_id):
+    return pltpu.CompilerParams(
+        collective_id=collective_id, has_side_effects=True, vmem_limit_bytes=VMEM_LIMIT
+    )
+
+
+def in_vmem(count):
+    return [pl.BlockSpec(memory_space=pltpu.VMEM)] * count
+
+
+def shape_of(shape, dtype):
+    return jax.ShapeDtypeStruct(shape, dtype)
+
+
+def square_peers():
+    me = lax.axis_index("wide")
+    return me, me + 1 - 2 * lax.rem(me, 2), lax.rem(me + 2, 4), 3 - me
+
+
+def greet(axis, peers):
+    barrier = pltpu.get_barrier_semaphore()
+    for peer in peers:
+        pl.semaphore_signal(barrier, inc=1, device_id={axis: peer}, device_id_type=MESH)
+    pl.semaphore_wait(barrier, len(peers))
+
+
+def remote(src, dst, send_sem, recv_sem, axis, peer):
+    return pltpu.make_async_remote_copy(
+        src_ref=src,
+        dst_ref=dst,
+        send_sem=send_sem,
+        recv_sem=recv_sem,
+        device_id={axis: peer},
+        device_id_type=MESH,
+    )
+
+
+def start_kernel(
+    x_ref, dy_ref, gain_ref, shift_ref, vec_ref,
+    norm_ref, stat_ref, xt_ref, dyt_ref, vecs_ref,
+    sums, all_sums, send_sem, recv_sem, local_sem,
+):
+    feats, tokens = x_ref.shape
+    wide = 4
+    block = tokens // wide
+    me, xp, yp, dg = square_peers()
+    peers = (xp, yp, dg)
+    greet("wide", peers)
+    x = x_ref[...]
+    sums[...] = jnp.zeros_like(sums)
+    stat_ref[...] = jnp.zeros_like(stat_ref)
+    sums[0:1, :] = jnp.sum(x, axis=0, keepdims=True)
+    sums[1:2, :] = jnp.sum(x * x, axis=0, keepdims=True)
+    copies = []
+
+    def send(k, j, src, dst, peer):
+        copy = remote(src, dst, send_sem.at[k, j], recv_sem.at[k, j], "wide", peer)
+        copy.start()
+        copies.append(copy)
+
+    mine = pl.ds(me * feats, feats)
+    for j, peer in enumerate(peers):
+        send(0, j, sums, all_sums.at[me], peer)
+    for j, peer in enumerate(peers):
+        send(1, j, vec_ref, vecs_ref.at[me], peer)
+        theirs = pl.ds(pl.multiple_of(peer * block, 128), block)
+        send(2, j, x_ref.at[:, theirs], xt_ref.at[mine, :], peer)
+        send(3, j, dy_ref.at[:, theirs], dyt_ref.at[mine, :], peer)
+    own = pl.ds(pl.multiple_of(me * block, 128), block)
+    xt_ref[mine, :] = x_ref[:, own]
+    dyt_ref[mine, :] = dy_ref[:, own]
+    vecs_ref[me] = vec_ref[...]
+    for j in range(3):
+        copies[j].wait()
+    total = sums[...]
+    for peer in peers:
+        total = total + all_sums[peer]
+    width = feats * wide
+    mean = total[0:1, :] / width
+    inv = lax.rsqrt(total[1:2, :] / width - mean * mean + EPS)
+    stat_ref[0:1, :] = mean
+    stat_ref[1:2, :] = inv
+    norm_ref[...] = ((x - mean) * inv * gain_ref[...] + shift_ref[...]).astype(BF)
+    for copy in copies[3:]:
+        copy.wait()
+
+
+def start_stage(x, dy, gain, shift, vec):
+    feats, tokens = x.shape
+    return pl.pallas_call(
+        start_kernel,
+        out_shape=(
+            shape_of((feats, tokens), BF),
+            shape_of((8, tokens), F32),
+            shape_of((4 * feats, tokens // 4), F32),
+            shape_of((4 * feats, tokens // 4), F32),
+            shape_of((4,) + vec.shape, F32),
+        ),
+        in_specs=in_vmem(5),
+        out_specs=tuple(in_vmem(5)),
+        scratch_shapes=[
+            pltpu.VMEM((8, tokens), F32),
+            pltpu.VMEM((4, 8, tokens), F32),
+            pltpu.SemaphoreType.DMA((4, 3)),
+            pltpu.SemaphoreType.DMA((4, 3)),
+            pltpu.SemaphoreType.DMA,
+        ],
+        compiler_params=params(1),
+        cost_estimate=pl.CostEstimate(flops=10**9, bytes_accessed=30 * 10**6, transcendentals=0),
+        name="start_stage",
+    )(x, dy, gain, shift, vec)
+
+
+def qkv_kernel(
+    norm_ref, w_ref, bias_ref, out_ref, acc, first_out, first_in, second_out, second_in, send_sem, recv_sem
+):
+    pieces, feats, cols = w_ref.shape
+    tokens = norm_ref.shape[1]
+    block = tokens // 4
+    me, xp, yp, dg = square_peers()
+    greet("wide", (xp, yp))
+
+    def rows(index):
+        return pl.ds(pl.multiple_of(index * block, block), block)
+
+    def ways(p):
+        turn = lax.rem(p, 2)
+        return xp * (1 - turn) + yp * turn, yp * (1 - turn) + xp * turn
+
+    def first_copy(p):
+        return remote(first_out.at[p], first_in.at[p], send_sem.at[0, p], recv_sem.at[0, p], "wide", ways(p)[0])
+
+    def second_copy(p):
+        return remote(second_out.at[p], second_in.at[p], send_sem.at[1, p], recv_sem.at[1, p], "wide", ways(p)[1])
+
+    def issue(p, carry):
+        acc[p] = dot(norm_ref[...], w_ref[p], 0, 0)
+        first_out[p, 0] = acc[p, rows(ways(p)[0]), :].astype(BF)
+        first_out[p, 1] = acc[p, rows(dg), :].astype(BF)
+        first_copy(p).start()
+        return carry
+
+    lax.fori_loop(0, pieces, issue, 0)
+
+    def middle(p, carry):
+        first_copy(p).wait()
+        second_out[p] = (acc[p, rows(ways(p)[1]), :] + first_in[p, 1].astype(F32)).astype(BF)
+        second_copy(p).start()
+        return carry
+
+    lax.fori_loop(0, pieces, middle, 0)
+
+    def last(p, carry):
+        second_copy(p).wait()
+        total = acc[p, rows(me), :] + first_in[p, 0].astype(F32) + second_in[p].astype(F32)
+        out_ref[p] = (total + bias_ref[p]).astype(BF)
+        return carry
+
+    lax.fori_loop(0, pieces, last, 0)
+
+
+def qkv_stage(norm, w, bias):
+    pieces, feats, cols = w.shape
+    tokens = norm.shape[1]
+    block = tokens // 4
+    return pl.pallas_call(
+        qkv_kernel,
+        out_shape=shape_of((pieces, block, cols), BF),
+        in_specs=in_vmem(3),
+        out_specs=pl.BlockSpec(memory_space=pltpu.VMEM),
+        scratch_shapes=[
+            pltpu.VMEM((pieces, tokens, cols), F32),
+            pltpu.VMEM((pieces, 2, block, cols), BF),
+            pltpu.VMEM((pieces, 2, block, cols), BF),
+            pltpu.VMEM((pieces, block, cols), BF),
+            pltpu.VMEM((pieces, block, cols), BF),
+            pltpu.SemaphoreType.DMA((2, pieces)),
+            pltpu.SemaphoreType.DMA((2, pieces)),
+        ],
+        compiler_params=params(2),
+        cost_estimate=pl.CostEstimate(flops=3 * 10**10, bytes_accessed=10**8, transcendentals=0),
+        name="qkv_stage",
+    )(norm, w, bias)
+
+
+def spread_kernel(own_ref, all_ref, send_sem, recv_sem):
+    pieces, block, cols = own_ref.shape
+    me, xp, yp, dg = square_peers()
+    greet("wide", (xp, yp))
+
+    def rows(index):
+        return pl.ds(pl.multiple_of(index * block, block), block)
+
+    def ways(p):
+        turn = lax.rem(p, 2)
+        return xp * (1 - turn) + yp * turn, yp * (1 - turn) + xp * turn
+
+    def own_copy(p, k):
+        return remote(
+            own_ref.at[p], all_ref.at[p, rows(me), :], send_sem.at[k, p], recv_sem.at[k, p], "wide", ways(p)[k]
+        )
+
+    def pass_copy(p):
+        source = all_ref.at[p, rows(ways(p)[0]), :]
+        return remote(source, source, send_sem.at[2, p], recv_sem.at[2, p], "wide", ways(p)[1])
+
+    def issue(p, carry):
+        own_copy(p, 0).start()
+        return carry
+
+    def issue_second(p, carry):
+        own_copy(p, 1).start()
+        all_ref[p, rows(me), :] = own_ref[p]
+        return carry
+
+    def relay(p, carry):
+        own_copy(p, 0).wait()
+        pass_copy(p).start()
+        return carry
+
+    def finish(p, carry):
+        own_copy(p, 1).wait()
+        pass_copy(p).wait()
+        return carry
+
+    for step in (issue, issue_second, relay, finish):
+        lax.fori_loop(0, pieces, step, 0)
+
+
+def spread_stage(own):
+    pieces, block, cols = own.shape
+    return pl.pallas_call(
+        spread_kernel,
+        out_shape=shape_of((pieces, 4 * block, cols), BF),
+        in_specs=in_vmem(1),
+        out_specs=pl.BlockSpec(memory_space=pltpu.VMEM),
+        scratch_shapes=[pltpu.SemaphoreType.DMA((3, pieces)), pltpu.SemaphoreType.DMA((3, pieces))],
+        compiler_params=params(3),
+        cost_estimate=pl.CostEstimate(flops=3 * 10**10, bytes_accessed=10**8, transcendentals=0),
+        name="spread_stage",
+    )(own)
+
+
+def line_sides():
+    n, count = lax.axis_index("narrow"), lax.axis_size("narrow")
+    return n, count, n > 0, n < count - 1
+
+
+def greet_line(n, has_down, has_up):
+    barrier = pltpu.get_barrier_semaphore()
+    for has, peer in ((has_down, n - 1), (has_up, n + 1)):
+
+        @pl.when(has)
+        def _():
+            pl.semaphore_signal(barrier, inc=1, device_id={"narrow": peer}, device_id_type=MESH)
+
+    pl.semaphore_wait(barrier, has_down.astype(jnp.int32) + has_up.astype(jnp.int32))
+
+
+def line_gather_kernel(own_ref, all_ref, send_sem, recv_sem):
+    n, count, has_down, has_up = line_sides()
+    greet_line(n, has_down, has_up)
+
+    def copy(block, way, src=None):
+        place = all_ref.at[block]
+        return remote(
+            place if src is None else src, place, send_sem.at[way, block], recv_sem.at[block], "narrow", n + 1 - 2 * way
+        )
+
+    @pl.when(has_up)
+    def _():
+        copy(n, 0, own_ref).start()
+
+    @pl.when(has_down)
+    def _():
+        copy(n, 1, own_ref).start()
+
+    all_ref[n] = own_ref[...]
+    for step in range(1, count):
+        below, above = n - step, n + step
+
+        @pl.when(below >= 0)
+        def _():
+            copy(below, 0).wait_recv()
+
+            @pl.when(has_up)
+            def _():
+                copy(below, 0).start()
+
+        @pl.when(above < count)
+        def _():
+            copy(above, 1).wait_recv()
+
+            @pl.when(has_down)
+            def _():
+                copy(above, 1).start()
+
+    for step in range(count):
+        below, above = n - step, n + step
+
+        @pl.when((below >= 0) & has_up)
+        def _():
+            copy(below, 0).wait_send()
+
+        @pl.when((above < count) & has_down)
+        def _():
+            copy(above, 1).wait_send()
+
+
+def line_gather(own):
+    count = lax.axis_size("narrow")
+    return pl.pallas_call(
+        line_gather_kernel,
+        out_shape=shape_of((count,) + own.shape, own.dtype),
+        in_specs=in_vmem(1),
+        out_specs=pl.BlockSpec(memory_space=pltpu.VMEM),
+        scratch_shapes=[pltpu.SemaphoreType.DMA((2, count)), pltpu.SemaphoreType.DMA((count,))],
+        compiler_params=params(4),
+        cost_estimate=pl.CostEstimate(flops=2 * 10**10, bytes_accessed=7 * 10**7, transcendentals=0),
+        name="line_gather",
+    )(own)
+
+
+def line_sum_kernel(part_ref, out_ref, leave, arrive, send_sem, recv_sem):
+    n, count, has_down, has_up = line_sides()
+    greet_line(n, has_down, has_up)
+
+    def copy(way, block):
+        return remote(
+            leave.at[way, block],
+            arrive.at[way, block],
+            send_sem.at[way, block],
+            recv_sem.at[way, block],
+            "narrow",
+            n + 1 - 2 * way,
+        )
+
+    def turn(way, block, sends, joins):
+        @pl.when(sends & joins)
+        def _():
+            copy(way, block).wait_recv()
+            leave[way, block] = (part_ref[block].astype(F32) + arrive[way, block].astype(F32)).astype(BF)
+            copy(way, block).start()
+
+        @pl.when(sends & jnp.logical_not(joins))
+        def _():
+            leave[way, block] = part_ref[block]
+            copy(way, block).start()
+
+    for step in range(count - 1):
+        turn(0, count - 1 - step, n < count - 1 - step, has_down)
+        turn(1, step, n > step, has_up)
+    out_ref[...] = part_ref[n].astype(F32)
+
+    @pl.when(has_down)
+    def _():
+        copy(0, n).wait_recv()
+        out_ref[...] += arrive[0, n].astype(F32)
+
+    @pl.when(has_up)
+    def _():
+        copy(1, n).wait_recv()
+        out_ref[...] += arrive[1, n].astype(F32)
+
+    for step in range(count - 1):
+
+        @pl.when(n < count - 1 - step)
+        def _():
+            copy(0, count - 1 - step).wait_send()
+
+        @pl.when(n > step)
+        def _():
+            copy(1, step).wait_send()
+
+
+def line_sum(part):
+    count, block, cols = part.shape
+    return pl.pallas_call(
+        line_sum_kernel,
+        out_shape=shape_of((block, cols), F32),
+        in_specs=in_vmem(1),
+        out_specs=pl.BlockSpec(memory_space=pltpu.VMEM),
+        scratch_shapes=[
+            pltpu.VMEM((2, count, block, cols), BF),
+            pltpu.VMEM((2, count, block, cols), BF),
+            pltpu.SemaphoreType.DMA((2, count)),
+            pltpu.SemaphoreType.DMA((2, count)),
+        ],
+        compiler_params=params(5),
+        cost_estimate=pl.CostEstimate(flops=2 * 10**10, bytes_accessed=7 * 10**7, transcendentals=0),
+        name="line_sum",
+    )(part)
 
 
 def own_half(values, axis):
@@ -159,9 +559,6 @@
     wo_all = lax.all_gather(wo_mine, ("wide", "dp"), axis=0, tiled=True)
     wf_all = lax.all_gather(own_half(w_fc.astype(BF), 0), ("wide", "dp"), axis=0, tiled=True)
     wp_all = lax.all_gather(own_half(w_proj.astype(BF), 0), ("wide", "dp"), axis=0, tiled=True)
-    b_out_full, gain_two_full, shift_two_full = lax.all_gather(
-        jnp.stack([b_out, ln2_gain, ln2_shift]), "wide", axis=1, tiled=True
-    )
     bias_qv = lax.all_gather(b_qv, "narrow", axis=0).reshape(narrow, 1, 2, part)
     bias_three = jnp.concatenate(
         [bias_qv[:, :, 0], jnp.zeros((narrow, 1, part), F32), bias_qv[:, :, 1]], axis=2
@@ -169,14 +566,30 @@
 
     rows_input = block_input.T
     rows_cot = block_cotangent.T
-    x_tok = to_tokens(rows_input)
-    dy_tok = to_tokens(rows_cot)
+    square = wide == 4
+    if square:
+        vec = jnp.zeros((8, feats), F32)
+        vec = vec.at[0].set(b_out).at[1].set(ln2_gain).at[2].set(ln2_shift)
+        norm_t, stats, x_tok, dy_tok, vecs = start_stage(
+            block_input, block_cotangent, ln1_gain[:, None], ln1_shift[:, None], vec
+        )
+        x_tok, dy_tok = x_tok.T, dy_tok.T
+        b_out_full, gain_two_full, shift_two_full = (vecs[:, i].reshape(width) for i in range(3))
+        norm_one = norm_t.T
+        inv_one = stats[1][:, None]
+        normed_one = (rows_input - stats[0][:, None]) * inv_one
+        qkv_rows = qkv_stage(norm_t, wq_all, bias_three)
+    else:
+        b_out_full, gain_two_full, shift_two_full = lax.all_gather(
+            jnp.stack([b_out, ln2_gain, ln2_shift]), "wide", axis=1, tiled=True
+        )
+        x_tok = to_tokens(rows_input)
+        dy_tok = to_tokens(rows_cot)
+        normed_one, inv_one, norm_one = norm_forward(rows_input, ln1_gain, ln1_shift)
+        qkv_part = jnp.einsum("tk,nkc->tnc", norm_one, wq_all, preferred_element_type=F32)
+        qkv_rows = sum_tokens(qkv_part).transpose(1, 0, 2)
+        qkv_rows = (qkv_rows + bias_three).astype(BF)
     cot_all = gather_narrow(dy_tok.astype(BF))
-
-    normed_one, inv_one, norm_one = norm_forward(rows_input, ln1_gain, ln1_shift)
-    qkv_part = jnp.einsum("tk,nkc->tnc", norm_one, wq_all, preferred_element_type=F32)
-    qkv_rows = sum_tokens(qkv_part.transpose(0, 1, 2)).transpose(1, 0, 2)
-    qkv_rows = (qkv_rows + bias_three).astype(BF)
     heads_all = qkv_rows.reshape(narrow, -1, 3, part).transpose(1, 2, 0, 3).reshape(-1, 3, width)
     attended, log_total = attend_forward(heads_all, allowed)
     residual = x_tok + dot(attended, wo_all, 1, 1) + b_out_full
@@ -184,7 +597,7 @@
     inv_two = lax.rsqrt(jnp.mean(residual * residual, axis=1, keepdims=True) - mean_two * mean_two + EPS)
     normed_two = (residual - mean_two) * inv_two
     norm_two = (normed_two * gain_two_full + shift_two_full).astype(BF)
-    norm_two_all = gather_narrow(norm_two)
+    norm_two_all = line_gather(norm_two).reshape(-1, width)
     pre_act = dot(norm_two_all, wf_all, 1, 0) + b_fc
     hidden = gelu_value(pre_act).astype(BF)
     out_tok = residual + sum_narrow(dot(hidden, wp_all, 1, 1))
@@ -192,7 +605,7 @@
 
     pre_grad = dot(cot_all, wp_all, 1, 0) * gelu_slope(pre_act)
     pre_cot = pre_grad.astype(BF)
-    norm_two_grad = sum_narrow(dot(pre_cot, wf_all, 1, 1))
+    norm_two_grad = line_sum(dot(pre_cot, wf_all, 1, 1).astype(BF).reshape(narrow, -1, width))
 
     def reduce_wide(grad):
         total = lax.psum_scatter(grad.astype(BF), ("wide", "dp"), scatter_dimension=0, tiled=True)
@@ -215,10 +628,14 @@
     grad_w_out = share(wo_grad)
 
     qkv_grad = attend_backward(heads_all, allowed, log_total, attended_cot)
-    qkv_cot = qkv_grad.astype(BF).reshape(-1, 3, narrow, part).transpose(0, 2, 1, 3)
-    qkv_cot_all = gather_tokens(qkv_cot.reshape(-1, narrow, 3 * part))
-    norm_one_grad = jnp.einsum("tnc,nkc->tk", qkv_cot_all, wq_all, preferred_element_type=F32)
-    wq_grad = jnp.einsum("tk,tnc->nkc", norm_one, qkv_cot_all, preferred_element_type=F32).astype(BF)
+    qkv_cot = qkv_grad.astype(BF).reshape(-1, 3, narrow, part).transpose(2, 0, 1, 3)
+    qkv_cot = qkv_cot.reshape(narrow, -1, 3 * part)
+    if square:
+        qkv_cot_all = spread_stage(qkv_cot)
+    else:
+        qkv_cot_all = lax.all_gather(qkv_cot, "wide", axis=1, tiled=True)
+    norm_one_grad = jnp.einsum("ntc,nkc->tk", qkv_cot_all, wq_all, preferred_element_type=F32)
+    wq_grad = jnp.einsum("tk,ntc->nkc", norm_one, qkv_cot_all, preferred_element_type=F32).astype(BF)
     wq_grad = lax.psum_scatter(
         wq_grad.reshape(narrow * feats, 3 * part), ("narrow", "dp"), scatter_dimension=0, tiled=True
     )

time: 824 us -> 764 us (0.927)
  Pallas kernels: 0 us -> 203 us
  waiting for transfers between devices: 498 us -> 302 us
  blocking collectives: 93.3 us -> 50.8 us
  local copies, waits for them, and re-layouts: 59.9 us -> 50.1 us
    pallas_call x0 -> x5, Pallas kernels: none -> 203 us  [the longest x1 70 us: qkv_stage(): pl.pallas_call(qkv_kernel, out_shape=shape_of((pieces, block, cols), BF),...]
    unnamed x25 -> x18, waiting for transfers between devices: 250 us -> 78 us
    psum x1, waiting for transfers between devices: 60 us -> 126 us  [local(): lax.psum((token_terms, feature_full, fc_full), ('dp', 'wide', 'narrow'))]
    reduce_scatter x1, waiting for transfers between devices: 0.01 us -> 47.5 us  [local(): lax.psum_scatter(wq_grad.reshape(narrow * feats, 3 * part), ('narrow', 'd...]
    all_gather x2 -> x1, waiting for transfers between devices: 70.7 us -> 26.8 us  [gather_narrow(): return lax.all_gather(values, 'narrow', axis=0, tiled=True)]
    all_gather x1, waiting for transfers between devices: 38.4 us -> 0.02 us  [local(): wq_all = lax.all_gather(wq_mine, ('narrow', 'dp'), axis=0, tiled=True)]
    all_gather x1, waiting for transfers between devices: 43 us -> 9.17 us  [local(): lax.all_gather(own_half(w_proj.astype(BF), 0), ('wide', 'dp'), axis=0, ti...]
    unnamed x72 -> x64, local copies, waits for them, and re-layouts: 33.6 us -> 10 us
  transfers between devices with their start and end apart: 22 -> 17, of which waited for: 13 -> 9; matrix products, arithmetic and copies ran while one was open for 17% -> 21% of each run, Pallas kernels for 0% -> 27%
where the time goes in v3:
time: 764 us; the launch traced here: 753 us
  waiting for transfers between devices  302 us (40%)
  Pallas kernels  203 us (27%)
  matrix products  96.9 us (13%)
  blocking collectives  50.8 us (7%)
  local copies, waits for them, and re-layouts  50.1 us (7%)
  other arithmetic  20.9 us (3%)
  between operations  14.7 us (2%)
  starting transfers between devices  13.7 us (2%)
    psum x1, waiting for transfers between devices, local(): lax.psum((token_terms, feature_full, fc_full), ('dp', 'wide', 'narrow'))  126 us
    unnamed x18, waiting for transfers between devices  78 us
    pallas_call x1, Pallas kernels, qkv_stage(): pl.pallas_call(qkv_kernel, out_shape=shape_of((pieces, block, cols), BF),...  70 us
    dot_general x9, matrix products, dot(): lax.dot_general(a, b, (((ca,), (cb,)), ((), ())), preferred_element_type=...  61.2 us
    reduce_scatter x1, waiting for transfers between devices, local(): lax.psum_scatter(wq_grad.reshape(narrow * feats, 3 * part), ('narrow', 'd...  47.5 us
    pallas_call x1, Pallas kernels, spread_stage(): pl.pallas_call(spread_kernel, out_shape=shape_of((pieces, 4 * block, cols...  47.1 us
    pallas_call x1, Pallas kernels, line_sum(): pl.pallas_call(line_sum_kernel, out_shape=shape_of((block, cols), F32), i...  34 us
    pallas_call x1, Pallas kernels, line_gather(): pl.pallas_call(line_gather_kernel, out_shape=shape_of((count,) + own.shap...  30.1 us
  transfers between devices with their start and end apart: 17, of which 9 were waited for; matrix products, arithmetic and copies ran while one was open for 21% of the time, Pallas kernels for 27%

profile of v3, /device:TPU:17, one launch (start us, length us, event | category | flops | bytes accessed | tf_op | source)
XLA Modules:
  0.0 753.1 jit_solution(6260867678046681689)
XLA Ops:
  17.1 22.8 %all_gather.39 = bf16[200,1600]{0,1:T(8,128)(2,1)S(1)} all-gather(bf16[200,400]{0,1:T(8,128)(2,1)} %copy.201), channel_id=1, replica_groups=mesh['dp'=2,'wide'=4,'narrow'=4] {'narrow'}, dimensions={1}, use_global_device_ids=true | all-gather | bytes 800000 | tf_op jit(solution)/shard_map/all_gather | solution.py:558
  52.2 22.2 %start_stage.1 = (bf16[400,512]{1,0:T(8,128)(2,1)}, f32[8,512]{1,0:T(8,128)}, f32[1600,128]{1,0:T(8,128)}, f32[1600,128]{1,0:T(8,128)}, f32[4,8,400]{2,1,0:T(8,128)}) custom-call(f32[400,512]{1,0:T(8,128)} %x_ref.1, f32[400,512]{1,0:T(8,128)} %dy_ref.1, f32[400,1]{1,0:T(8,128)} %copy.159.gain_ref, f32[400,1]{1,0:T(8,128)} %copy.160.shift_ref, ...), custom_call_target="tpu_custom_call" | custom-call | flops 1000000000 | bytes 30000000 | tf_op jit(solution)/shard_map/start_stage/pallas_call | solution.py:214
  76.8 11.0 %all-gather.1 = f32[4,2,400]{2,1,0:T(2,128)S(1)} all-gather(f32[1,2,400]{2,1,0:T(2,128)S(1)} %bitcast.185), channel_id=2, replica_groups=mesh['dp'=2,'wide'=4,'narrow'=4] {'narrow'}, dimensions={0}, use_global_device_ids=true | all-gather | bytes 16000 | tf_op jit(solution)/shard_map/all_gather | solution.py:562
  90.3 70.0 %qkv_stage.1 = bf16[4,128,1200]{2,1,0:T(8,128)(2,1)} custom-call(bf16[400,512]{1,0:T(8,128)(2,1)} %get-tuple-element.56.norm_ref, bf16[4,400,1200]{2,1,0:T(8,128)(2,1)} %bitcast.201, f32[4,1,1200]{2,1,0:T(1,128)} %concatenate.12.bias_ref), custom_call_target="tpu_custom_call" | custom-call | flops 30000001024 | bytes 100000000 | tf_op jit(solution)/shard_map/qkv_stage/pallas_call | solution.py:290
  174.5 30.1 %line_gather.1 = bf16[4,128,1600]{2,1,0:T(8,128)(2,1)} custom-call(bf16[128,1600]{1,0:T(8,128)(2,1)} %add_convert_fusion.own_ref), custom_call_target="tpu_custom_call" | custom-call | flops 20000000000 | bytes 70000000 | tf_op jit(solution)/shard_map/line_gather/pallas_call | solution.py:436
  204.6 7.9 %convolution_add_fusion = f32[512,1600]{0,1:T(8,128)} fusion(bf16[512,1600]{1,0:T(8,128)(2,1)} %bitcast.203, bf16[1600,1600]{1,0:T(8,128)(2,1)} %all-gather.14.cloned.1.call-done, f32[1600]{0:T(1024)S(1)} %copy-done.27), kind=kOutput, calls=%fused_computation.15 | convolution fusion | flops 2622259200 | bytes 10041600 | tf_op jit(solution)/shard_map/dot_general | solution.py:32
  212.5 9.2 %all-gather.16.cloned.1.call-done = bf16[1600,1600]{1,0:T(8,128)(2,1)} async-done(((bf16[200,1600]{1,0:T(8,128)(2,1)}), bf16[1600,1600]{1,0:T(8,128)(2,1)}) %all-gather.16.cloned.1.call-update) | async-done | bytes 5120016 | tf_op jit(solution)/shard_map/all_gather | solution.py:561
  221.7 8.0 %convolution_convert_fusion.5 = bf16[512,1600]{0,1:T(8,128)(2,1)} fusion(bf16[1600,1600]{1,0:T(8,128)(2,1)} %all-gather.16.cloned.1.call-done, f32[512,1600]{0,1:T(8,128)} %convolution_add_fusion), kind=kOutput, calls=%fused_computation.17 | convolution fusion | flops 2629632000 | bytes 10035200 | tf_op jit(solution)/shard_map/dot_general | solution.py:32
  233.8 26.8 %all-gather.18.cloned.1.call-done = bf16[512,1600]{1,0:T(8,128)(2,1)} async-done(((bf16[128,1600]{1,0:T(8,128)(2,1)}), bf16[512,1600]{1,0:T(8,128)(2,1)}) %all-gather.18.cloned.1.call-update) | async-done | bytes 1638416 | tf_op jit(solution)/shard_map/all_gather | solution.py:63
  260.6 9.2 %fusion.81 = (f32[1600]{0:T(1024)S(1)}, bf16[512,1600]{0,1:T(8,128)(2,1)S(1)}) fusion(f32[512,1600]{0,1:T(8,128)} %convolution_add_fusion, bf16[512,1600]{1,0:T(8,128)(2,1)} %all-gather.18.cloned.1.call-done, bf16[1600,1600]{1,0:T(8,128)(2,1)} %all-gather.16.cloned.1.call-done), kind=kOutput, calls=%fused_computation.114 | convolution fusion | flops 2637822464 | bytes 11680000 | tf_op jit(solution)/shard_map/dot_general | solution.py:32
  271.0 7.1 convolution_convert_fusion.1
  278.2 8.2 %convolution_convert_fusion = bf16[1600,1600]{1,0:T(8,128)(2,1)} fusion(bf16[512,1600]{1,0:T(8,128)(2,1)} %all-gather.18.cloned.1.call-done, f32[512,1600]{0,1:T(8,128)} %convolution_add_fusion), kind=kOutput, calls=%fused_computation.2 | convolution fusion | flops 2631372800 | bytes 10035200 | tf_op jit(solution)/shard_map/dot_general | solution.py:32
  286.6 7.4 convolution_convert_fusion.4
  297.5 34.0 %line_sum.1 = f32[128,1600]{1,0:T(8,128)} custom-call(bf16[4,128,1600]{2,1,0:T(8,128)(2,1)} %bitcast.157), custom_call_target="tpu_custom_call" | custom-call | flops 20000000000 | bytes 70000000 | tf_op jit(solution)/shard_map/line_sum/pallas_call | solution.py:502
  366.0 47.1 %spread_stage.1 = bf16[4,512,1200]{2,1,0:T(8,128)(2,1)} custom-call(bf16[4,128,1200]{2,1,0:T(8,128)(2,1)} %copy.183.own_ref), custom_call_target="tpu_custom_call" | custom-call | flops 30000001024 | bytes 100000000 | tf_op jit(solution)/shard_map/spread_stage/pallas_call | solution.py:356
  413.2 7.1 fusion.29
  424.3 19.0 %reduce-scatter.27.cloned.1.call-done = bf16[200,1600]{1,0:T(8,128)(2,1)} async-done(((bf16[1600,1600]{1,0:T(8,128)(2,1)}), bf16[200,1600]{1,0:T(8,128)(2,1)}) %reduce-scatter.27.cloned.1.call-update) | async-done | bytes 640016
  443.3 6.9 convolution_convert_fusion.3
  456.2 11.6 %all-reduce.5 = (f32[512,1]{0,1:T(1,128)S(1)}, f32[512,1]{0,1:T(1,128)S(1)}) all-reduce(f32[512,1]{0,1:T(1,128)S(1)} %bitcast.199, f32[512,1]{0,1:T(1,128)S(1)} %bitcast.200), channel_id=1, replica_groups=mesh['dp'=2,'wide'=4,'narrow'=4] {'wide'}, use_global_device_ids=true, to_apply=%region_10.11 | all-reduce | flops 1024 | bytes 8192 | tf_op jit(solution)/shard_map/psum | solution.py:36
  467.8 41.3 %reduce-scatter.23.cloned.1.call-done = bf16[200,1600]{1,0:T(8,128)(2,1)} async-done(((bf16[1600,1600]{1,0:T(8,128)(2,1)}), bf16[200,1600]{1,0:T(8,128)(2,1)}) %reduce-scatter.23.cloned.1.call-update) | async-done | bytes 640016
  515.1 126.5 %all-reduce.8.cloned.1.call-done = (f32[3,1600]{1,0:T(4,128)}, f32[5,1600]{1,0:T(8,128)}, f32[6400]{0:T(1024)}) async-done(((f32[3,1600]{1,0:T(4,128)}, f32[5,1600]{1,0:T(8,128)}, f32[6400]{0:T(1024)}), (f32[3,1600]{1,0:T(4,128)}, f32[5,1600]{1,0:T(8,128)}, f32[6400]{0:T(1024)})) %all-reduce.8.cloned.1.call-update) | async-done | bytes 76816 | tf_op jit(solution)/shard_map/psum | solution.py:670
  658.0 9.0 %all-gather.22.cloned.1.call-done = bf16[400,1600]{1,0:T(8,128)(2,1)} async-done(((bf16[200,1600]{1,0:T(8,128)(2,1)}), bf16[400,1600]{1,0:T(8,128)(2,1)}) %all-gather.22.cloned.1.call-update) | async-done | bytes 1280016 | tf_op jit(solution)/shard_map/all_gather | solution.py:615
  670.1 47.5 %reduce-scatter.19.cloned.1.call-done = bf16[200,1200]{1,0:T(8,128)(2,1)} async-done(((bf16[1600,1200]{1,0:T(8,128)(2,1)}), bf16[200,1200]{1,0:T(8,128)(2,1)}) %reduce-scatter.19.cloned.1.call-update) | async-done | bytes 480016 | tf_op jit(solution)/shard_map/reduce_scatter | solution.py:639
  724.8 16.8 %reduce-scatter.21.cloned.1.call-done = bf16[400,200]{1,0:T(8,128)(2,1)} async-done(((bf16[1600,200]{1,0:T(8,128)(2,1)}), bf16[400,200]{1,0:T(8,128)(2,1)}) %reduce-scatter.21.cloned.1.call-update) | async-done | bytes 160016
  (182 shorter events, 131.7 us)
Async XLA Ops:
  7.2 33.9 %copy-start = (f32[400,1600]{1,0:T(8,128)S(1)}, f32[400,1600]{1,0:T(8,128)}, u32[]{:S(2)}) copy-start(f32[400,1600]{1,0:T(8,128)} %param.32) | copy-start | bytes 7680004
  7.2 83.1 %all-gather.10.cloned.1.call-start = ((), (), s32[]{:S(2)}) async-start(), calls=%async_computation.8 | async-start | bytes 4608000 | tf_op jit(solution)/shard_map/all_gather | solution.py:556
  15.2 153.6 %all-gather.12.cloned.1.call-start = ((), (), s32[]{:S(2)}) async-start(), calls=%async_computation.9 | async-start | bytes 5990400 | tf_op jit(solution)/shard_map/all_gather | solution.py:559
  41.0 163.5 %all-gather.14.cloned.1.call-start = ((), (), s32[]{:S(2)}) async-start(), calls=%async_computation.10 | async-start | bytes 5990400 | tf_op jit(solution)/shard_map/all_gather | solution.py:560
  42.0 179.6 %all-gather.16.cloned.1.call-start = ((), (), s32[]{:S(2)}) async-start(), calls=%async_computation.11 | async-start | bytes 5990400 | tf_op jit(solution)/shard_map/all_gather | solution.py:561
  44.4 216.2 %all-gather.18.cloned.1.call-start = ((), (), s32[]{:S(2)}) async-start(), calls=%async_computation.13 | async-start | bytes 2129920 | tf_op jit(solution)/shard_map/all_gather | solution.py:63
  44.4 45.8 %collective-permute-start = (s32[1,128]{1,0:T(1,128)S(1)}, s32[1,128]{1,0:T(1,128)S(1)}, u32[]{:S(2)}, u32[]{:S(2)}) collective-permute-start(s32[1,128]{1,0:T(1,128)S(1)} %copy-done.28), channel_id=1, source_target_pairs={{0,0},{4,1},{8,2},{12,3},{1,4},{5,5},{9,6},{13,7},{2,8},{6,9},{10,... | collective-permute-start | bytes 1544 | tf_op jit(solution)/shard_map/ppermute | solution.py:552
  76.8 256.4 %reduce-scatter.17.cloned.1.call-start = ((), (), s32[]{:S(2)}) async-start(), calls=%async_computation.12 | async-start | bytes 2129920 | tf_op jit(solution)/shard_map/reduce_scatter | solution.py:71
  174.5 30.1 %copy-start.27 = (f32[1600]{0:T(1024)S(1)}, f32[1600]{0:T(1024)}, u32[]{:S(2)}) copy-start(f32[1600]{0:T(1024)} %param.33) | copy-start | bytes 19204
  233.3 190.3 %reduce-scatter.25.cloned.1.call-start = ((), (), s32[]{:S(2)}) async-start(), calls=%async_computation.19 | async-start | bytes 5990400
  278.1 165.1 %reduce-scatter.27.cloned.1.call-start = ((), (), s32[]{:S(2)}) async-start(), calls=%async_computation.20 | async-start | bytes 5990400
  286.4 222.7 %reduce-scatter.23.cloned.1.call-start = ((), (), s32[]{:S(2)}) async-start(), calls=%async_computation.18 | async-start | bytes 5990400
  338.9 302.7 %all-reduce.8.cloned.1.call-start = ((), (), s32[]{:S(2)}) async-start(), calls=%async_computation.21 | async-start | bytes 217088 | tf_op jit(solution)/shard_map/psum | solution.py:670
  366.0 47.1 %copy-start.10 = (f32[400,512]{1,0:T(8,128)S(1)}, f32[400,512]{1,0:T(8,128)}, u32[]{:S(2)}) copy-start(f32[400,512]{1,0:T(8,128)} %x_ref.1) | copy-start | bytes 2457604
  366.0 47.2 %copy-start.20 = (f32[400]{0:T(512)S(1)}, f32[400]{0:T(512)}, u32[]{:S(2)}) copy-start(f32[400]{0:T(512)} %param.24) | copy-start | bytes 4804
  423.5 231.5 %all-gather.20.cloned.1.call-start = ((), (), s32[]{:S(2)}) async-start(), calls=%async_computation.14 | async-start | bytes 1996800 | tf_op jit(solution)/shard_map/all_gather | solution.py:615
  424.2 242.8 %all-gather.22.cloned.1.call-start = ((), (), s32[]{:S(2)}) async-start(), calls=%async_computation.15 | async-start | bytes 1996800 | tf_op jit(solution)/shard_map/all_gather | solution.py:615
  443.3 274.3 %reduce-scatter.19.cloned.1.call-start = ((), (), s32[]{:S(2)}) async-start(), calls=%async_computation.16 | async-start | bytes 4608000 | tf_op jit(solution)/shard_map/reduce_scatter | solution.py:639
  451.5 60.0 %all-to-all-start = ((f32[128,4,400]{0,2,1:T(8,128)}), f32[128,4,400]{0,2,1:T(8,128)S(1)}, u32[]{:S(2)}, u32[]{:S(2)}) async-start(f32[128,4,400]{0,2,1:T(8,128)} %bitcast.21), calls=%async_computation.1 | async-start | bytes 1638400 | tf_op jit(solution)/shard_map/all_to_all | solution.py:79
  455.0 286.6 %reduce-scatter.21.cloned.1.call-start = ((), (), s32[]{:S(2)}) async-start(), calls=%async_computation.17 | async-start | bytes 1024000
  467.8 179.6 %copy-start.23 = (f32[400]{0:T(512)S(1)}, f32[400]{0:T(512)}, u32[]{:S(2)}) copy-start(f32[400]{0:T(512)} %param.35) | copy-start | bytes 4804
  511.4 137.0 %copy-start.11 = (f32[512,400]{0,1:T(8,128)S(1)}, f32[512,400]{0,1:T(8,128)}, u32[]{:S(2)}) copy-start(f32[512,400]{0,1:T(8,128)} %get-tuple-element.175) | copy-start | bytes 2457604
  511.4 137.0 %all-to-all-start.1 = ((f32[128,4,400]{0,2,1:T(8,128)}), f32[128,4,400]{0,2,1:T(8,128)S(1)}, u32[]{:S(2)}, u32[]{:S(2)}) async-start(f32[128,4,400]{0,2,1:T(8,128)} %bitcast.26), calls=%async_computation.2 | async-start | bytes 1638400 | tf_op jit(solution)/shard_map/all_to_all | solution.py:79
  721.9 24.5 %copy-start.1 = (f32[400,1600]{1,0:T(8,128)S(1)}, f32[400,1600]{1,0:T(8,128)}, u32[]{:S(2)}) copy-start(f32[400,1600]{1,0:T(8,128)} %param.32) | copy-start | bytes 7680004
  (23 other events, 121.7 us)
Sparse Core Ops, SparseCore 0:
  15.3 54.3 all-gather.9
  72.1 54.1 all-gather.11
  128.8 49.1 all-gather.13
  180.3 41.3 all-gather.15
  223.1 37.4 all-gather.17
  263.3 36.4 reduce-scatter.16
  303.2 62.2 reduce-scatter.24
  369.0 74.2 reduce-scatter.26
  446.7 62.3 reduce-scatter.22
  516.1 125.4 all-reduce.7
  643.1 11.8 all-gather.19
  656.4 10.6 all-gather.21
  669.4 48.1 reduce-scatter.18
  719.8 21.7 reduce-scatter.20

commit v4 on v2

--- a/solution.py
+++ b/solution.py
@@ -1,8 +1,11 @@
+import functools
 import math
 
 import jax
 import jax.numpy as jnp
 from jax import lax
+from jax.experimental import pallas as pl
+from jax.experimental.pallas import tpu as pltpu
 from jax.sharding import PartitionSpec as P
 
 HEADS = 25
@@ -114,6 +117,887 @@
     value_grad = jnp.einsum("hij,ihd->jhd", probs_full.astype(BF), cot_heads, preferred_element_type=F32)
     stacked = jnp.stack([query_grad, key_grad, value_grad], axis=1)
     return stacked.reshape(heads_all.shape[0], 3, HEADS * HEAD)
+
+
+MESH = pl.DeviceIdType.MESH
+VMEM_LIMIT = 60 * 1024 * 1024
+def params(collective_id):
+    return pltpu.CompilerParams(
+        collective_id=collective_id, has_side_effects=True, vmem_limit_bytes=VMEM_LIMIT
+    )
+
+
+def in_vmem(count):
+    return [pl.BlockSpec(memory_space=pltpu.VMEM)] * count
+
+
+def shape_of(shape, dtype):
+    return jax.ShapeDtypeStruct(shape, dtype)
+
+
+def square_peers():
+    me = lax.axis_index("wide")
+    return me, me + 1 - 2 * lax.rem(me, 2), lax.rem(me + 2, 4), 3 - me
+
+
+def greet(peers, line=None):
+    barrier = pltpu.get_barrier_semaphore()
+    count = len(peers)
+    for axis, peer in peers:
+        pl.semaphore_signal(barrier, inc=1, device_id={axis: peer}, device_id_type=MESH)
+    if line is not None:
+        n, _, has_down, has_up = line
+        for has, peer in ((has_down, n - 1), (has_up, n + 1)):
+
+            @pl.when(has)
+            def _():
+                pl.semaphore_signal(barrier, inc=1, device_id={"narrow": peer}, device_id_type=MESH)
+
+        count = count + has_down.astype(jnp.int32) + has_up.astype(jnp.int32)
+    pl.semaphore_wait(barrier, count)
+
+
+def remote(src, dst, send_sem, recv_sem, axis, peer):
+    return pltpu.make_async_remote_copy(
+        src_ref=src,
+        dst_ref=dst,
+        send_sem=send_sem,
+        recv_sem=recv_sem,
+        device_id={axis: peer},
+        device_id_type=MESH,
+    )
+
+
+def line_sides():
+    n, count = lax.axis_index("narrow"), lax.axis_size("narrow")
+    return n, count, n > 0, n < count - 1
+
+
+def halves(cols):
+    first = cols // 256 * 128
+    return (0, first), (first, cols - first)
+
+
+class SquareGather:
+    def __init__(self, items, send_sem, recv_sem):
+        self.items, self.send_sem, self.recv_sem = items, send_sem, recv_sem
+        self.me, xp, yp, self.dg = square_peers()
+        self.ways = ((xp, yp), (yp, xp))
+        self.core = lax.axis_index("dp")
+
+    def place(self, i, chip):
+        return self.items[i][1](chip * 2 + self.core)
+
+    def copy(self, i, k):
+        first, second = self.ways[i % 2]
+        own = self.items[i][0]
+        src, dst, axis, peer = {
+            0: (own, self.me, "wide", first),
+            1: (own, self.me, "wide", second),
+            2: (own, self.me, "dp", 1 - self.core),
+            3: (None, first, "wide", second),
+            4: (None, first, "dp", 1 - self.core),
+            5: (None, second, "dp", 1 - self.core),
+            6: (None, self.dg, "dp", 1 - self.core),
+        }[k]
+        dst = self.place(i, dst)
+        return remote(dst if src is None else src, dst, self.send_sem.at[i, k], self.recv_sem.at[i, k], axis, peer)
+
+    def start(self):
+        for k in range(3):
+            for i in range(len(self.items)):
+                self.copy(i, k).start()
+        for i in range(len(self.items)):
+            self.place(i, self.me)[...] = self.items[i][0][...]
+
+    def relay(self, i):
+        self.copy(i, 0).wait_recv()
+        self.copy(i, 3).start()
+        self.copy(i, 4).start()
+        self.copy(i, 1).wait_recv()
+        self.copy(i, 5).start()
+
+    def finish(self):
+        for i in range(len(self.items)):
+            self.copy(i, 3).wait_recv()
+            self.copy(i, 6).start()
+        for i in range(len(self.items)):
+            for k in (2, 4, 5, 6):
+                self.copy(i, k).wait_recv()
+            for k in range(7):
+                self.copy(i, k).wait_send()
+
+
+class LineGather:
+    def __init__(self, own_ref, all_ref, send_sem, recv_sem, core_send=None, core_recv=None):
+        self.own_ref, self.all_ref, self.send_sem, self.recv_sem = own_ref, all_ref, send_sem, recv_sem
+        self.core_send, self.core_recv = core_send, core_recv
+        self.core = lax.axis_index("dp")
+        self.n, self.count, self.has_down, self.has_up = line_sides()
+
+    def place(self, block):
+        return self.all_ref.at[block] if self.core_send is None else self.all_ref.at[block, self.core]
+
+    def copy(self, block, way, src=None):
+        place = self.place(block)
+        return remote(
+            place if src is None else src,
+            place,
+            self.send_sem.at[way, block],
+            self.recv_sem.at[block],
+            "narrow",
+            self.n + 1 - 2 * way,
+        )
+
+    def share(self, block, src=None):
+        place = self.place(block)
+        return remote(
+            place if src is None else src, place, self.core_send.at[block], self.core_recv.at[block], "dp", 1 - self.core
+        )
+
+    def start(self):
+        @pl.when(self.has_up)
+        def _():
+            self.copy(self.n, 0, self.own_ref).start()
+
+        @pl.when(self.has_down)
+        def _():
+            self.copy(self.n, 1, self.own_ref).start()
+
+        if self.core_send is not None:
+            self.share(self.n, self.own_ref).start()
+        self.place(self.n)[...] = self.own_ref[...]
+
+    def step(self, step):
+        below, above = self.n - step, self.n + step
+
+        @pl.when(below >= 0)
+        def _():
+            self.copy(below, 0).wait_recv()
+
+            @pl.when(self.has_up)
+            def _():
+                self.copy(below, 0).start()
+
+            if self.core_send is not None:
+                self.share(below).start()
+
+        @pl.when(above < self.count)
+        def _():
+            self.copy(above, 1).wait_recv()
+
+            @pl.when(self.has_down)
+            def _():
+                self.copy(above, 1).start()
+
+            if self.core_send is not None:
+                self.share(above).start()
+
+    def finish(self):
+        for step in range(self.count):
+            below, above = self.n - step, self.n + step
+
+            @pl.when((below >= 0) & self.has_up)
+            def _():
+                self.copy(below, 0).wait_send()
+
+            @pl.when((above < self.count) & self.has_down)
+            def _():
+                self.copy(above, 1).wait_send()
+
+        if self.core_send is not None:
+            for block in range(self.count):
+                self.share(block).wait()
+
+
+def front_kernel(
+    x_ref, dy_ref, gain_ref, shift_ref, vec_ref, bias_ref, wo_ref, wq_ref,
+    norm_ref, stat_ref, xt_ref, dyt_ref, vecs_ref, biases_ref, wos_ref, wqs_ref,
+    sums, all_sums, wo_parts, wo_row,
+    send_sem, recv_sem, near_send, near_recv, line_send, line_recv, core_send, core_recv, square_send, square_recv,
+):
+    feats, tokens = x_ref.shape
+    wide = 4
+    block = tokens // wide
+    me, xp, yp, dg = square_peers()
+    peers = (xp, yp, dg)
+    n, count = lax.axis_index("narrow"), lax.axis_size("narrow")
+    others = [lax.rem(n + k, count) for k in range(1, count)]
+    greet(
+        [("wide", peer) for peer in peers]
+        + [("narrow", peer) for peer in others]
+        + [("dp", 1 - lax.axis_index("dp"))]
+    )
+    copies = []
+
+    def send(src, dst, sems, k, j, axis, peer):
+        copy = remote(src, dst, sems[0].at[k, j], sems[1].at[k, j], axis, peer)
+        copy.start()
+        copies.append(copy)
+
+    near, across = (near_send, near_recv), (send_sem, recv_sem)
+    for j, peer in enumerate(others):
+        send(wo_ref, wo_parts.at[n], near, 0, j, "narrow", peer)
+        send(bias_ref, biases_ref.at[n], near, 1, j, "narrow", peer)
+    line = LineGather(wq_ref, wqs_ref, line_send, line_recv, core_send, core_recv)
+    line.start()
+    wo_parts[n] = wo_ref[...]
+    biases_ref[n] = bias_ref[...]
+    x = x_ref[...]
+    sums[...] = jnp.zeros_like(sums)
+    stat_ref[...] = jnp.zeros_like(stat_ref)
+    sums[0:1, :] = jnp.sum(x, axis=0, keepdims=True)
+    sums[1:2, :] = jnp.sum(x * x, axis=0, keepdims=True)
+    for j, peer in enumerate(peers):
+        send(sums, all_sums.at[me], across, 0, j, "wide", peer)
+        send(vec_ref, vecs_ref.at[me], across, 1, j, "wide", peer)
+    vecs_ref[me] = vec_ref[...]
+    mine = pl.ds(me * feats, feats)
+    for k, (src, dst) in enumerate(((x_ref, xt_ref), (dy_ref, dyt_ref))):
+        for j, peer in enumerate(peers):
+            theirs = pl.ds(pl.multiple_of(peer * block, 128), block)
+            send(src.at[:, theirs], dst.at[mine, :], across, 2 + k, j, "wide", peer)
+        dst[mine, :] = src[:, pl.ds(pl.multiple_of(me * block, 128), block)]
+    for copy in copies[: 2 * (count - 1)]:
+        copy.wait()
+    part = wo_ref.shape[1]
+    for k in range(count):
+        wo_row[:, k * part : (k + 1) * part] = wo_parts[k]
+    items = [
+        (wo_row.at[:, pl.ds(*span)], lambda index, span=span: wos_ref.at[index, :, pl.ds(*span)])
+        for span in halves(wo_row.shape[1])
+    ]
+    gather = SquareGather(items, square_send, square_recv)
+    gather.start()
+    rest = copies[2 * (count - 1) :]
+    for copy in rest[:6]:
+        copy.wait()
+    total = sums[...]
+    for peer in peers:
+        total = total + all_sums[peer]
+    width = feats * wide
+    mean = total[0:1, :] / width
+    inv = lax.rsqrt(total[1:2, :] / width - mean * mean + EPS)
+    stat_ref[0:1, :] = mean
+    stat_ref[1:2, :] = inv
+    norm_ref[...] = ((x_ref[...] - mean) * inv * gain_ref[...] + shift_ref[...]).astype(BF)
+    line.step(1)
+    for copy in rest[6:]:
+        copy.wait()
+    line.step(2)
+    gather.relay(0)
+    gather.relay(1)
+    for step in range(3, count):
+        line.step(step)
+    gather.finish()
+    line.finish()
+
+
+def front_stage(x, dy, gain, shift, vec, bias, wo, wq):
+    feats, tokens = x.shape
+    count = lax.axis_size("narrow")
+    width = wo.shape[1] * count
+    return pl.pallas_call(
+        front_kernel,
+        out_shape=(
+            shape_of((feats, tokens), BF),
+            shape_of((8, tokens), F32),
+            shape_of((4 * feats, tokens // 4), F32),
+            shape_of((4 * feats, tokens // 4), F32),
+            shape_of((4,) + vec.shape, F32),
+            shape_of((count,) + bias.shape, F32),
+            shape_of((8, wo.shape[0], width), BF),
+            shape_of((count, 2) + wq.shape, BF),
+        ),
+        in_specs=in_vmem(8),
+        out_specs=tuple(in_vmem(8)),
+        scratch_shapes=[
+            pltpu.VMEM((8, tokens), F32),
+            pltpu.VMEM((4, 8, tokens), F32),
+            pltpu.VMEM((count,) + wo.shape, BF),
+            pltpu.VMEM((wo.shape[0], width), BF),
+            pltpu.SemaphoreType.DMA((4, 3)),
+            pltpu.SemaphoreType.DMA((4, 3)),
+            pltpu.SemaphoreType.DMA((2, count - 1)),
+            pltpu.SemaphoreType.DMA((2, count - 1)),
+            pltpu.SemaphoreType.DMA((2, count)),
+            pltpu.SemaphoreType.DMA((count,)),
+            pltpu.SemaphoreType.DMA((count,)),
+            pltpu.SemaphoreType.DMA((count,)),
+            pltpu.SemaphoreType.DMA((2, 7)),
+            pltpu.SemaphoreType.DMA((2, 7)),
+        ],
+        compiler_params=params(1),
+        cost_estimate=pl.CostEstimate(flops=10**10, bytes_accessed=60 * 10**6, transcendentals=0),
+        name="front_stage",
+    )(x, dy, gain, shift, vec, bias, wo, wq)
+
+
+def qkv_kernel(
+    norm_ref, w_ref, bias_ref, dy_ref, out_ref, dys_ref,
+    acc, first_out, first_in, second_out, second_in, send_sem, recv_sem, line_send, line_recv,
+):
+    pieces, feats, cols = w_ref.shape
+    tokens = norm_ref.shape[0]
+    block = tokens // 4
+    me, xp, yp, dg = square_peers()
+    greet((("wide", xp), ("wide", yp)), line_sides())
+    line = LineGather(dy_ref, dys_ref, line_send, line_recv)
+    line.start()
+
+    def rows(index):
+        return pl.ds(pl.multiple_of(index * block, block), block)
+
+    def ways(p):
+        turn = lax.rem(p, 2)
+        return xp * (1 - turn) + yp * turn, yp * (1 - turn) + xp * turn
+
+    def first_copy(p):
+        return remote(first_out.at[p], first_in.at[p], send_sem.at[0, p], recv_sem.at[0, p], "wide", ways(p)[0])
+
+    def second_copy(p):
+        return remote(second_out.at[p], second_in.at[p], send_sem.at[1, p], recv_sem.at[1, p], "wide", ways(p)[1])
+
+    def issue(p, carry):
+        acc[p] = dot(norm_ref[...], w_ref[p], 1, 0)
+        first_out[p, 0] = acc[p, rows(ways(p)[0]), :].astype(BF)
+        first_out[p, 1] = acc[p, rows(dg), :].astype(BF)
+        first_copy(p).start()
+        return carry
+
+    lax.fori_loop(0, pieces, issue, 0)
+    line.step(1)
+
+    def middle(p, carry):
+        first_copy(p).wait()
+        second_out[p] = (acc[p, rows(ways(p)[1]), :] + first_in[p, 1].astype(F32)).astype(BF)
+        second_copy(p).start()
+        return carry
+
+    lax.fori_loop(0, pieces // 2, middle, 0)
+    line.step(2)
+    lax.fori_loop(pieces // 2, pieces, middle, 0)
+    for step in range(3, line.count):
+        line.step(step)
+
+    def last(p, carry):
+        second_copy(p).wait()
+        total = acc[p, rows(me), :] + first_in[p, 0].astype(F32) + second_in[p].astype(F32)
+        out_ref[p] = (total + bias_ref[p]).astype(BF)
+        return carry
+
+    lax.fori_loop(0, pieces, last, 0)
+    line.finish()
+
+
+def qkv_stage(norm, w, bias, dy):
+    count = lax.axis_size("narrow")
+    pieces, feats, cols = w.shape
+    tokens = norm.shape[0]
+    block = tokens // 4
+    return pl.pallas_call(
+        qkv_kernel,
+        out_shape=(shape_of((pieces, block, cols), BF), shape_of((count,) + dy.shape, BF)),
+        in_specs=in_vmem(4),
+        out_specs=tuple(in_vmem(2)),
+        scratch_shapes=[
+            pltpu.VMEM((pieces, tokens, cols), F32),
+            pltpu.VMEM((pieces, 2, block, cols), BF),
+            pltpu.VMEM((pieces, 2, block, cols), BF),
+            pltpu.VMEM((pieces, block, cols), BF),
+            pltpu.VMEM((pieces, block, cols), BF),
+            pltpu.SemaphoreType.DMA((2, pieces)),
+            pltpu.SemaphoreType.DMA((2, pieces)),
+            pltpu.SemaphoreType.DMA((2, count)),
+            pltpu.SemaphoreType.DMA((count,)),
+        ],
+        compiler_params=params(2),
+        cost_estimate=pl.CostEstimate(flops=3 * 10**10, bytes_accessed=10**8, transcendentals=0),
+        name="qkv_stage",
+    )(norm, w, bias, dy)
+
+
+def line_gather_kernel(own_ref, all_ref, send_sem, recv_sem):
+    greet((), line_sides())
+    line = LineGather(own_ref, all_ref, send_sem, recv_sem)
+    line.start()
+    for step in range(1, line.count):
+        line.step(step)
+    line.finish()
+
+
+def line_gather(own):
+    count = lax.axis_size("narrow")
+    return pl.pallas_call(
+        line_gather_kernel,
+        out_shape=shape_of((count,) + own.shape, own.dtype),
+        in_specs=in_vmem(1),
+        out_specs=pl.BlockSpec(memory_space=pltpu.VMEM),
+        scratch_shapes=[pltpu.SemaphoreType.DMA((2, count)), pltpu.SemaphoreType.DMA((count,))],
+        compiler_params=params(4),
+        cost_estimate=pl.CostEstimate(flops=2 * 10**10, bytes_accessed=7 * 10**7, transcendentals=0),
+        name="line_gather",
+    )(own)
+
+
+def pair_kernel(count, own_ref, *refs):
+    weight_refs, all_ref, whole_refs = refs[:count], refs[count], refs[count + 1 : 2 * count + 1]
+    send_sem, recv_sem, line_send, line_recv = refs[2 * count + 1 :]
+    me, xp, yp, dg = square_peers()
+    greet((("wide", xp), ("wide", yp), ("dp", 1 - lax.axis_index("dp"))), line_sides())
+    line = LineGather(own_ref, all_ref, line_send, line_recv)
+    items = [
+        (weight.at[:, pl.ds(*span)], lambda index, span=span, whole=whole: whole.at[index, :, pl.ds(*span)])
+        for weight, whole in zip(weight_refs, whole_refs)
+        for span in halves(weight.shape[1])
+    ]
+    gather = SquareGather(items, send_sem, recv_sem)
+    line.start()
+    gather.start()
+    line.step(1)
+    gather.relay(0)
+    gather.relay(1)
+    line.step(2)
+    for i in range(2, len(items)):
+        gather.relay(i)
+    for step in range(3, line.count):
+        line.step(step)
+    gather.finish()
+    line.finish()
+
+
+def pair_stage(own, *weights):
+    count = lax.axis_size("narrow")
+    items = 2 * len(weights)
+    return pl.pallas_call(
+        functools.partial(pair_kernel, len(weights)),
+        out_shape=(
+            shape_of((count,) + own.shape, own.dtype),
+            *(shape_of((8,) + weight.shape, weight.dtype) for weight in weights),
+        ),
+        in_specs=in_vmem(1 + len(weights)),
+        out_specs=tuple(in_vmem(1 + len(weights))),
+        scratch_shapes=[
+            pltpu.SemaphoreType.DMA((items, 7)),
+            pltpu.SemaphoreType.DMA((items, 7)),
+            pltpu.SemaphoreType.DMA((2, count)),
+            pltpu.SemaphoreType.DMA((count,)),
+        ],
+        compiler_params=params(7),
+        cost_estimate=pl.CostEstimate(flops=2 * 10**10, bytes_accessed=7 * 10**7, transcendentals=0),
+        name="pair_stage",
+    )(own, *weights)
+
+
+class SquareSum:
+    def __init__(self, part_ref, bufs, sems):
+        self.part_ref = part_ref
+        self.core_in, self.half, self.first_out, self.first_in, self.second_out, self.second_in = bufs
+        self.core_send, self.core_recv, self.send_sem, self.recv_sem = sems
+        self.me, xp, yp, self.dg = square_peers()
+        self.ways = ((xp, yp), (yp, xp))
+        self.core = lax.axis_index("dp")
+        self.spans = halves(part_ref.shape[2])
+
+    def core_copy(self, chip):
+        return remote(
+            self.part_ref.at[chip * 2 + 1 - self.core],
+            self.core_in.at[chip],
+            self.core_send.at[chip],
+            self.core_recv.at[chip],
+            "dp",
+            1 - self.core,
+        )
+
+    def first_copy(self, i, k):
+        cols = pl.ds(*self.spans[i])
+        return remote(
+            self.first_out.at[k, :, cols],
+            self.first_in.at[k, :, cols],
+            self.send_sem.at[i, k],
+            self.recv_sem.at[i, k],
+            "wide",
+            self.ways[i][0],
+        )
+
+    def second_copy(self, i):
+        cols = pl.ds(*self.spans[i])
+        return remote(
+            self.second_out.at[:, cols],
+            self.second_in.at[:, cols],
+            self.send_sem.at[i, 2],
+            self.recv_sem.at[i, 2],
+            "wide",
+            self.ways[i][1],
+        )
+
+    def start(self):
+        for chip in range(4):
+            self.core_copy(chip).start()
+
+    def issue(self):
+        for chip in range(4):
+            self.core_copy(chip).wait()
+            total = self.part_ref[chip * 2 + self.core].astype(F32) + self.core_in[chip].astype(F32)
+            self.half[chip] = total.astype(BF)
+        for i, (at, size) in enumerate(self.spans):
+            for k, chip in enumerate((self.ways[i][0], self.dg)):
+                self.first_out[k, :, at : at + size] = self.half[chip, :, at : at + size]
+                self.first_copy(i, k).start()
+
+    def middle(self):
+        for i, (at, size) in enumerate(self.spans):
+            self.first_copy(i, 1).wait()
+            total = self.half[self.ways[i][1], :, at : at + size].astype(F32)
+            total = total + self.first_in[1, :, at : at + size].astype(F32)
+            self.second_out[:, at : at + size] = total.astype(BF)
+            self.second_copy(i).start()
+
+    def finish(self, out_ref):
+        for i, (at, size) in enumerate(self.spans):
+            self.first_copy(i, 0).wait()
+            self.second_copy(i).wait()
+            total = self.half[self.me, :, at : at + size].astype(F32)
+            total = total + self.first_in[0, :, at : at + size].astype(F32)
+            out_ref[:, at : at + size] = total + self.second_in[:, at : at + size].astype(F32)
+
+
+def square_sum_scratch(rows, cols):
+    return [
+        pltpu.VMEM((4, rows, cols), BF),
+        pltpu.VMEM((4, rows, cols), BF),
+        pltpu.VMEM((2, rows, cols), BF),
+        pltpu.VMEM((2, rows, cols), BF),
+        pltpu.VMEM((rows, cols), BF),
+        pltpu.VMEM((rows, cols), BF),
+        pltpu.SemaphoreType.DMA((4,)),
+        pltpu.SemaphoreType.DMA((4,)),
+        pltpu.SemaphoreType.DMA((2, 3)),
+        pltpu.SemaphoreType.DMA((2, 3)),
+    ]
+
+
+def back_kernel(
+    cot_ref, norm_ref, w_ref, wo_ref,
+    grad_ref, wq_out, wo_out,
+    cots, full, other, core_in, leave, arrive, wo_row, wo_leave, wo_arrive,
+    send_sem, recv_sem, core_send, core_recv, line_send, line_recv, near_send, near_recv, share_send, share_recv,
+    *square,
+):
+    pieces, block, cols = cot_ref.shape
+    me, xp, yp, dg = square_peers()
+    n, count, has_down, has_up = line_sides()
+    core = lax.axis_index("dp")
+    others = [lax.rem(n + k, count) for k in range(1, count)]
+    greet(
+        [("wide", xp), ("wide", yp), ("dp", 1 - core)] + [("narrow", peer) for peer in others]
+    )
+    spans = halves(cols)
+    ways = ((xp, yp), (yp, xp))
+    rows_half = core_in.shape[1]
+
+    def order(i):
+        odd = lax.rem(i, 2)
+        return (1 - odd) * (i // 2) + odd * (pieces - 1 - i // 2)
+
+    def rows(index):
+        return pl.ds(pl.multiple_of(index * block, block), block)
+
+    def spread(i, h, k):
+        p = order(i)
+        span = pl.ds(*spans[h])
+        first, second = ways[h]
+        place = cots.at[p, rows(first if k == 2 else me), span]
+        src = place if k == 2 else cot_ref.at[p, :, span]
+        return remote(
+            src, place, send_sem.at[h, k, p], recv_sem.at[h, k, p], "wide", first if k == 0 else second
+        )
+
+    def own(i):
+        for h in range(2):
+            for k in range(2):
+                spread(i, h, k).start()
+        p = order(i)
+        cots[p, rows(me), :] = cot_ref[p]
+
+    def core_copy(p):
+        return remote(other.at[p], core_in.at[p], core_send.at[p], core_recv.at[p], "dp", 1 - core)
+
+    def line_copy(way, p):
+        return remote(
+            leave.at[p], arrive.at[way, p], line_send.at[p], line_recv.at[way, p], "narrow", n + 1 - 2 * way
+        )
+
+    own_rows = pl.ds(pl.multiple_of(core * rows_half, 8), rows_half)
+    sibling_rows = pl.ds(pl.multiple_of((1 - core) * rows_half, 8), rows_half)
+    square_sum = SquareSum(wo_ref, square[:6], square[6:])
+    own(0)
+    own(1)
+    square_sum.start()
+    grad_ref[...] = jnp.zeros_like(grad_ref)
+
+    def turn(p):
+        core_copy(p).wait()
+        mine = full[p, own_rows, :] + core_in[p].astype(F32)
+        full[p, own_rows, :] = mine
+
+        def pass_on(way, sends, joins):
+            @pl.when(sends & joins)
+            def _():
+                line_copy(way, p).wait_recv()
+                leave[p] = (full[p, own_rows, :] + arrive[way, p].astype(F32)).astype(BF)
+                line_copy(way, p).start()
+
+            @pl.when(sends & jnp.logical_not(joins))
+            def _():
+                leave[p] = full[p, own_rows, :].astype(BF)
+                line_copy(way, p).start()
+
+        pass_on(0, n < p, has_down)
+        pass_on(1, n > p, has_up)
+
+    def body(i, carry):
+        @pl.when(i < pieces)
+        def _():
+            for h in range(2):
+                spread(i, h, 0).wait_recv()
+                spread(i, h, 2).start()
+
+        @pl.when(i + 2 < pieces)
+        def _():
+            own(i + 2)
+
+        @pl.when((i >= 1) & (i <= pieces))
+        def _():
+            p = order(i - 1)
+            for h in range(2):
+                spread(i - 1, h, 1).wait_recv()
+                spread(i - 1, h, 2).wait_recv()
+            full[p] = dot(norm_ref[...], cots[p], 1, 0)
+            other[p] = full[p, sibling_rows, :].astype(BF)
+            core_copy(p).start()
+            grad_ref[...] += dot(w_ref[p], cots[p], 1, 1)
+
+        @pl.when(i >= 2)
+        def _():
+            turn(order(i - 2))
+
+        @pl.when(i == pieces - 1)
+        def _():
+            square_sum.issue()
+
+        return carry
+
+    lax.fori_loop(0, pieces + 2, body, 0)
+    square_sum.middle()
+    square_sum.finish(wo_row)
+    part = wo_leave.shape[2]
+    for k in range(count):
+        wo_leave[k] = wo_row[:, k * part : (k + 1) * part].astype(BF)
+    near = []
+    for j, peer in enumerate(others):
+        copy = remote(wo_leave.at[peer], wo_arrive.at[n], near_send.at[j], near_recv.at[j], "narrow", peer)
+        copy.start()
+        near.append(copy)
+    total = full[n, own_rows, :]
+    for way, joins in ((0, has_down), (1, has_up)):
+
+        @pl.when(joins)
+        def _():
+            line_copy(way, n).wait_recv()
+            full[n, own_rows, :] += arrive[way, n].astype(F32)
+
+    wq_out[core] = full[n, own_rows, :]
+    share_wq = remote(wq_out.at[core], wq_out.at[core], share_send.at[0], share_recv.at[0], "dp", 1 - core)
+    share_wq.start()
+    for copy in near:
+        copy.wait()
+    wo_total = wo_leave[n].astype(F32)
+    for peer in others:
+        wo_total = wo_total + wo_arrive[peer].astype(F32)
+    wo_out[core] = wo_total
+    share_wo = remote(wo_out.at[core], wo_out.at[core], share_send.at[1], share_recv.at[1], "dp", 1 - core)
+    share_wo.start()
+
+    def drain(i, carry):
+        for h in range(2):
+            for k in range(3):
+                spread(i, h, k).wait_send()
+        p = order(i)
+
+        @pl.when(n < p)
+        def _():
+            line_copy(0, p).wait_send()
+
+        @pl.when(n > p)
+        def _():
+            line_copy(1, p).wait_send()
+
+        return carry
+
+    lax.fori_loop(0, pieces, drain, 0)
+    share_wq.wait()
+    share_wo.wait()
+
+
+def back_stage(cot, norm, w, wo):
+    pieces, block, cols = cot.shape
+    count = lax.axis_size("narrow")
+    feats, tokens = norm.shape
+    rows, wo_cols = wo.shape[1:]
+    half = feats // 2
+    part = wo_cols // count
+    return pl.pallas_call(
+        back_kernel,
+        out_shape=(
+            shape_of((feats, tokens), F32),
+            shape_of((2, half, cols), F32),
+            shape_of((2, rows, part), F32),
+        ),
+        in_specs=in_vmem(4),
+        out_specs=tuple(in_vmem(3)),
+        scratch_shapes=[
+            pltpu.VMEM((pieces, tokens, cols), BF),
+            pltpu.VMEM((pieces, feats, cols), F32),
+            pltpu.VMEM((pieces, half, cols), BF),
+            pltpu.VMEM((pieces, half, cols), BF),
+            pltpu.VMEM((pieces, half, cols), BF),
+            pltpu.VMEM((2, pieces, half, cols), BF),
+            pltpu.VMEM((rows, wo_cols), F32),
+            pltpu.VMEM((count, rows, part), BF),
+            pltpu.VMEM((count, rows, part), BF),
+            pltpu.SemaphoreType.DMA((2, 3, pieces)),
+            pltpu.SemaphoreType.DMA((2, 3, pieces)),
+            pltpu.SemaphoreType.DMA((pieces,)),
+            pltpu.SemaphoreType.DMA((pieces,)),
+            pltpu.SemaphoreType.DMA((pieces,)),
+            pltpu.SemaphoreType.DMA((2, pieces)),
+            pltpu.SemaphoreType.DMA((count - 1,)),
+            pltpu.SemaphoreType.DMA((count - 1,)),
+            pltpu.SemaphoreType.DMA((2,)),
+            pltpu.SemaphoreType.DMA((2,)),
+        ]
+        + square_sum_scratch(rows, wo_cols),
+        compiler_params=params(3),
+        cost_estimate=pl.CostEstimate(flops=4 * 10**10, bytes_accessed=10**8, transcendentals=0),
+        name="back_stage",
+    )(cot, norm, w, wo)
+
+
+TOKEN_TERMS = 5
+
+
+def final_kernel(
+    x_ref, stat_ref, grad_ref, resid_ref, gain_ref, sums_ref, wide_ref, feat_ref, wf_ref, wp_ref,
+    out_ref, wide_out, feat_out, wf_out, wp_out,
+    all_sums, wide_in, wide_mid, line_wide, line_feat, wide_two, feat_two, last_wide, last_feat,
+    wf_in, wp_in, send_sem, recv_sem, line_send, line_recv, core_send, core_recv,
+):
+    me, xp, yp, dg = square_peers()
+    n, count = lax.axis_index("narrow"), lax.axis_size("narrow")
+    core = lax.axis_index("dp")
+    peers = (xp, yp, dg)
+    others = [lax.rem(n + k, count) for k in range(1, count)]
+    greet(
+        [("wide", peer) for peer in peers] + [("narrow", peer) for peer in others] + [("dp", 1 - core)]
+    )
+    shares = []
+    for k, (src, dst) in enumerate(((wf_ref, wf_in), (wp_ref, wp_in))):
+        copy = remote(src, dst, core_send.at[2 + k], core_recv.at[2 + k], "dp", 1 - core)
+        copy.start()
+        shares.append(copy)
+    square = []
+    for j, peer in enumerate(peers):
+        for k, (src, dst) in enumerate(((sums_ref, all_sums), (wide_ref, wide_in))):
+            copy = remote(src, dst.at[me], send_sem.at[k, j], recv_sem.at[k, j], "wide", peer)
+            copy.start()
+            square.append(copy)
+    for copy in square:
+        copy.wait()
+    total = wide_ref[...]
+    for peer in peers:
+        total = total + wide_in[peer]
+    wide_mid[...] = total
+    line = []
+    for j, peer in enumerate(others):
+        for k, (src, dst) in enumerate(((wide_mid, line_wide), (feat_ref, line_feat))):
+            copy = remote(src, dst.at[n], line_send.at[k, j], line_recv.at[k, j], "narrow", peer)
+            copy.start()
+            line.append(copy)
+    sums = sums_ref[...]
+    for peer in peers:
+        sums = sums + all_sums[peer]
+    width = x_ref.shape[0] * 4
+    inv = stat_ref[1:2, :]
+    normed = (x_ref[...] - stat_ref[0:1, :]) * inv
+    scaled = grad_ref[...] * gain_ref[...]
+    out_ref[...] = resid_ref[...] + inv * (scaled - sums[0:1, :] / width - normed * (sums[1:2, :] / width))
+    wf_out[core] = wf_ref[...].astype(F32)
+    wp_out[core] = wp_ref[...].astype(F32)
+    for copy in shares:
+        copy.wait()
+    wf_out[1 - core] = wf_in[...].astype(F32)
+    wp_out[1 - core] = wp_in[...].astype(F32)
+    for copy in line:
+        copy.wait()
+    feat_total = feat_ref[...]
+    shared = lax.broadcasted_iota(jnp.int32, total.shape, 0) < TOKEN_TERMS
+    for peer in others:
+        total = total + jnp.where(shared, line_wide[peer], 0.0)
+        feat_total = feat_total + line_feat[peer]
+    wide_two[...] = total
+    feat_two[...] = feat_total
+    cores = []
+    for k, (src, dst) in enumerate(((wide_two, last_wide), (feat_two, last_feat))):
+        copy = remote(src, dst, core_send.at[k], core_recv.at[k], "dp", 1 - core)
+        copy.start()
+        cores.append(copy)
+    for copy in cores:
+        copy.wait()
+    wide_out[...] = total + last_wide[...]
+    feat_out[...] = feat_total + last_feat[...]
+
+
+def final_stage(x, stats, grad, resid, gain, sums, wide_terms, feat_terms, wf, wp):
+    count = lax.axis_size("narrow")
+    return pl.pallas_call(
+        final_kernel,
+        out_shape=(
+            shape_of(x.shape, F32),
+            shape_of(wide_terms.shape, F32),
+            shape_of(feat_terms.shape, F32),
+            shape_of((2,) + wf.shape, F32),
+            shape_of((2,) + wp.shape, F32),
+        ),
+        in_specs=in_vmem(10),
+        out_specs=tuple(in_vmem(5)),
+        scratch_shapes=[
+            pltpu.VMEM((4,) + sums.shape, F32),
+            pltpu.VMEM((4,) + wide_terms.shape, F32),
+            pltpu.VMEM(wide_terms.shape, F32),
+            pltpu.VMEM((count,) + wide_terms.shape, F32),
+            pltpu.VMEM((count,) + feat_terms.shape, F32),
+            pltpu.VMEM(wide_terms.shape, F32),
+            pltpu.VMEM(feat_terms.shape, F32),
+            pltpu.VMEM(wide_terms.shape, F32),
+            pltpu.VMEM(feat_terms.shape, F32),
+            pltpu.VMEM(wf.shape, BF),
+            pltpu.VMEM(wp.shape, BF),
+            pltpu.SemaphoreType.DMA((2, 3)),
+            pltpu.SemaphoreType.DMA((2, 3)),
+            pltpu.SemaphoreType.DMA((2, count - 1)),
+            pltpu.SemaphoreType.DMA((2, count - 1)),
+            pltpu.SemaphoreType.DMA((4,)),
+            pltpu.SemaphoreType.DMA((4,)),
+        ],
+        compiler_params=params(8),
+        cost_estimate=pl.CostEstimate(flops=10**9, bytes_accessed=2 * 10**7, transcendentals=0),
+        name="final_stage",
+    )(x, stats, grad, resid, gain, sums, wide_terms, feat_terms, wf, wp)
+
+
+def as_rows(rows):
+    return jnp.concatenate([jnp.stack(rows), jnp.zeros((8 - len(rows), rows[0].shape[0]), F32)])
 
 
 def own_half(values, axis):
@@ -152,31 +1036,50 @@
     starts = lax.ppermute(seq_start, ("wide", "narrow"), perm)[0]
     allowed = block_mask(starts)
 
-    wq_mine = own_half(w_qkv.astype(BF).reshape(feats, 3 * part), 0)
-    wq_all = lax.all_gather(wq_mine, ("narrow", "dp"), axis=0, tiled=True)
-    wq_all = wq_all.reshape(narrow, feats, 3 * part)
-    wo_mine = lax.all_gather(own_half(w_out.astype(BF), 0), "narrow", axis=1, tiled=True)
-    wo_all = lax.all_gather(wo_mine, ("wide", "dp"), axis=0, tiled=True)
-    wf_all = lax.all_gather(own_half(w_fc.astype(BF), 0), ("wide", "dp"), axis=0, tiled=True)
-    wp_all = lax.all_gather(own_half(w_proj.astype(BF), 0), ("wide", "dp"), axis=0, tiled=True)
-    b_out_full, gain_two_full, shift_two_full = lax.all_gather(
-        jnp.stack([b_out, ln2_gain, ln2_shift]), "wide", axis=1, tiled=True
-    )
-    bias_qv = lax.all_gather(b_qv, "narrow", axis=0).reshape(narrow, 1, 2, part)
-    bias_three = jnp.concatenate(
-        [bias_qv[:, :, 0], jnp.zeros((narrow, 1, part), F32), bias_qv[:, :, 1]], axis=2
-    )
+    wq_half = own_half(w_qkv, 0).astype(BF).reshape(-1, 3 * part)
+    wo_half, wf_half, wp_half = (own_half(w, 0).astype(BF) for w in (w_out, w_fc, w_proj))
+
+    def three(biases):
+        zeros = jnp.zeros((narrow, 1, part), F32)
+        return jnp.concatenate([biases[:, None, 0], zeros, biases[:, None, 1]], axis=2)
 
     rows_input = block_input.T
     rows_cot = block_cotangent.T
-    x_tok = to_tokens(rows_input)
-    dy_tok = to_tokens(rows_cot)
-    cot_all = gather_narrow(dy_tok.astype(BF))
-
-    normed_one, inv_one, norm_one = norm_forward(rows_input, ln1_gain, ln1_shift)
-    qkv_part = jnp.einsum("tk,nkc->tnc", norm_one, wq_all, preferred_element_type=F32)
-    qkv_rows = sum_tokens(qkv_part.transpose(0, 1, 2)).transpose(1, 0, 2)
-    qkv_rows = (qkv_rows + bias_three).astype(BF)
+    square = wide == 4 and cores == 2
+    if square:
+        norm_t, stats, x_tok, dy_tok, vecs, biases, wo_all, wq_all = front_stage(
+            block_input,
+            block_cotangent,
+            ln1_gain[:, None],
+            ln1_shift[:, None],
+            as_rows([b_out, ln2_gain, ln2_shift]),
+            as_rows([b_qv[0], b_qv[1]]),
+            wo_half,
+            wq_half,
+        )
+        x_tok, dy_tok = x_tok.T, dy_tok.T
+        wo_all = wo_all.reshape(width, width)
+        wq_all = wq_all.reshape(narrow, feats, 3 * part)
+        b_out_full, gain_two_full, shift_two_full = (vecs[:, i].reshape(width) for i in range(3))
+        qkv_rows, cot_all = qkv_stage(norm_t.T, wq_all, three(biases), dy_tok.astype(BF))
+        cot_all = cot_all.reshape(-1, width)
+    else:
+        wq_all = lax.all_gather(wq_half, ("narrow", "dp"), axis=0, tiled=True).reshape(narrow, feats, 3 * part)
+        wo_mine = lax.all_gather(wo_half, "narrow", axis=1, tiled=True)
+        wo_all = lax.all_gather(wo_mine, ("wide", "dp"), axis=0, tiled=True)
+        wf_all = lax.all_gather(wf_half, ("wide", "dp"), axis=0, tiled=True)
+        wp_all = lax.all_gather(wp_half, ("wide", "dp"), axis=0, tiled=True)
+        bias_three = three(lax.all_gather(b_qv, "narrow", axis=0))
+        b_out_full, gain_two_full, shift_two_full = lax.all_gather(
+            jnp.stack([b_out, ln2_gain, ln2_shift]), "wide", axis=1, tiled=True
+        )
+        x_tok = to_tokens(rows_input)
+        dy_tok = to_tokens(rows_cot)
+        normed_one, inv_one, norm_one = norm_forward(rows_input, ln1_gain, ln1_shift)
+        qkv_part = jnp.einsum("tk,nkc->tnc", norm_one, wq_all, preferred_element_type=F32)
+        qkv_rows = sum_tokens(qkv_part).transpose(1, 0, 2)
+        qkv_rows = (qkv_rows + bias_three).astype(BF)
+        cot_all = gather_narrow(dy_tok.astype(BF))
     heads_all = qkv_rows.reshape(narrow, -1, 3, part).transpose(1, 2, 0, 3).reshape(-1, 3, width)
     attended, log_total = attend_forward(heads_all, allowed)
     residual = x_tok + dot(attended, wo_all, 1, 1) + b_out_full
@@ -184,7 +1087,12 @@
     inv_two = lax.rsqrt(jnp.mean(residual * residual, axis=1, keepdims=True) - mean_two * mean_two + EPS)
     normed_two = (residual - mean_two) * inv_two
     norm_two = (normed_two * gain_two_full + shift_two_full).astype(BF)
-    norm_two_all = gather_narrow(norm_two)
+    if square:
+        norm_two_all, wf_all, wp_all = pair_stage(norm_two, wf_half, wp_half)
+        norm_two_all = norm_two_all.reshape(-1, width)
+        wf_all, wp_all = wf_all.reshape(width, hid), wp_all.reshape(width, hid)
+    else:
+        norm_two_all = line_gather(norm_two).reshape(-1, width)
     pre_act = dot(norm_two_all, wf_all, 1, 0) + b_fc
     hidden = gelu_value(pre_act).astype(BF)
     out_tok = residual + sum_narrow(dot(hidden, wp_all, 1, 1))
@@ -201,8 +1109,8 @@
     def share(total):
         return lax.all_gather(total, "dp", axis=0, tiled=True).astype(F32)
 
-    grad_w_proj = share(reduce_wide(dot(cot_all, hidden, 0, 0)))
-    grad_w_fc = share(reduce_wide(dot(norm_two_all, pre_cot, 0, 0)))
+    wp_grad = reduce_wide(dot(cot_all, hidden, 0, 0))
+    wf_grad = reduce_wide(dot(norm_two_all, pre_cot, 0, 0))
 
     scaled = norm_two_grad * gain_two_full
     mean_scaled = jnp.mean(scaled, axis=1, keepdims=True)
@@ -210,28 +1118,31 @@
     resid_grad = dy_tok + inv_two * (scaled - mean_scaled - normed_two * mean_cross)
     resid_cot = resid_grad.astype(BF)
     attended_cot = dot(resid_cot, wo_all, 1, 0).astype(BF)
-    wo_grad = reduce_wide(dot(resid_cot, attended, 0, 0))
-    wo_grad = lax.psum_scatter(wo_grad, "narrow", scatter_dimension=1, tiled=True)
-    grad_w_out = share(wo_grad)
+    wo_grad = dot(resid_cot, attended, 0, 0).astype(BF)
 
     qkv_grad = attend_backward(heads_all, allowed, log_total, attended_cot)
-    qkv_cot = qkv_grad.astype(BF).reshape(-1, 3, narrow, part).transpose(0, 2, 1, 3)
-    qkv_cot_all = gather_tokens(qkv_cot.reshape(-1, narrow, 3 * part))
-    norm_one_grad = jnp.einsum("tnc,nkc->tk", qkv_cot_all, wq_all, preferred_element_type=F32)
-    wq_grad = jnp.einsum("tk,tnc->nkc", norm_one, qkv_cot_all, preferred_element_type=F32).astype(BF)
-    wq_grad = lax.psum_scatter(
-        wq_grad.reshape(narrow * feats, 3 * part), ("narrow", "dp"), scatter_dimension=0, tiled=True
-    )
-    grad_w_qkv = share(wq_grad).reshape(feats, 3, part)
-
-    resid_back = to_features(resid_grad)
-    grad_input_rows = resid_back + norm_backward(norm_one_grad, normed_one, inv_one, ln1_gain)
-
+    qkv_cot = qkv_grad.astype(BF).reshape(-1, 3, narrow, part).transpose(2, 0, 1, 3)
+    qkv_cot = qkv_cot.reshape(narrow, -1, 3 * part)
+    if square:
+        norm_one_grad, grad_w_qkv, grad_w_out = back_stage(
+            qkv_cot, norm_t, wq_all, wo_grad.reshape(2 * wide, -1, width)
+        )
+        grad_w_qkv = grad_w_qkv.reshape(feats, 3, part)
+        grad_w_out = grad_w_out.reshape(feats, part)
+    else:
+        qkv_cot_all = lax.all_gather(qkv_cot, "wide", axis=1, tiled=True)
+        wq_grad = jnp.einsum("tk,ntc->nkc", norm_one, qkv_cot_all, preferred_element_type=F32).astype(BF)
+        wq_grad = lax.psum_scatter(
+            wq_grad.reshape(narrow * feats, 3 * part), ("narrow", "dp"), scatter_dimension=0, tiled=True
+        )
+        grad_w_qkv = share(wq_grad).reshape(feats, 3, part)
+        norm_one_grad = jnp.einsum("nkc,ntc->kt", wq_all, qkv_cot_all, preferred_element_type=F32)
+        wo_grad = lax.psum_scatter(reduce_wide(wo_grad), "narrow", scatter_dimension=1, tiled=True)
+        grad_w_out = share(wo_grad)
+
+    resid_back = to_features(resid_grad).T
     qkv_sums = jnp.sum(qkv_grad, axis=0)
-    fc_full = lax.dynamic_update_slice_in_dim(
-        jnp.zeros((narrow * hid,), F32), jnp.sum(pre_grad, axis=0), n_index * hid, 0
-    )
-    token_terms = jnp.stack(
+    wide_terms = as_rows(
         [
             qkv_sums[0],
             qkv_sums[2],
@@ -240,24 +1151,56 @@
             jnp.sum(norm_two_grad, axis=0),
         ]
     )
-    feature_terms = jnp.stack(
-        [
-            jnp.sum(norm_one_grad * normed_one, axis=0),
-            jnp.sum(norm_one_grad, axis=0),
-            jnp.sum(rows_cot, axis=0),
-        ]
-    )
-    feature_full = lax.dynamic_update_slice_in_dim(
-        jnp.zeros((3, width), F32), feature_terms, w_index * feats, 1
-    )
-    token_sum, feature_sum, fc_sum = lax.psum((token_terms, feature_full, fc_full), ("dp", "wide", "narrow"))
+    fc_terms = jnp.sum(pre_grad, axis=0)
+    if square:
+        normed = (block_input - stats[0:1]) * stats[1:2]
+        scaled = norm_one_grad * ln1_gain[:, None]
+        sums = as_rows([jnp.sum(scaled, axis=0), jnp.sum(scaled * normed, axis=0)])
+        feat_terms = as_rows(
+            [jnp.sum(norm_one_grad * normed, axis=1), jnp.sum(norm_one_grad, axis=1), jnp.sum(block_cotangent, axis=1)]
+        )
+        span = max(width, hid)
+        packed = jnp.zeros((8, span), F32)
+        packed = packed.at[:, :width].set(wide_terms).at[TOKEN_TERMS, :hid].set(fc_terms)
+        grad_input, packed_sum, feat_sum, grad_w_fc, grad_w_proj = final_stage(
+            block_input,
+            stats,
+            norm_one_grad,
+            resid_back,
+            ln1_gain[:, None],
+            sums,
+            packed,
+            feat_terms,
+            wf_grad,
+            wp_grad,
+        )
+        grad_w_fc, grad_w_proj = grad_w_fc.reshape(w_fc.shape), grad_w_proj.reshape(w_proj.shape)
+        token_sum = packed_sum[:TOKEN_TERMS, :width]
+        grad_b_fc = packed_sum[TOKEN_TERMS, :hid]
+        gain_one, shift_one, proj_bias = feat_sum[0], feat_sum[1], feat_sum[2]
+    else:
+        grad_w_proj, grad_w_fc = share(wp_grad), share(wf_grad)
+        norm_one_grad = norm_one_grad.T
+        grad_input = (resid_back.T + norm_backward(norm_one_grad, normed_one, inv_one, ln1_gain)).T
+        feature_terms = jnp.stack(
+            [
+                jnp.sum(norm_one_grad * normed_one, axis=0),
+                jnp.sum(norm_one_grad, axis=0),
+                jnp.sum(rows_cot, axis=0),
+            ]
+        )
+        feature_full = lax.dynamic_update_slice_in_dim(
+            jnp.zeros((3, width), F32), feature_terms, w_index * feats, 1
+        )
+        fc_full = lax.dynamic_update_slice_in_dim(jnp.zeros((narrow * hid,), F32), fc_terms, n_index * hid, 0)
+        token_sum, feature_sum, fc_sum = lax.psum((wide_terms, feature_full, fc_full), ("dp", "wide", "narrow"))
+        gain_one, shift_one, proj_bias = lax.dynamic_slice_in_dim(feature_sum, w_index * feats, feats, 1)
+        grad_b_fc = lax.dynamic_slice_in_dim(fc_sum, n_index * hid, hid, 0)
     grad_b_qv = lax.dynamic_slice_in_dim(token_sum[:2], n_index * part, part, 1)
-    out_bias, gain_two, shift_two = lax.dynamic_slice_in_dim(token_sum[2:], w_index * feats, feats, 1)
-    gain_one, shift_one, proj_bias = lax.dynamic_slice_in_dim(feature_sum, w_index * feats, feats, 1)
-    grad_b_fc = lax.dynamic_slice_in_dim(fc_sum, n_index * hid, hid, 0)
+    out_bias, gain_two, shift_two = lax.dynamic_slice_in_dim(token_sum[2:5], w_index * feats, feats, 1)
     return (
         output_rows.T,
-        grad_input_rows.T,
+        grad_input,
         gain_one,
         shift_one,
         grad_w_qkv,

time: 824 us -> 564 us (0.68)
  waiting for transfers between devices: 498 us -> 50.2 us
  Pallas kernels: 0 us -> 331 us
  blocking collectives: 93.3 us -> 0 us
  matrix products: 104 us -> 75.1 us
  other arithmetic: 23.3 us -> 12.5 us
    pallas_call x0 -> x5, Pallas kernels: none -> 331 us  [the longest x1 137 us: back_stage(): pl.pallas_call(back_kernel, out_shape=(shape_of((feats, tokens), F32), sh...]
    unnamed x25 -> x6, waiting for transfers between devices: 250 us -> 0.07 us
    all_gather x9 -> x0, waiting for transfers between devices: 180 us -> none  [the longest x2 70.7 us: gather_narrow(): return lax.all_gather(values, 'narrow', axis=0, tiled=True)]
    psum x1 -> x0, waiting for transfers between devices: 60 us -> none  [local(): lax.psum((token_terms, feature_full, fc_full), ('dp', 'wide', 'narrow'))]
    all_gather x5 -> x0, blocking collectives: 56.7 us -> none  [the longest x1 22.2 us: local(): lax.all_gather(jnp.stack([b_out, ln2_gain, ln2_shift]), 'wide', axis=1, t...]
    reduce_scatter x1 -> x2, waiting for transfers between devices: 0.01 us -> 40.3 us  [sum_narrow(): lax.psum_scatter(partial_value.astype(BF), 'narrow', scatter_dimension=0,...]
    dot_general x3 -> x0, matrix products: 21 us -> none  [the longest x1 8.21 us: local(): jnp.einsum('tk,nkc->tnc', norm_one, wq_all, preferred_element_type=F32)]
    all_to_all x1 -> x0, blocking collectives: 20 us -> none  [to_tokens(): lax.all_to_all(values, 'wide', split_axis=0, concat_axis=1, tiled=True)]
  transfers between devices with their start and end apart: 22 -> 7, of which waited for: 13 -> 3; matrix products, arithmetic and copies ran while one was open for 17% -> 19% of each run, Pallas kernels for 0% -> 46%
where the time goes in v4:
time: 564 us; the launch traced here: 554 us
  Pallas kernels  331 us (59%)
  matrix products  75.1 us (13%)
  local copies, waits for them, and re-layouts  59.8 us (11%)
  waiting for transfers between devices  50.2 us (9%)
  between operations  14.4 us (3%)
  other arithmetic  12.5 us (2%)
  starting transfers between devices  10.9 us (2%)
    pallas_call x1, Pallas kernels, back_stage(): pl.pallas_call(back_kernel, out_shape=(shape_of((feats, tokens), F32), sh...  137 us
    pallas_call x1, Pallas kernels, front_stage(): pl.pallas_call(front_kernel, out_shape=(shape_of((feats, tokens), BF), sh...  61.9 us
    pallas_call x1, Pallas kernels, pair_stage(): pl.pallas_call(functools.partial(pair_kernel, len(weights)), out_shape=(s...  56.1 us
    pallas_call x1, Pallas kernels, qkv_stage(): pl.pallas_call(qkv_kernel, out_shape=(shape_of((pieces, block, cols), BF)...  55.1 us
    dot_general x9, matrix products, dot(): lax.dot_general(a, b, (((ca,), (cb,)), ((), ())), preferred_element_type=...  53.8 us
    reduce_scatter x2, waiting for transfers between devices, sum_narrow(): lax.psum_scatter(partial_value.astype(BF), 'narrow', scatter_dimension=0,...  40.3 us
    pallas_call x1, Pallas kernels, final_stage(): pl.pallas_call(final_kernel, out_shape=(shape_of(x.shape, F32), shape_of(...  20.8 us
    unnamed x77, local copies, waits for them, and re-layouts  14 us
  transfers between devices with their start and end apart: 7, of which 3 were waited for; matrix products, arithmetic and copies ran while one was open for 19% of the time, Pallas kernels for 46%

profile of v4, /device:TPU:17, one launch (start us, length us, event | category | flops | bytes accessed | tf_op | source)
XLA Modules:
  0.0 553.9 jit_solution(6036522659438151461)
XLA Ops:
  17.8 61.9 %front_stage.1 = (bf16[400,512]{1,0:T(8,128)(2,1)}, f32[8,512]{1,0:T(8,128)}, f32[1600,128]{1,0:T(8,128)}, f32[1600,128]{1,0:T(8,128)}, f32[4,8,400]{2,1,0:T(8,1...) custom-call(f32[400,512]{1,0:T(8,128)} %x_ref.3, f32[400,512]{1,0:T(8,128)} %dy_ref.1, ...), custom_call_target="tpu_custom_call" | custom-call | flops 10000000000 | bytes 60000000 | tf_op jit(solution)/shard_map/front_stage/pallas_call | solution.py:400
  85.8 55.1 %qkv_stage.1 = (bf16[4,128,1200]{2,1,0:T(8,128)(2,1)}, bf16[4,128,1600]{2,1,0:T(8,128)(2,1)}) custom-call(bf16[512,400]{1,0:T(8,128)(2,1)} %bitcast.144, bf16[4,400,1200]{2,1,0:T(8,128)(2,1)} %bitcast.173, f32[4,1,1200]{2,1,0:T(1,128)} %concatenate.28.bias_ref, bf16[128,1600]{1,0:T(8,128)(2,1)} %bitcast_convert_fusion.dy_ref), custom_call_target="tpu_custom_call" | custom-call | flops 30000001024 | bytes 100000000 | tf_op jit(solution)/shard_map/qkv_stage/pallas_call | solution.py:498
  154.4 4.6 fusion.70
  160.0 56.1 %pair_stage.1 = (bf16[4,128,1600]{2,1,0:T(8,128)(2,1)}, bf16[8,200,1600]{2,1,0:T(8,128)(2,1)}, bf16[8,200,1600]{2,1,0:T(8,128)(2,1)}) custom-call(bf16[128,1600]{1,0:T(8,128)(2,1)} %add_convert_fusion.own_ref, bf16[200,1600]{1,0:T(8,128)(2,1)} %get-tuple-element.201.refs_0_, bf16[200,1600]{1,0:T(8,128)(2,1)} %get-tuple-element.200.refs_1_), custom_call_target="tpu_custom_call" | custom-call | flops 20000000000 | bytes 70000000 | tf_op jit(solution)/shard_map/pair_stage/pallas_call | solution.py:572
  216.1 6.3 %convolution_add_fusion = f32[512,1600]{0,1:T(8,128)S(1)} fusion(bf16[512,1600]{1,0:T(8,128)(2,1)} %bitcast.177, bf16[1600,1600]{1,0:T(8,128)(2,1)} %bitcast.169, f32[1600]{0:T(1024)S(1)} %copy-done.29), kind=kOutput, calls=%fused_computation.14 | convolution fusion | flops 2622259200 | bytes 10041600 | tf_op jit(solution)/shard_map/dot_general | solution.py:33
  222.5 6.3 %fusion.85 = (f32[1600]{0:T(1024)S(1)}, bf16[512,1600]{0,1:T(8,128)(2,1)S(1)}) fusion(f32[512,1600]{0,1:T(8,128)S(1)} %convolution_add_fusion, bf16[512,1600]{1,0:T(8,128)(2,1)S(1)} %bitcast.176, bf16[1600,1600]{1,0:T(8,128)(2,1)S(1)} %bitcast.168), kind=kOutput, calls=%fused_computation.111 | convolution fusion | flops 2637822464 | bytes 11680000 | tf_op jit(solution)/shard_map/dot_general | solution.py:33
  230.0 4.2 convolution_convert_fusion.3
  234.2 3.5 copy.140
  237.8 8.0 %convolution_convert_fusion.4 = bf16[512,1600]{0,1:T(8,128)(2,1)} fusion(bf16[1600,1600]{1,0:T(8,128)(2,1)} %bitcast.167, f32[512,1600]{0,1:T(8,128)} %copy-done.32), kind=kOutput, calls=%fused_computation.16 | convolution fusion | flops 2629632000 | bytes 10035200 | tf_op jit(solution)/shard_map/dot_general | solution.py:33
  245.8 3.5 copy.137
  249.6 7.6 %convolution_convert_fusion.1 = bf16[1600,1600]{1,0:T(8,128)(2,1)} fusion(bf16[512,1600]{1,0:T(8,128)(2,1)} %bitcast.178, bf16[512,1600]{0,1:T(8,128)(2,1)} %copy-done.33), kind=kOutput, calls=%fused_computation.3 | convolution fusion | flops 2624000000 | bytes 8396800 | tf_op jit(solution)/shard_map/dot_general | solution.py:33
  261.9 8.2 %convolution_convert_fusion = bf16[1600,1600]{1,0:T(8,128)(2,1)} fusion(bf16[512,1600]{1,0:T(8,128)(2,1)} %bitcast.175, f32[512,1600]{0,1:T(8,128)} %copy-done.32), kind=kOutput, calls=%fused_computation.2 | convolution fusion | flops 2631372800 | bytes 10035200 | tf_op jit(solution)/shard_map/dot_general | solution.py:33
  274.0 37.9 %reduce-scatter.9.cloned.1.call-done = bf16[128,1600]{1,0:T(8,128)(2,1)} async-done(((bf16[512,1600]{1,0:T(8,128)(2,1)}), bf16[128,1600]{1,0:T(8,128)(2,1)}) %reduce-scatter.9.cloned.1.call-update) | async-done | bytes 409616 | tf_op jit(solution)/shard_map/reduce_scatter | solution.py:72
  317.8 4.7 convolution_convert_fusion.5
  322.4 3.7 bitcast_convert_fusion.1
  327.7 4.8 bitcast_convert_fusion.2
  332.5 4.7 bitcast_convert_fusion.3
  340.0 3.9 all-to-all-start.1
  344.0 3.9 convolution_convert_fusion.2
  347.9 137.1 %back_stage.1 = (f32[400,512]{1,0:T(8,128)}, f32[2,200,1200]{2,1,0:T(8,128)}, f32[2,200,400]{2,1,0:T(8,128)}) custom-call(bf16[4,128,1200]{2,1,0:T(8,128)(2,1)} %copy.147.cot_ref, bf16[400,512]{1,0:T(8,128)(2,1)} %get-tuple-element.68.norm_ref, bf16[4,400,1200]{2,1,0:T(8,128)(2,1)} %bitcast.174, bf16[8,200,1600]{2,1,0:T(8,128)(2,1)} %bitcast.121), custom_call_target="tpu_custom_call" | custom-call | flops 40000000000 | bytes 100000000 | tf_op jit(solution)/shard_map/back_stage/pallas_call | solution.py:850
  485.0 5.5 reshape.209
  490.5 4.3 copy.152
  502.5 9.8 %all-to-all-done = f32[128,4,400]{0,2,1:T(8,128)S(1)} async-done(((f32[128,4,400]{0,2,1:T(8,128)}), f32[128,4,400]{0,2,1:T(8,128)S(1)}, u32[]{:S(2)}, u32[]{:S(2)}) %all-to-all-start) | async-done | bytes 819232 | tf_op jit(solution)/shard_map/all_to_all | solution.py:80
  513.3 20.8 %final_stage.1 = (f32[400,512]{1,0:T(8,128)}, f32[8,1600]{1,0:T(8,128)}, f32[8,400]{1,0:T(8,128)}, f32[2,200,1600]{2,1,0:T(8,128)}, f32[2,200,1600]{2,1,0:T(8,128)}) custom-call(f32[400,512]{1,0:T(8,128)} %x_ref.3, f32[8,512]{1,0:T(8,128)} %get-tuple-element.78.stat_ref, f32[400,512]{1,0:T(8,128)} %get-tuple-element.80.grad_ref, ...), custom_call_target="tpu_custom_call" | custom-call | flops 1000000000 | bytes 20000000 | tf_op jit(solution)/shard_map/final_stage/pallas_call | solution.py:963
  (155 shorter events, 72.9 us)
Async XLA Ops:
  7.2 7.8 %copy-start = (f32[400,3,400]{2,0,1:T(8,128)S(1)}, f32[400,3,400]{2,0,1:T(8,128)}, u32[]{:S(2)}) copy-start(f32[400,3,400]{2,0,1:T(8,128)} %param.26) | copy-start | bytes 5760004
  7.2 265.3 %reduce-scatter.11.cloned.1.call-start = ((), (), s32[]{:S(2)}) async-start(), calls=%async_computation.7 | async-start | bytes 2129920 | tf_op jit(solution)/shard_map/reduce_scatter | solution.py:72
  7.2 144.3 %collective-permute-start = (s32[1,128]{1,0:T(1,128)}, s32[1,128]{1,0:T(1,128)S(1)}, u32[]{:S(2)}, u32[]{:S(2)}) collective-permute-start(s32[1,128]{1,0:T(1,128)} %param.23), channel_id=1, source_target_pairs={{0,0},{4,1},{8,2},{12,3},{1,4},{5,5},{9,6},{13,7},{2,8},{6,9},{10,... | collective-permute-start | bytes 1544 | tf_op jit(solution)/shard_map/ppermute | solution.py:1036
  17.1 62.6 %copy-start.27 = (f32[8]{0:T(128)}, f32[8]{0:T(128)S(1)}, u32[]{:S(2)}) copy-start(f32[8]{0:T(128)S(1)} %pad.22.clone) | copy-start | bytes 100
  154.4 4.6 copy-start.13
  160.0 56.1 %copy-start.29 = (f32[1600]{0:T(1024)S(1)}, f32[1600]{0:T(1024)}, u32[]{:S(2)}) copy-start(f32[1600]{0:T(1024)} %param.33) | copy-start | bytes 19204
  216.1 6.4 %copy-start.30 = (bf16[8,200,1600]{2,1,0:T(8,128)(2,1)S(1)}, bf16[8,200,1600]{2,1,0:T(8,128)(2,1)}, u32[]{:S(2)}) copy-start(bf16[8,200,1600]{2,1,0:T(8,128)(2,1)} %get-tuple-element.77) | copy-start | bytes 15360004
  216.1 6.4 %copy-start.31 = (bf16[4,128,1600]{2,1,0:T(8,128)(2,1)S(1)}, bf16[4,128,1600]{2,1,0:T(8,128)(2,1)}, u32[]{:S(2)}) copy-start(bf16[4,128,1600]{2,1,0:T(8,128)(2,1)} %get-tuple-element.79) | copy-start | bytes 4915204
  216.1 13.9 %slice-start = ((s8[5324800]{0:T(1024)(128)(4,1)}), s8[4194304]{0:T(1024)(128)(4,1)S(1)}, s32[]{:S(2)}) async-start(s8[5324800]{0:T(1024)(128)(4,1)} %bitcast.170), calls=%async_computation.10 | async-start | bytes 8388608
  222.5 6.3 %copy-start.32 = (f32[512,1600]{0,1:T(8,128)}, f32[512,1600]{0,1:T(8,128)S(1)}, u32[]{:S(2)}) copy-start(f32[512,1600]{0,1:T(8,128)S(1)} %convolution_add_fusion) | copy-start | bytes 9830404
  222.5 7.5 %slice-start.1 = ((s8[5324800]{0:T(1024)(128)(4,1)}), s8[1130496]{0:T(1024)(128)(4,1)S(1)}, s32[]{:S(2)}) async-start(s8[5324800]{0:T(1024)(128)(4,1)} %bitcast.170), calls=%async_computation.11 | async-start | bytes 2260992
  237.8 74.1 %reduce-scatter.9.cloned.1.call-start = ((), (), s32[]{:S(2)}) async-start(), calls=%async_computation.6 | async-start | bytes 2129920 | tf_op jit(solution)/shard_map/reduce_scatter | solution.py:72
  249.4 263.9 %reduce-scatter.13.cloned.1.call-start = ((), (), s32[]{:S(2)}) async-start(), calls=%async_computation.8 | async-start | bytes 5990400
  257.3 256.0 %reduce-scatter.15.cloned.1.call-start = ((), (), s32[]{:S(2)}) async-start(), calls=%async_computation.9 | async-start | bytes 5990400
  338.5 5.4 copy-start.14
  340.0 156.6 %all-to-all-start.1 = ((f32[128,4,400]{0,2,1:T(8,128)}), f32[128,4,400]{0,2,1:T(8,128)S(1)}, u32[]{:S(2)}, u32[]{:S(2)}) async-start(f32[128,4,400]{0,2,1:T(8,128)} %bitcast.41), calls=%async_computation.3 | async-start | bytes 1638400 | tf_op jit(solution)/shard_map/all_to_all | solution.py:80
  490.5 4.3 copy-start.18
  490.5 4.3 copy-start.19
  495.7 5.1 copy-start.28
  495.9 6.6 %copy-start.20 = (f32[8,1600]{1,0:T(8,128)}, f32[8,1600]{1,0:T(8,128)S(1)}, u32[]{:S(2)}) copy-start(f32[8,1600]{1,0:T(8,128)S(1)} %scatter.4.wide_ref) | copy-start | bytes 153604
  496.6 15.7 %copy-start.23 = (f32[400]{0:T(512)S(1)}, f32[400]{0:T(512)}, u32[]{:S(2)}) copy-start(f32[400]{0:T(512)} %param.35) | copy-start | bytes 4804
  496.6 15.6 %all-to-all-start = ((f32[128,4,400]{0,2,1:T(8,128)}), f32[128,4,400]{0,2,1:T(8,128)S(1)}, u32[]{:S(2)}, u32[]{:S(2)}) async-start(f32[128,4,400]{0,2,1:T(8,128)} %bitcast.23), calls=%async_computation.1 | async-start | bytes 1638400 | tf_op jit(solution)/shard_map/all_to_all | solution.py:80
  513.2 28.8 %copy-start.15 = (f32[2,200,400]{2,1,0:T(8,128)S(1)}, f32[2,200,400]{2,1,0:T(8,128)}, u32[]{:S(2)}) copy-start(f32[2,200,400]{2,1,0:T(8,128)} %get-tuple-element.85) | copy-start | bytes 1920004
  534.9 8.1 %copy-start.5 = (f32[2,200,1600]{2,1,0:T(8,128)S(1)}, f32[2,200,1600]{2,1,0:T(8,128)}, u32[]{:S(2)}) copy-start(f32[2,200,1600]{2,1,0:T(8,128)} %get-tuple-element.86) | copy-start | bytes 7680004
  (19 other events, 42.4 us)
Sparse Core Ops, SparseCore 0:
  237.9 34.6 reduce-scatter.10
  275.4 36.3 reduce-scatter.8
  315.3 84.6 reduce-scatter.12
  403.3 76.8 reduce-scatter.14

commit v5 on v4

v5 whole, which is shorter than its diff:
```python
import functools
import math

import jax
import jax.numpy as jnp
from jax import lax
from jax.experimental import pallas as pl
from jax.experimental.pallas import tpu as pltpu
from jax.sharding import PartitionSpec as P

HEADS = 25
HEAD = 64

EPS = 1e-05
GELU_C = math.sqrt(2.0 / math.pi)
BF = jnp.bfloat16
F32 = jnp.float32


def gelu_value(pre_act):
    inner = GELU_C * (pre_act + 0.044715 * pre_act * pre_act * pre_act)
    return 0.5 * pre_act * (1.0 + jnp.tanh(inner))


def gelu_slope(pre_act):
    tanh_part = jnp.tanh(GELU_C * (pre_act + 0.044715 * pre_act * pre_act * pre_act))
    return 0.5 * (1.0 + tanh_part) + 0.5 * pre_act * (1.0 - tanh_part * tanh_part) * GELU_C * (
        1.0 + 3.0 * 0.044715 * pre_act * pre_act
    )


def dot(a, b, ca, cb):
    return lax.dot_general(a, b, (((ca,), (cb,)), ((), ())), preferred_element_type=F32)


def row_totals(first_term, second_term):
    return lax.psum(
        (jnp.sum(first_term, axis=1, keepdims=True), jnp.sum(second_term, axis=1, keepdims=True)),
        "wide",
    )


def norm_forward(inputs, gain_shard, shift_shard):
    full_width = inputs.shape[1] * lax.axis_size("wide")
    total_sum, square_sum = row_totals(inputs, inputs * inputs)
    mean_row = total_sum / full_width
    inv_std = lax.rsqrt(square_sum / full_width - mean_row * mean_row + EPS)
    normed = (inputs - mean_row) * inv_std
    return (normed, inv_std, (normed * gain_shard + shift_shard).astype(BF))


def norm_backward(row_grads, normed, inv_std, gain_shard):
    full_width = row_grads.shape[1] * lax.axis_size("wide")
    scaled = row_grads * gain_shard
    first_sum, second_sum = row_totals(scaled, scaled * normed)
    return inv_std * (scaled - first_sum / full_width - normed * (second_sum / full_width))


def gather_narrow(values):
    return lax.all_gather(values, "narrow", axis=1, tiled=True)


def sum_tokens(partial_value):
    return lax.psum_scatter(partial_value.astype(BF), "wide", scatter_dimension=0, tiled=True).astype(F32)


def sum_narrow(partial_value):
    return lax.psum_scatter(partial_value.astype(BF), "narrow", scatter_dimension=1, tiled=True).astype(F32)


def to_tokens(values):
    return lax.all_to_all(values, "wide", split_axis=1, concat_axis=0, tiled=True)


def to_features(values):
    return lax.all_to_all(values, "wide", split_axis=0, concat_axis=1, tiled=True)


def block_mask(starts):
    position = jnp.arange(starts.shape[0])
    return (position[None, :] <= position[:, None]) & (starts[:, None] == starts[None, :])


def split_heads(values):
    return values.reshape(values.shape[0], HEADS, HEAD)


def attend_forward(heads_all, allowed):
    score_scale = 1.0 / math.sqrt(HEAD)
    queries = split_heads(heads_all[:, 0])
    keys_part = split_heads(heads_all[:, 1])
    values_part = split_heads(heads_all[:, 2])
    scores = jnp.einsum("ihd,jhd->hij", queries, keys_part, preferred_element_type=F32) * score_scale
    log_total = jnp.log(jnp.sum(jnp.where(allowed, jnp.exp(scores), 0.0), axis=2, keepdims=True))
    attn_probs = jnp.where(allowed, jnp.exp(scores - log_total), 0.0).astype(BF)
    attended = jnp.einsum("hij,jhd->ihd", attn_probs, values_part, preferred_element_type=F32)
    return (attended.reshape(heads_all.shape[0], HEADS * HEAD).astype(BF), log_total)


def attend_backward(heads_all, allowed, log_total, attended_cot):
    score_scale = 1.0 / math.sqrt(HEAD)
    queries = split_heads(heads_all[:, 0])
    keys_part = split_heads(heads_all[:, 1])
    values_part = split_heads(heads_all[:, 2])
    scores = jnp.einsum("ihd,jhd->hij", queries, keys_part, preferred_element_type=F32) * score_scale
    probs_full = jnp.where(allowed, jnp.exp(scores - log_total), 0.0)
    cot_heads = split_heads(attended_cot)
    dprobs = jnp.einsum("ihd,jhd->hij", cot_heads, values_part, preferred_element_type=F32)
    row_delta = jnp.sum(probs_full * dprobs, axis=2, keepdims=True)
    score_cot = (probs_full * (dprobs - row_delta) * score_scale).astype(BF)
    query_grad = jnp.einsum("hij,jhd->ihd", score_cot, keys_part, preferred_element_type=F32)
    key_grad = jnp.einsum("hij,ihd->jhd", score_cot, queries, preferred_element_type=F32)
    value_grad = jnp.einsum("hij,ihd->jhd", probs_full.astype(BF), cot_heads, preferred_element_type=F32)
    stacked = jnp.stack([query_grad, key_grad, value_grad], axis=1)
    return stacked.reshape(heads_all.shape[0], 3, HEADS * HEAD)


MESH = pl.DeviceIdType.MESH
VMEM_LIMIT = 60 * 1024 * 1024
def params(collective_id):
    return pltpu.CompilerParams(
        collective_id=collective_id, has_side_effects=True, vmem_limit_bytes=VMEM_LIMIT
    )


def in_vmem(count):
    return [pl.BlockSpec(memory_space=pltpu.VMEM)] * count


def shape_of(shape, dtype):
    return jax.ShapeDtypeStruct(shape, dtype)


def square_peers():
    me = lax.axis_index("wide")
    return me, me + 1 - 2 * lax.rem(me, 2), lax.rem(me + 2, 4), 3 - me


def greet(peers, line=None):
    barrier = pltpu.get_barrier_semaphore()
    count = len(peers)
    for axis, peer in peers:
        pl.semaphore_signal(barrier, inc=1, device_id={axis: peer}, device_id_type=MESH)
    if line is not None:
        n, _, has_down, has_up = line
        for has, peer in ((has_down, n - 1), (has_up, n + 1)):

            @pl.when(has)
            def _():
                pl.semaphore_signal(barrier, inc=1, device_id={"narrow": peer}, device_id_type=MESH)

        count = count + has_down.astype(jnp.int32) + has_up.astype(jnp.int32)
    pl.semaphore_wait(barrier, count)


def remote(src, dst, send_sem, recv_sem, axis, peer):
    return pltpu.make_async_remote_copy(
        src_ref=src,
        dst_ref=dst,
        send_sem=send_sem,
        recv_sem=recv_sem,
        device_id={axis: peer},
        device_id_type=MESH,
    )


def line_sides():
    n, count = lax.axis_index("narrow"), lax.axis_size("narrow")
    return n, count, n > 0, n < count - 1


def halves(cols):
    first = cols // 256 * 128
    return (0, first), (first, cols - first)


class SquareGather:
    def __init__(self, items, send_sem, recv_sem, siblings=True):
        self.items, self.send_sem, self.recv_sem, self.siblings = items, send_sem, recv_sem, siblings
        self.me, xp, yp, self.dg = square_peers()
        self.ways = ((xp, yp), (yp, xp))
        self.core = lax.axis_index("dp")

    def place(self, i, chip):
        return self.items[i][1](chip)

    def copy(self, i, k):
        first, second = self.ways[i % 2]
        own = self.items[i][0]
        src, dst, axis, peer = {
            0: (own, self.me, "wide", first),
            1: (own, self.me, "wide", second),
            2: (own, self.me, "dp", 1 - self.core),
            3: (None, first, "wide", second),
            4: (None, first, "dp", 1 - self.core),
            5: (None, second, "dp", 1 - self.core),
            6: (None, self.dg, "dp", 1 - self.core),
        }[k]
        dst = self.place(i, dst)
        return remote(dst if src is None else src, dst, self.send_sem.at[i, k], self.recv_sem.at[i, k], axis, peer)

    def start(self):
        for k in range(3 if self.siblings else 2):
            for i in range(len(self.items)):
                self.copy(i, k).start()
        for i in range(len(self.items)):
            self.place(i, self.me)[...] = self.items[i][0][...]

    def relay(self, i):
        self.copy(i, 0).wait_recv()
        self.copy(i, 3).start()
        if self.siblings:
            self.copy(i, 4).start()
            self.copy(i, 1).wait_recv()
            self.copy(i, 5).start()

    def finish(self):
        if self.siblings:
            for i in range(len(self.items)):
                self.copy(i, 3).wait_recv()
                self.copy(i, 6).start()
        for i in range(len(self.items)):
            for k in (2, 4, 5, 6) if self.siblings else (1, 3):
                self.copy(i, k).wait_recv()
            for k in range(7) if self.siblings else (0, 1, 3):
                self.copy(i, k).wait_send()


def gather_items(own_refs, whole_refs):
    core = lax.axis_index("dp")
    return [
        (own.at[:, pl.ds(*span)], lambda chip, span=span, whole=whole: whole.at[chip * 2 + core, :, pl.ds(*span)])
        for own, whole in zip(own_refs, whole_refs)
        for span in halves(own.shape[1])
    ]


class LineGather:
    def __init__(self, own_ref, place, send_sem, recv_sem, core_send=None, core_recv=None):
        self.own_ref, self.place, self.send_sem, self.recv_sem = own_ref, place, send_sem, recv_sem
        self.core_send, self.core_recv = core_send, core_recv
        self.core = lax.axis_index("dp")
        self.n, self.count, self.has_down, self.has_up = line_sides()

    def copy(self, block, way, src=None):
        place = self.place(block)
        return remote(
            place if src is None else src,
            place,
            self.send_sem.at[way, block],
            self.recv_sem.at[block],
            "narrow",
            self.n + 1 - 2 * way,
        )

    def share(self, block, src=None):
        place = self.place(block)
        return remote(
            place if src is None else src, place, self.core_send.at[block], self.core_recv.at[block], "dp", 1 - self.core
        )

    def start(self):
        @pl.when(self.has_up)
        def _():
            self.copy(self.n, 0, self.own_ref).start()

        @pl.when(self.has_down)
        def _():
            self.copy(self.n, 1, self.own_ref).start()

        if self.core_send is not None:
            self.share(self.n, self.own_ref).start()
        self.place(self.n)[...] = self.own_ref[...]

    def step(self, step):
        below, above = self.n - step, self.n + step

        @pl.when(below >= 0)
        def _():
            self.copy(below, 0).wait_recv()

            @pl.when(self.has_up)
            def _():
                self.copy(below, 0).start()

            if self.core_send is not None:
                self.share(below).start()

        @pl.when(above < self.count)
        def _():
            self.copy(above, 1).wait_recv()

            @pl.when(self.has_down)
            def _():
                self.copy(above, 1).start()

            if self.core_send is not None:
                self.share(above).start()

    def finish(self):
        for step in range(self.count):
            below, above = self.n - step, self.n + step

            @pl.when((below >= 0) & self.has_up)
            def _():
                self.copy(below, 0).wait_send()

            @pl.when((above < self.count) & self.has_down)
            def _():
                self.copy(above, 1).wait_send()

        if self.core_send is not None:
            for block in range(self.count):
                self.share(block).wait()


def lane_block(ref, index):
    return ref.at[:, pl.ds(pl.multiple_of(index * 128, 128), 128)]


def own_rows(half):
    return pl.ds(pl.multiple_of(lax.axis_index("dp") * half, 8), half)


def front_kernel(
    x_ref, dy_ref, gain_ref, shift_ref, vec_ref, bias_ref, wo_ref, wq_ref, wf_ref,
    norm_ref, stat_ref, xt_ref, dyt_ref, vecs_ref, biases_ref, wos_ref, wqs_ref, wfs_ref,
    dy_half, sums, all_sums, wo_own, wo_parts, wo_row, wq_own, wf_own,
    send_sem, recv_sem, near_send, near_recv, line_send, line_recv, core_send, core_recv, square_send, square_recv,
    early_send, early_recv,
):
    feats, tokens = x_ref.shape
    wide = 4
    block = tokens // wide
    me, xp, yp, dg = square_peers()
    peers = (xp, yp, dg)
    n, count = lax.axis_index("narrow"), lax.axis_size("narrow")
    core = lax.axis_index("dp")
    others = [lax.rem(n + k, count) for k in range(1, count)]
    part = wo_ref.shape[1]
    half = feats // 2
    wo_own[...] = wo_ref[own_rows(half), :].astype(BF)
    for k in range(3):
        wq_own[:, k * part : (k + 1) * part] = wq_ref[k, own_rows(half), :].astype(BF)
    greet(
        [("wide", peer) for peer in peers] + [("narrow", peer) for peer in others] + [("dp", 1 - core)]
    )
    copies = []

    def send(src, dst, sems, k, j, axis, peer):
        copy = remote(src, dst, sems[0].at[k, j], sems[1].at[k, j], axis, peer)
        copy.start()
        copies.append(copy)

    near, across = (near_send, near_recv), (send_sem, recv_sem)
    for j, peer in enumerate(others):
        send(wo_own, wo_parts.at[n], near, 0, j, "narrow", peer)
        send(bias_ref, biases_ref.at[n], near, 1, j, "narrow", peer)
    line = LineGather(wq_own, lambda b: wqs_ref.at[b, core], line_send, line_recv, core_send, core_recv)
    line.start()
    x = x_ref[...]
    sums[...] = jnp.zeros_like(sums)
    stat_ref[...] = jnp.zeros_like(stat_ref)
    sums[0:1, :] = jnp.sum(x, axis=0, keepdims=True)
    sums[1:2, :] = jnp.sum(x * x, axis=0, keepdims=True)
    for j, peer in enumerate(peers):
        send(sums, all_sums.at[me], across, 0, j, "wide", peer)
        send(vec_ref, vecs_ref.at[me], across, 1, j, "wide", peer)
    dy_half[...] = dy_ref[...].astype(BF)
    wo_parts[n] = wo_own[...]
    biases_ref[n] = bias_ref[...]
    vecs_ref[me] = vec_ref[...]
    mine = pl.ds(pl.multiple_of(me * feats, 16), feats)
    for k, (src, dst) in enumerate(((dy_half, dyt_ref), (x_ref, xt_ref))):
        for j, peer in enumerate(peers):
            send(lane_block(src, peer), dst.at[mine, :], across, 2 + k, j, "wide", peer)
        dst[mine, :] = lane_block(src, me)[...]
    wf_own[...] = wf_ref[own_rows(half), : wf_own.shape[1]].astype(BF)
    early = SquareGather(gather_items((wf_own,), (wfs_ref,)), early_send, early_recv)
    early.start()
    for copy in copies[: 2 * (count - 1)]:
        copy.wait()
    for k in range(count):
        wo_row[:, k * part : (k + 1) * part] = wo_parts[k]
    gather = SquareGather(gather_items((wo_row,), (wos_ref,)), square_send, square_recv)
    gather.start()
    rest = copies[2 * (count - 1) :]
    for copy in rest[:6]:
        copy.wait()
    total = sums[...]
    for peer in peers:
        total = total + all_sums[peer]
    width = feats * wide
    mean = total[0:1, :] / width
    inv = lax.rsqrt(total[1:2, :] / width - mean * mean + EPS)
    stat_ref[0:1, :] = mean
    stat_ref[1:2, :] = inv
    line.step(1)
    norm_ref[...] = ((x_ref[...] - mean) * inv * gain_ref[...] + shift_ref[...]).astype(BF)
    early.relay(0)
    early.relay(1)
    line.step(2)
    gather.relay(0)
    gather.relay(1)
    for step in range(3, count):
        line.step(step)
    for copy in rest[6:]:
        copy.wait()
    early.finish()
    gather.finish()
    line.finish()


def front_stage(x, dy, gain, shift, vec, bias, wo, wq, wf):
    feats, tokens = x.shape
    count = lax.axis_size("narrow")
    half, part = feats // 2, wo.shape[1]
    width = part * count
    ahead = halves(wf.shape[1])[0][1]
    return pl.pallas_call(
        front_kernel,
        out_shape=(
            shape_of((feats, tokens), BF),
            shape_of((8, tokens), F32),
            shape_of((4 * feats, tokens // 4), F32),
            shape_of((4 * feats, tokens // 4), BF),
            shape_of((4,) + vec.shape, F32),
            shape_of((count,) + bias.shape, F32),
            shape_of((8, half, width), BF),
            shape_of((count, 2, half, 3 * part), BF),
            shape_of((8, half, ahead), BF),
        ),
        in_specs=in_vmem(9),
        out_specs=tuple(in_vmem(9)),
        scratch_shapes=[
            pltpu.VMEM((feats, tokens), BF),
            pltpu.VMEM((8, tokens), F32),
            pltpu.VMEM((4, 8, tokens), F32),
            pltpu.VMEM((half, part), BF),
            pltpu.VMEM((count, half, part), BF),
            pltpu.VMEM((half, width), BF),
            pltpu.VMEM((half, 3 * part), BF),
            pltpu.VMEM((half, ahead), BF),
            pltpu.SemaphoreType.DMA((4, 3)),
            pltpu.SemaphoreType.DMA((4, 3)),
            pltpu.SemaphoreType.DMA((2, count - 1)),
            pltpu.SemaphoreType.DMA((2, count - 1)),
            pltpu.SemaphoreType.DMA((2, count)),
            pltpu.SemaphoreType.DMA((count,)),
            pltpu.SemaphoreType.DMA((count,)),
            pltpu.SemaphoreType.DMA((count,)),
            pltpu.SemaphoreType.DMA((2, 7)),
            pltpu.SemaphoreType.DMA((2, 7)),
            pltpu.SemaphoreType.DMA((2, 7)),
            pltpu.SemaphoreType.DMA((2, 7)),
        ],
        compiler_params=params(1),
        cost_estimate=pl.CostEstimate(flops=10**10, bytes_accessed=60 * 10**6, transcendentals=0),
        name="front_stage",
    )(x, dy, gain, shift, vec, bias, wo, wq, wf)


def qkv_kernel(
    norm_ref, w_ref, bias_ref, dy_ref, out_ref, dys_ref,
    acc, first_out, first_in, second_out, second_in, send_sem, recv_sem, line_send, line_recv,
):
    pieces, feats, cols = w_ref.shape
    tokens = norm_ref.shape[0]
    block = tokens // 4
    me, xp, yp, dg = square_peers()
    greet((("wide", xp), ("wide", yp)), line_sides())
    line = LineGather(dy_ref, lambda b: lane_block(dys_ref, b), line_send, line_recv)
    line.start()

    def rows(index):
        return pl.ds(pl.multiple_of(index * block, block), block)

    def ways(p):
        turn = lax.rem(p, 2)
        return xp * (1 - turn) + yp * turn, yp * (1 - turn) + xp * turn

    def first_copy(p):
        return remote(first_out.at[p], first_in.at[p], send_sem.at[0, p], recv_sem.at[0, p], "wide", ways(p)[0])

    def second_copy(p):
        return remote(second_out.at[p], second_in.at[p], send_sem.at[1, p], recv_sem.at[1, p], "wide", ways(p)[1])

    def issue(p, carry):
        acc[p] = dot(norm_ref[...], w_ref[p], 1, 0)
        first_out[p, 0] = acc[p, rows(ways(p)[0]), :].astype(BF)
        first_out[p, 1] = acc[p, rows(dg), :].astype(BF)
        first_copy(p).start()
        return carry

    lax.fori_loop(0, pieces, issue, 0)
    line.step(1)

    def middle(p, carry):
        first_copy(p).wait()
        second_out[p] = (acc[p, rows(ways(p)[1]), :] + first_in[p, 1].astype(F32)).astype(BF)
        second_copy(p).start()
        return carry

    lax.fori_loop(0, pieces // 2, middle, 0)
    line.step(2)
    lax.fori_loop(pieces // 2, pieces, middle, 0)
    for step in range(3, line.count):
        line.step(step)

    def last(p, carry):
        second_copy(p).wait()
        total = acc[p, rows(me), :] + first_in[p, 0].astype(F32) + second_in[p].astype(F32)
        out_ref[p] = (total + bias_ref[p]).astype(BF)
        return carry

    lax.fori_loop(0, pieces, last, 0)
    line.finish()


def qkv_stage(norm, w, bias, dy):
    count = lax.axis_size("narrow")
    pieces, feats, cols = w.shape
    tokens = norm.shape[0]
    block = tokens // 4
    return pl.pallas_call(
        qkv_kernel,
        out_shape=(shape_of((pieces, block, cols), BF), shape_of((dy.shape[0], count * dy.shape[1]), BF)),
        in_specs=in_vmem(4),
        out_specs=tuple(in_vmem(2)),
        scratch_shapes=[
            pltpu.VMEM((pieces, tokens, cols), F32),
            pltpu.VMEM((pieces, 2, block, cols), BF),
            pltpu.VMEM((pieces, 2, block, cols), BF),
            pltpu.VMEM((pieces, block, cols), BF),
            pltpu.VMEM((pieces, block, cols), BF),
            pltpu.SemaphoreType.DMA((2, pieces)),
            pltpu.SemaphoreType.DMA((2, pieces)),
            pltpu.SemaphoreType.DMA((2, count)),
            pltpu.SemaphoreType.DMA((count,)),
        ],
        compiler_params=params(2),
        cost_estimate=pl.CostEstimate(flops=3 * 10**10, bytes_accessed=10**8, transcendentals=0),
        name="qkv_stage",
    )(norm, w, bias, dy)


def pair_kernel(
    own_ref, ahead_ref, wf_ref, wp_ref, all_ref, wfs_ref, wps_ref,
    wf_own, wp_own, send_sem, recv_sem, line_send, line_recv, local_sem,
):
    me, xp, yp, dg = square_peers()
    half, ahead = wp_own.shape[0], ahead_ref.shape[2]
    wf_own[...] = wf_ref[own_rows(half), ahead:].astype(BF)
    wp_own[...] = wp_ref[own_rows(half), :].astype(BF)
    greet((("wide", xp), ("wide", yp), ("dp", 1 - lax.axis_index("dp"))), line_sides())
    line = LineGather(own_ref, lambda b: lane_block(all_ref, b), line_send, line_recv)
    line.start()
    rest = wfs_ref.at[:, :, pl.ds(ahead, wf_own.shape[1])]
    gather = SquareGather(gather_items((wf_own, wp_own), (rest, wps_ref)), send_sem, recv_sem)
    gather.start()
    move = pltpu.make_async_copy(ahead_ref, wfs_ref.at[:, :, pl.ds(0, ahead)], local_sem)
    move.start()
    line.step(1)
    gather.relay(0)
    gather.relay(1)
    line.step(2)
    gather.relay(2)
    gather.relay(3)
    for step in range(3, line.count):
        line.step(step)
    gather.finish()
    line.finish()
    move.wait()


def pair_stage(own, ahead, wf, wp):
    count = lax.axis_size("narrow")
    rows, cols = wf.shape[0] // 2, wf.shape[1]
    return pl.pallas_call(
        pair_kernel,
        out_shape=(
            shape_of((own.shape[0], count * own.shape[1]), own.dtype),
            shape_of((8, rows, cols), BF),
            shape_of((8, rows, cols), BF),
        ),
        in_specs=in_vmem(4),
        out_specs=tuple(in_vmem(3)),
        scratch_shapes=[
            pltpu.VMEM((rows, cols - ahead.shape[2]), BF),
            pltpu.VMEM((rows, cols), BF),
            pltpu.SemaphoreType.DMA((4, 7)),
            pltpu.SemaphoreType.DMA((4, 7)),
            pltpu.SemaphoreType.DMA((2, count)),
            pltpu.SemaphoreType.DMA((count,)),
            pltpu.SemaphoreType.DMA,
        ],
        compiler_params=params(7),
        cost_estimate=pl.CostEstimate(flops=2 * 10**10, bytes_accessed=7 * 10**7, transcendentals=0),
        name="pair_stage",
    )(own, ahead, wf, wp)


class SquareSum:
    def __init__(self, part_ref, bufs, sems):
        self.part_ref = part_ref
        self.core_in, self.half, self.first_out, self.first_in, self.second_out, self.second_in = bufs
        self.core_send, self.core_recv, self.send_sem, self.recv_sem = sems
        self.me, xp, yp, self.dg = square_peers()
        self.ways = ((xp, yp), (yp, xp))
        self.core = lax.axis_index("dp")
        self.spans = halves(part_ref.shape[2])

    def core_copy(self, chip):
        return remote(
            self.part_ref.at[chip * 2 + 1 - self.core],
            self.core_in.at[chip],
            self.core_send.at[chip],
            self.core_recv.at[chip],
            "dp",
            1 - self.core,
        )

    def first_copy(self, i, k):
        cols = pl.ds(*self.spans[i])
        return remote(
            self.first_out.at[k, :, cols],
            self.first_in.at[k, :, cols],
            self.send_sem.at[i, k],
            self.recv_sem.at[i, k],
            "wide",
            self.ways[i][0],
        )

    def second_copy(self, i):
        cols = pl.ds(*self.spans[i])
        return remote(
            self.second_out.at[:, cols],
            self.second_in.at[:, cols],
            self.send_sem.at[i, 2],
            self.recv_sem.at[i, 2],
            "wide",
            self.ways[i][1],
        )

    def start(self):
        for chip in range(4):
            self.core_copy(chip).start()

    def issue(self):
        for chip in range(4):
            self.core_copy(chip).wait()
            total = self.part_ref[chip * 2 + self.core].astype(F32) + self.core_in[chip].astype(F32)
            self.half[chip] = total.astype(BF)
        for i, (at, size) in enumerate(self.spans):
            for k, chip in enumerate((self.ways[i][0], self.dg)):
                self.first_out[k, :, at : at + size] = self.half[chip, :, at : at + size]
                self.first_copy(i, k).start()

    def middle(self):
        for i, (at, size) in enumerate(self.spans):
            self.first_copy(i, 1).wait()
            total = self.half[self.ways[i][1], :, at : at + size].astype(F32)
            total = total + self.first_in[1, :, at : at + size].astype(F32)
            self.second_out[:, at : at + size] = total.astype(BF)
            self.second_copy(i).start()

    def finish(self, write):
        for i, (at, size) in enumerate(self.spans):
            self.first_copy(i, 0).wait()
            self.second_copy(i).wait()
            total = self.half[self.me, :, at : at + size].astype(F32)
            total = total + self.first_in[0, :, at : at + size].astype(F32)
            write(at, size, total + self.second_in[:, at : at + size].astype(F32))


def square_sum_scratch(rows, cols):
    return [
        pltpu.VMEM((4, rows, cols), BF),
        pltpu.VMEM((4, rows, cols), BF),
        pltpu.VMEM((2, rows, cols), BF),
        pltpu.VMEM((2, rows, cols), BF),
        pltpu.VMEM((rows, cols), BF),
        pltpu.VMEM((rows, cols), BF),
        pltpu.SemaphoreType.DMA((4,)),
        pltpu.SemaphoreType.DMA((4,)),
        pltpu.SemaphoreType.DMA((2, 3)),
        pltpu.SemaphoreType.DMA((2, 3)),
    ]


def ffn_back_kernel(
    part_ref, out_part_ref, cot_ref, hidden_ref, norm_ref, pre_ref, att_ref,
    sum_ref, out_sum_ref, wp_ref, wf_ref, atts_ref,
    wp_part, wf_part, leave, arrive, line_send, line_recv, share_send, share_recv, att_send, att_recv, *square,
):
    me, xp, yp, dg = square_peers()
    n, count, has_down, has_up = line_sides()
    core = lax.axis_index("dp")
    greet((("wide", xp), ("wide", yp), ("dp", 1 - core)), line_sides())
    rows = wp_part.shape[1]

    lines = ((part_ref, sum_ref), (out_part_ref, out_sum_ref))

    def line_copy(k, way, b):
        return remote(
            leave.at[k, way, b],
            arrive.at[k, way, b],
            line_send.at[k, way, b],
            line_recv.at[k, way, b],
            "narrow",
            n + 1 - 2 * way,
        )

    def turn(k, way, b, sends, joins):
        own = lines[k][0]

        @pl.when(sends & joins)
        def _():
            line_copy(k, way, b).wait_recv()
            total = own[:, b * 128 : (b + 1) * 128].astype(F32) + arrive[k, way, b].astype(F32)
            leave[k, way, b] = total.astype(BF)
            line_copy(k, way, b).start()

        @pl.when(sends & jnp.logical_not(joins))
        def _():
            leave[k, way, b] = own[:, b * 128 : (b + 1) * 128]
            line_copy(k, way, b).start()

    def turns(k, slot):
        for step in range(count - 1):
            hop = slot - step
            turn(k, 0, count - 1 - step, (n == hop) & (n < count - 1 - step), has_down)
            turn(k, 1, step, (count - 1 - n == hop) & (n > step), has_up)

    sums = [
        SquareSum(ref, square[10 * k : 10 * k + 6], square[10 * k + 6 : 10 * k + 10])
        for k, ref in enumerate((wp_part, wf_part))
    ]

    def products(total, left, right):
        def step(i, carry):
            chip = lax.rem(i, 4)
            index = chip * 2 + core + (1 - 2 * core) * (1 - i // 4)
            at = pl.ds(pl.multiple_of(index * rows, 8), rows)
            total.part_ref[index] = dot(left[at, :], right[...], 1, 1).astype(BF)

            @pl.when(i < 4)
            def _():
                total.core_copy(chip).start()

            return carry

        lax.fori_loop(0, 8, step, 0)

    block = att_ref.shape[1]
    gather = SquareGather(
        [
            (
                att_ref.at[p],
                lambda chip, p=p: atts_ref.at[p, pl.ds(pl.multiple_of(chip * block, block), block), :],
            )
            for p in range(att_ref.shape[0])
        ],
        att_send,
        att_recv,
        siblings=False,
    )
    slots = 2 * count - 3
    turns(0, 0)
    turns(1, 0)
    gather.start()
    products(sums[0], cot_ref, hidden_ref)
    sums[0].issue()
    turns(0, 1)
    products(sums[1], norm_ref, pre_ref)
    sums[1].issue()
    turns(1, 1)
    for p in range(att_ref.shape[0]):
        gather.relay(p)
    turns(0, 2)
    sums[0].middle()
    turns(1, 2)
    sums[1].middle()
    for slot in range(3, slots):
        turns(0, slot)
        turns(1, slot)
    for k, (own, out) in enumerate(lines):
        out[...] = lane_block(own, n)[...].astype(F32)
        for way, joins in ((0, has_down), (1, has_up)):

            @pl.when(joins)
            def _():
                line_copy(k, way, n).wait_recv()
                out[...] += arrive[k, way, n].astype(F32)

    shares = []
    for k, out in enumerate((wp_ref, wf_ref)):

        def write(at, size, value):
            out[core, :, at : at + size] = value.astype(BF)

        sums[k].finish(write)
        copy = remote(out.at[core], out.at[core], share_send.at[k], share_recv.at[k], "dp", 1 - core)
        copy.start()
        shares.append(copy)
    for k in range(2):
        for step in range(count - 1):

            @pl.when(n < count - 1 - step)
            def _():
                line_copy(k, 0, count - 1 - step).wait_send()

            @pl.when(n > step)
            def _():
                line_copy(k, 1, step).wait_send()

    gather.finish()
    for copy in shares:
        copy.wait()


def ffn_back_stage(part, out_part, cot, hidden, norm, pre, attended):
    count = lax.axis_size("narrow")
    width, tokens = part.shape
    hid = hidden.shape[0]
    rows = width // 8
    return pl.pallas_call(
        ffn_back_kernel,
        out_shape=(
            shape_of((width, tokens // count), F32),
            shape_of((width, tokens // count), F32),
            shape_of((2, rows, hid), BF),
            shape_of((2, rows, hid), BF),
            shape_of((attended.shape[0], 4 * attended.shape[1], attended.shape[2]), BF),
        ),
        in_specs=in_vmem(7),
        out_specs=tuple(in_vmem(5)),
        scratch_shapes=[
            pltpu.VMEM((8, rows, hid), BF),
            pltpu.VMEM((8, rows, hid), BF),
            pltpu.VMEM((2, 2, count, width, tokens // count), BF),
            pltpu.VMEM((2, 2, count, width, tokens // count), BF),
            pltpu.SemaphoreType.DMA((2, 2, count)),
            pltpu.SemaphoreType.DMA((2, 2, count)),
            pltpu.SemaphoreType.DMA((2,)),
            pltpu.SemaphoreType.DMA((2,)),
            pltpu.SemaphoreType.DMA((attended.shape[0], 7)),
            pltpu.SemaphoreType.DMA((attended.shape[0], 7)),
        ]
        + square_sum_scratch(rows, hid)
        + square_sum_scratch(rows, hid),
        compiler_params=params(5),
        cost_estimate=pl.CostEstimate(flops=4 * 10**10, bytes_accessed=10**8, transcendentals=0),
        name="ffn_back_stage",
    )(part, out_part, cot, hidden, norm, pre, attended)


TOKEN_TERMS = 5


def back_kernel(
    cot_ref, norm_ref, w_ref, att_ref, resid_ref, x_ref, dy_ref, stat_ref, gain_ref, terms_ref,
    out_ref, wq_out, wo_out, terms_out, feat_out,
    grad_ref, cots, full, other, core_in, leave, arrive,
    resid_in, columns, sums, all_sums, terms_in, terms_mid, line_terms, feat, line_feat, terms_two, terms_last,
    feat_two, feat_last,
    send_sem, recv_sem, core_send, core_recv, line_send, line_recv, share_send, share_recv,
    around_send, around_recv, along_send, along_recv,
):
    pieces, block, cols = cot_ref.shape
    feats, tokens = norm_ref.shape
    me, xp, yp, dg = square_peers()
    peers = (xp, yp, dg)
    n, count, has_down, has_up = line_sides()
    core = lax.axis_index("dp")
    others = [lax.rem(n + k, count) for k in range(1, count)]
    greet(
        [("wide", peer) for peer in peers] + [("narrow", peer) for peer in others] + [("dp", 1 - core)]
    )
    spans = halves(cols)
    ways = ((xp, yp), (yp, xp))
    rows_half = core_in.shape[1]

    def order(i):
        odd = lax.rem(i, 2)
        return (1 - odd) * (i // 2) + odd * (pieces - 1 - i // 2)

    def rows(index):
        return pl.ds(pl.multiple_of(index * block, block), block)

    def spread(i, h, k):
        p = order(i)
        span = pl.ds(*spans[h])
        first, second = ways[h]
        place = cots.at[p, rows(first if k == 2 else me), span]
        src = place if k == 2 else cot_ref.at[p, :, span]
        return remote(
            src, place, send_sem.at[h, k, p], recv_sem.at[h, k, p], "wide", first if k == 0 else second
        )

    def own(i):
        for h in range(2):
            for k in range(2):
                spread(i, h, k).start()
        p = order(i)
        cots[p, rows(me), :] = cot_ref[p]

    def around(k, src, dst, start=True):
        copies = []
        for j, peer in enumerate(peers):
            copy = remote(src(peer), dst, around_send.at[k, j], around_recv.at[k, j], "wide", peer)
            if start:
                copy.start()
            copies.append(copy)
        return copies

    def resid_moves(start):
        return around(
            1, lambda peer: resid_ref.at[pl.ds(pl.multiple_of(peer * feats, 16), feats), :], resid_in.at[me], start
        )

    def along(k, src, dst):
        copies = []
        for j, peer in enumerate(others):
            copy = remote(src, dst, along_send.at[k, j], along_recv.at[k, j], "narrow", peer)
            copy.start()
            copies.append(copy)
        return copies

    def core_copy(p):
        return remote(other.at[p], core_in.at[p], core_send.at[p], core_recv.at[p], "dp", 1 - core)

    whole = halves(full.shape[2])

    def line_copy(way, p, h):
        span = pl.ds(*whole[h])
        return remote(
            leave.at[p, :, span],
            arrive.at[way, p, :, span],
            line_send.at[p, h],
            line_recv.at[way, p, h],
            "narrow",
            n + 1 - 2 * way,
        )

    mine_rows = own_rows(rows_half)
    sibling_rows = pl.ds(pl.multiple_of((1 - core) * rows_half, 8), rows_half)
    terms_moves = around(0, lambda peer: terms_ref, terms_in.at[me])
    own(0)
    resid_moves(True)
    resid_in[me] = resid_ref[pl.ds(pl.multiple_of(me * feats, 16), feats), :]
    grad_ref[...] = jnp.zeros_like(grad_ref)
    for copy in terms_moves:
        copy.wait()
    total = terms_ref[...]
    for peer in peers:
        total = total + terms_in[peer]
    terms_mid[...] = total
    terms_moves = along(0, terms_mid, line_terms.at[n])

    def pass_on(way, p, joins):
        for h, (at, size) in enumerate(whole):

            @pl.when(joins)
            def _():
                line_copy(way, p, h).wait_recv()
                mine = full[p, mine_rows, at : at + size]
                leave[p, :, at : at + size] = (mine + arrive[way, p, :, at : at + size].astype(F32)).astype(BF)

            @pl.when(jnp.logical_not(joins))
            def _():
                leave[p, :, at : at + size] = full[p, mine_rows, at : at + size].astype(BF)

            line_copy(way, p, h).start()

    def body(i, carry):
        @pl.when(i < pieces)
        def _():
            for h in range(2):
                spread(i, h, 0).wait_recv()
                spread(i, h, 2).start()

        @pl.when(i == 0)
        def _():
            own(1)

        @pl.when(i + 2 < pieces)
        def _():
            own(i + 2)

        @pl.when(i == 1)
        def _():
            for copy in resid_moves(False):
                copy.wait()

        @pl.when((i >= 1) & (i <= pieces))
        def _():
            p = order(i - 1)
            for h in range(2):
                spread(i - 1, h, 1).wait_recv()
                spread(i - 1, h, 2).wait_recv()
            full[p, :, :cols] = dot(norm_ref[...], cots[p], 1, 0)
            total = dot(resid_in[0], att_ref[p, :block, :], 1, 0)
            for chip in range(1, 4):
                total = total + dot(resid_in[chip], att_ref[p, chip * block : (chip + 1) * block, :], 1, 0)
            full[p, :, cols:] = total
            other[p] = full[p, sibling_rows, :].astype(BF)
            core_copy(p).start()
            grad_ref[...] += dot(w_ref[p], cots[p], 1, 1)
            core_copy(p).wait()
            full[p, mine_rows, :] = full[p, mine_rows, :] + core_in[p].astype(F32)

        @pl.when(i == pieces)
        def _():
            scaled = grad_ref[...] * gain_ref[...]
            normed = (x_ref[...] - stat_ref[0:1, :]) * stat_ref[1:2, :]
            sums[0:1, :] = jnp.sum(scaled, axis=0, keepdims=True)
            sums[1:2, :] = jnp.sum(scaled * normed, axis=0, keepdims=True)
            around(2, lambda peer: sums, all_sums.at[me])

        for hop in range(count - 1):
            turn = i - 1 - hop
            p = order(turn)
            here = (turn >= 0) & (turn < pieces)

            @pl.when(here & (n < p) & (n == hop))
            def _():
                pass_on(0, p, has_down)

            @pl.when(here & (n > p) & (count - 1 - n == hop))
            def _():
                pass_on(1, p, has_up)

        return carry

    sums[...] = jnp.zeros_like(sums)
    lax.fori_loop(0, pieces + count - 1, body, 0)
    inv = stat_ref[1:2, :]
    normed = (x_ref[...] - stat_ref[0:1, :]) * inv
    grad = grad_ref[...]
    scaled = grad * gain_ref[...]
    columns[...] = jnp.zeros_like(columns)
    columns[:feats, 0:1] = jnp.sum(grad * normed, axis=1, keepdims=True)
    columns[:feats, 1:2] = jnp.sum(grad, axis=1, keepdims=True)
    columns[:feats, 2:3] = jnp.sum(dy_ref[...], axis=1, keepdims=True)
    feat[...] = jnp.transpose(columns[...])[:8, :]
    feat_moves = along(1, feat, line_feat.at[n])
    for copy in around(2, lambda peer: sums, all_sums.at[me], False):
        copy.wait()
    total = sums[...]
    for peer in peers:
        total = total + all_sums[peer]
    width = feats * 4
    back = inv * (scaled - total[0:1, :] / width - normed * (total[1:2, :] / width))
    for k in range(4):
        at = slice(k * block, (k + 1) * block)
        out_ref[:, at] = resid_in[k].astype(F32) + back[:, at]

    for copy in terms_moves + feat_moves:
        copy.wait()
    total, feat_total = terms_mid[...], feat[...]
    shared = lax.broadcasted_iota(jnp.int32, total.shape, 0) < TOKEN_TERMS
    for peer in others:
        total = total + jnp.where(shared, line_terms[peer], 0.0)
        feat_total = feat_total + line_feat[peer]
    terms_two[...] = total
    feat_two[...] = feat_total
    shares = []

    def share(k, src, dst):
        copy = remote(src, dst, share_send.at[k], share_recv.at[k], "dp", 1 - core)
        copy.start()
        shares.append(copy)

    share(2, terms_two, terms_last)
    share(3, feat_two, feat_last)
    for way, joins in ((0, has_down), (1, has_up)):

        @pl.when(joins)
        def _():
            for h in range(2):
                line_copy(way, n, h).wait_recv()
            full[n, mine_rows, :] += arrive[way, n].astype(F32)

    part = wo_out.shape[2]
    wo_out[core] = full[n, mine_rows, cols:]
    share(1, wo_out.at[core], wo_out.at[core])
    for k in range(3):
        wq_out[k, core] = full[n, mine_rows, k * part : (k + 1) * part]
        share(4 + k, wq_out.at[k, core], wq_out.at[k, core])

    def drain(i, carry):
        for h in range(2):
            for k in range(3):
                spread(i, h, k).wait_send()
        p = order(i)

        @pl.when(n < p)
        def _():
            line_copy(0, p, 0).wait_send()
            line_copy(0, p, 1).wait_send()

        @pl.when(n > p)
        def _():
            line_copy(1, p, 0).wait_send()
            line_copy(1, p, 1).wait_send()

        return carry

    lax.fori_loop(0, pieces, drain, 0)
    for copy in shares:
        copy.wait()
    terms_out[...] = total + terms_last[...]
    feat_out[...] = feat_total + feat_last[...]


def back_stage(cot, norm, w, attended, resid, x, dy, stats, gain, terms):
    pieces, block, cols = cot.shape
    count = lax.axis_size("narrow")
    feats, tokens = norm.shape
    half, part = feats // 2, cols // 3
    both = cols + part
    long = -(-feats // 128) * 128
    return pl.pallas_call(
        back_kernel,
        out_shape=(
            shape_of((feats, tokens), F32),
            shape_of((3, 2, half, part), F32),
            shape_of((2, half, part), F32),
            shape_of(terms.shape, F32),
            shape_of((8, long), F32),
        ),
        in_specs=in_vmem(10),
        out_specs=tuple(in_vmem(5)),
        scratch_shapes=[
            pltpu.VMEM((feats, tokens), F32),
            pltpu.VMEM((pieces, tokens, cols), BF),
            pltpu.VMEM((pieces, feats, both), F32),
            pltpu.VMEM((pieces, half, both), BF),
            pltpu.VMEM((pieces, half, both), BF),
            pltpu.VMEM((pieces, half, both), BF),
            pltpu.VMEM((2, pieces, half, both), BF),
            pltpu.VMEM((4, feats, block), BF),
            pltpu.VMEM((long, 128), F32),
            pltpu.VMEM((8, tokens), F32),
            pltpu.VMEM((4, 8, tokens), F32),
            pltpu.VMEM((4,) + terms.shape, F32),
            pltpu.VMEM(terms.shape, F32),
            pltpu.VMEM((count,) + terms.shape, F32),
            pltpu.VMEM((8, long), F32),
            pltpu.VMEM((count, 8, long), F32),
            pltpu.VMEM(terms.shape, F32),
            pltpu.VMEM(terms.shape, F32),
            pltpu.VMEM((8, long), F32),
            pltpu.VMEM((8, long), F32),
            pltpu.SemaphoreType.DMA((2, 3, pieces)),
            pltpu.SemaphoreType.DMA((2, 3, pieces)),
            pltpu.SemaphoreType.DMA((pieces,)),
            pltpu.SemaphoreType.DMA((pieces,)),
            pltpu.SemaphoreType.DMA((pieces, 2)),
            pltpu.SemaphoreType.DMA((2, pieces, 2)),
            pltpu.SemaphoreType.DMA((7,)),
            pltpu.SemaphoreType.DMA((7,)),
            pltpu.SemaphoreType.DMA((3, 3)),
            pltpu.SemaphoreType.DMA((3, 3)),
            pltpu.SemaphoreType.DMA((2, count - 1)),
            pltpu.SemaphoreType.DMA((2, count - 1)),
        ],
        compiler_params=params(3),
        cost_estimate=pl.CostEstimate(flops=4 * 10**10, bytes_accessed=10**8, transcendentals=0),
        name="back_stage",
    )(cot, norm, w, attended, resid, x, dy, stats, gain, terms)


def as_rows(rows):
    return jnp.concatenate([jnp.stack(rows), jnp.zeros((8 - len(rows), rows[0].shape[0]), F32)])


def own_half(values, axis):
    half = values.shape[axis] // lax.axis_size("dp")
    return lax.dynamic_slice_in_dim(values, lax.axis_index("dp") * half, half, axis)


def local(
    block_input,
    block_cotangent,
    seq_start,
    ln1_gain,
    ln1_shift,
    w_qkv,
    b_qv,
    w_out,
    b_out,
    ln2_gain,
    ln2_shift,
    w_fc,
    b_fc,
    w_proj,
    b_proj,
):
    cores, wide, narrow = lax.axis_size("dp"), lax.axis_size("wide"), lax.axis_size("narrow")
    w_index, n_index = lax.axis_index("wide"), lax.axis_index("narrow")
    feats, part = w_qkv.shape[0], w_qkv.shape[2]
    width = feats * wide
    hid = w_fc.shape[1]

    perm = []
    for w in range(wide):
        for n in range(narrow):
            block = n * wide + w
            perm.append((block, w * narrow + n))
    starts = lax.ppermute(seq_start, ("wide", "narrow"), perm)[0]
    allowed = block_mask(starts)

    def three(biases):
        zeros = jnp.zeros((narrow, 1, part), F32)
        return jnp.concatenate([biases[:, None, 0], zeros, biases[:, None, 1]], axis=2)

    square = wide == 4 and cores == 2
    if square:
        norm_t, stats, x_tok, dy_tok, vecs, biases, wo_all, wq_all, wf_ahead = front_stage(
            block_input,
            block_cotangent,
            ln1_gain[:, None],
            ln1_shift[:, None],
            as_rows([b_out, ln2_gain, ln2_shift]),
            as_rows([b_qv[0], b_qv[1]]),
            w_out,
            w_qkv.transpose(1, 0, 2),
            w_fc,
        )
        wo_all = wo_all.reshape(width, width)
        wq_all = wq_all.reshape(narrow, feats, 3 * part)
        b_out_full, gain_two_full, shift_two_full = (vecs[:, i].reshape(width) for i in range(3))
        qkv_rows, cot_all = qkv_stage(norm_t.T, wq_all, three(biases), dy_tok)
    else:
        wq_half = own_half(w_qkv, 0).astype(BF).reshape(-1, 3 * part)
        wo_half, wf_half, wp_half = (own_half(w, 0).astype(BF) for w in (w_out, w_fc, w_proj))
        wq_all = lax.all_gather(wq_half, ("narrow", "dp"), axis=0, tiled=True).reshape(narrow, feats, 3 * part)
        wo_mine = lax.all_gather(wo_half, "narrow", axis=1, tiled=True)
        wo_all = lax.all_gather(wo_mine, ("wide", "dp"), axis=0, tiled=True)
        wf_all = lax.all_gather(wf_half, ("wide", "dp"), axis=0, tiled=True)
        wp_all = lax.all_gather(wp_half, ("wide", "dp"), axis=0, tiled=True)
        b_out_full, gain_two_full, shift_two_full = lax.all_gather(
            jnp.stack([b_out, ln2_gain, ln2_shift]), "wide", axis=1, tiled=True
        )
        x_tok = to_tokens(block_input)
        dy_tok = to_tokens(block_cotangent)
        normed_one, inv_one, norm_one = norm_forward(block_input.T, ln1_gain, ln1_shift)
        qkv_part = jnp.einsum("tk,nkc->tnc", norm_one, wq_all, preferred_element_type=F32)
        qkv_rows = sum_tokens(qkv_part).transpose(1, 0, 2)
        qkv_rows = (qkv_rows + three(lax.all_gather(b_qv, "narrow", axis=0))).astype(BF)
        cot_all = gather_narrow(dy_tok.astype(BF))

    heads_all = qkv_rows.reshape(narrow, -1, 3, part).transpose(1, 2, 0, 3).reshape(-1, 3, width)
    attended, log_total = attend_forward(heads_all, allowed)
    residual = x_tok + dot(wo_all, attended, 1, 1) + b_out_full[:, None]
    mean_two = jnp.mean(residual, axis=0, keepdims=True)
    inv_two = lax.rsqrt(jnp.mean(residual * residual, axis=0, keepdims=True) - mean_two * mean_two + EPS)
    normed_two = (residual - mean_two) * inv_two
    norm_two = (normed_two * gain_two_full[:, None] + shift_two_full[:, None]).astype(BF)
    if square:
        norm_two_all, wf_all, wp_all = pair_stage(norm_two, wf_ahead, w_fc, w_proj)
        wf_all, wp_all = wf_all.reshape(width, hid), wp_all.reshape(width, hid)
    else:
        norm_two_all = gather_narrow(norm_two)
    pre_act = dot(wf_all, norm_two_all, 0, 0) + b_fc[:, None]
    hidden = gelu_value(pre_act).astype(BF)
    pre_grad = dot(wp_all, cot_all, 0, 0) * gelu_slope(pre_act)
    pre_cot = pre_grad.astype(BF)
    norm_two_part = dot(wf_all, pre_cot, 1, 0)

    def reduce_wide(grad):
        return lax.psum_scatter(grad.astype(BF), ("wide", "dp"), scatter_dimension=0, tiled=True)

    def share(total):
        return lax.all_gather(total, "dp", axis=0, tiled=True).astype(F32)

    if square:
        norm_two_grad, out_sum, grad_w_proj, grad_w_fc, attended_all = ffn_back_stage(
            norm_two_part.astype(BF),
            dot(wp_all, hidden, 1, 0).astype(BF),
            cot_all,
            hidden,
            norm_two_all,
            pre_cot,
            attended.reshape(-1, narrow, part).transpose(1, 0, 2),
        )
        grad_w_fc = grad_w_fc.astype(F32).reshape(w_fc.shape)
        grad_w_proj = grad_w_proj.astype(F32).reshape(w_proj.shape)
    else:
        norm_two_grad = sum_narrow(norm_two_part)
        out_sum = sum_narrow(dot(wp_all, hidden, 1, 0))
        grad_w_proj = share(reduce_wide(dot(cot_all, hidden, 1, 1)))
        grad_w_fc = share(reduce_wide(dot(norm_two_all, pre_cot, 1, 1)))
    output = to_features((residual + out_sum).astype(BF)).astype(F32) + b_proj[:, None]

    scaled = norm_two_grad * gain_two_full[:, None]
    mean_scaled = jnp.mean(scaled, axis=0, keepdims=True)
    mean_cross = jnp.mean(scaled * normed_two, axis=0, keepdims=True)
    resid_grad = dy_tok.astype(F32) + inv_two * (scaled - mean_scaled - normed_two * mean_cross)
    resid_cot = resid_grad.astype(BF)
    attended_cot = dot(resid_cot, wo_all, 0, 0).astype(BF)

    qkv_grad = attend_backward(heads_all, allowed, log_total, attended_cot)
    qkv_cot = qkv_grad.astype(BF).reshape(-1, 3, narrow, part).transpose(2, 0, 1, 3)
    qkv_cot = qkv_cot.reshape(narrow, -1, 3 * part)
    qkv_sums = jnp.sum(qkv_grad, axis=0)
    wide_terms = as_rows(
        [
            qkv_sums[0],
            qkv_sums[2],
            jnp.sum(resid_grad, axis=1),
            jnp.sum(norm_two_grad * normed_two, axis=1),
            jnp.sum(norm_two_grad, axis=1),
        ]
    )
    fc_terms = jnp.sum(pre_grad, axis=1)
    if square:
        span = max(width, hid)
        packed = jnp.zeros((8, span), F32)
        packed = packed.at[:, :width].set(wide_terms).at[TOKEN_TERMS, :hid].set(fc_terms)
        grad_input, grad_w_qkv, grad_w_out, packed_sum, feat_sum = back_stage(
            qkv_cot,
            norm_t,
            wq_all,
            attended_all,
            resid_cot,
            block_input,
            block_cotangent,
            stats,
            ln1_gain[:, None],
            packed,
        )
        grad_w_qkv = grad_w_qkv.reshape(3, feats, part).transpose(1, 0, 2)
        grad_w_out = grad_w_out.reshape(feats, part)
        token_sum = packed_sum[:TOKEN_TERMS, :width]
        grad_b_fc = packed_sum[TOKEN_TERMS, :hid]
        gain_one, shift_one, proj_bias = (feat_sum[i, :feats] for i in range(3))
    else:
        qkv_cot_all = lax.all_gather(qkv_cot, "wide", axis=1, tiled=True)
        wq_grad = jnp.einsum("tk,ntc->nkc", norm_one, qkv_cot_all, preferred_element_type=F32).astype(BF)
        wq_grad = lax.psum_scatter(
            wq_grad.reshape(narrow * feats, 3 * part), ("narrow", "dp"), scatter_dimension=0, tiled=True
        )
        grad_w_qkv = share(wq_grad).reshape(feats, 3, part)
        wo_grad = reduce_wide(dot(resid_cot, attended, 1, 0))
        wo_grad = lax.psum_scatter(wo_grad, "narrow", scatter_dimension=1, tiled=True)
        grad_w_out = share(wo_grad)
        norm_one_grad = jnp.einsum("nkc,ntc->tk", wq_all, qkv_cot_all, preferred_element_type=F32)
        grad_input = to_features(resid_grad) + norm_backward(norm_one_grad, normed_one, inv_one, ln1_gain).T
        feature_terms = jnp.stack(
            [
                jnp.sum(norm_one_grad * normed_one, axis=0),
                jnp.sum(norm_one_grad, axis=0),
                jnp.sum(block_cotangent, axis=1),
            ]
        )
        feature_full = lax.dynamic_update_slice_in_dim(
            jnp.zeros((3, width), F32), feature_terms, w_index * feats, 1
        )
        fc_full = lax.dynamic_update_slice_in_dim(jnp.zeros((narrow * hid,), F32), fc_terms, n_index * hid, 0)
        token_sum, feature_sum, fc_sum = lax.psum((wide_terms, feature_full, fc_full), ("dp", "wide", "narrow"))
        gain_one, shift_one, proj_bias = lax.dynamic_slice_in_dim(feature_sum, w_index * feats, feats, 1)
        grad_b_fc = lax.dynamic_slice_in_dim(fc_sum, n_index * hid, hid, 0)
    grad_b_qv = lax.dynamic_slice_in_dim(token_sum[:2], n_index * part, part, 1)
    out_bias, gain_two, shift_two = lax.dynamic_slice_in_dim(token_sum[2:5], w_index * feats, feats, 1)
    return (
        output,
        grad_input,
        gain_one,
        shift_one,
        grad_w_qkv,
        grad_b_qv,
        grad_w_out,
        out_bias,
        gain_two,
        shift_two,
        grad_w_fc,
        grad_b_fc,
        grad_w_proj,
        proj_bias,
    )


def solution(mesh):
    return jax.shard_map(
        local,
        mesh=mesh,
        in_specs=(
            P("wide", ("dp", "narrow")),
            P("wide", ("dp", "narrow")),
            P(("dp", "wide", "narrow"), None),
            P("wide"),
            P("wide"),
            P("wide", None, "narrow"),
            P(None, "narrow"),
            P("wide", "narrow"),
            P("wide"),
            P("wide"),
            P("wide"),
            P("wide", "narrow"),
            P("narrow"),
            P("wide", "narrow"),
            P("wide"),
        ),
        out_specs=(
            P("wide", ("dp", "narrow")),
            P("wide", ("dp", "narrow")),
            P("wide"),
            P("wide"),
            P("wide", None, "narrow"),
            P(None, "narrow"),
            P("wide", "narrow"),
            P("wide"),
            P("wide"),
            P("wide"),
            P("wide", "narrow"),
            P("narrow"),
            P("wide", "narrow"),
            P("wide"),
        ),
        check_vma=False,
    )
```

time: 564 us -> 452 us (0.80)
  waiting for transfers between devices: 50.2 us -> 0.38 us
  local copies, waits for them, and re-layouts: 59.8 us -> 24.8 us
  matrix products: 75.1 us -> 44.6 us
  Pallas kernels: 331 us -> 353 us
  between operations: 14.4 us -> 1.5 us
    pallas_call x2, Pallas kernels: 76.9 us -> 122 us  [the longest x1 73.7 us: ffn_back_stage(): pl.pallas_call(ffn_back_kernel, out_shape=(shape_of((width, tokens // cou...]
    reduce_scatter x2 -> x0, waiting for transfers between devices: 40.3 us -> none  [sum_narrow(): lax.psum_scatter(partial_value.astype(BF), 'narrow', scatter_dimension=0,...]
    pallas_call x1, Pallas kernels: 137 us -> 110 us  [back_stage(): pl.pallas_call(back_kernel, out_shape=(shape_of((feats, tokens), F32), sh...]
    dot_general x9 -> x6, matrix products: 53.8 us -> 29.9 us  [dot(): lax.dot_general(a, b, (((ca,), (cb,)), ((), ())), preferred_element_type=...]
    convert_element_type x6 -> x1, local copies, waits for them, and re-layouts: 12.2 us -> 1.01 us  [attend_forward(): attended.reshape(heads_all.shape[0], HEADS * HEAD).astype(BF)]
    all_to_all x2 -> x1, waiting for transfers between devices: 9.78 us -> 0.38 us  [to_features(): lax.all_to_all(values, 'wide', split_axis=0, concat_axis=1, tiled=True)]
    unnamed x77 -> x45, local copies, waits for them, and re-layouts: 14 us -> 5.6 us
    reshape x2 -> x0, local copies, waits for them, and re-layouts: 6.51 us -> none  [the longest x1 5.49 us: local(): grad_w_qkv = grad_w_qkv.reshape(feats, 3, part)]
  transfers between devices with their start and end apart: 7 -> 2, of which waited for: 3 -> 1; matrix products, arithmetic and copies ran while one was open for 19% -> 4% of each run, Pallas kernels for 46% -> 27%
where the time goes in v5:
time: 452 us; the launch traced here: 444 us
  Pallas kernels  353 us (78%)
  matrix products  44.6 us (10%)
  local copies, waits for them, and re-layouts  24.8 us (5%)
  other arithmetic  13.3 us (3%)
  starting transfers between devices  6.38 us (1%)
    pallas_call x1, Pallas kernels, back_stage(): pl.pallas_call(back_kernel, out_shape=(shape_of((feats, tokens), F32), sh...  110 us
    pallas_call x1, Pallas kernels, ffn_back_stage(): pl.pallas_call(ffn_back_kernel, out_shape=(shape_of((width, tokens // cou...  73.7 us
    pallas_call x1, Pallas kernels, front_stage(): pl.pallas_call(front_kernel, out_shape=(shape_of((feats, tokens), BF), sh...  64.8 us
    pallas_call x1, Pallas kernels, qkv_stage(): pl.pallas_call(qkv_kernel, out_shape=(shape_of((pieces, block, cols), BF)...  56.1 us
    pallas_call x1, Pallas kernels, pair_stage(): pl.pallas_call(pair_kernel, out_shape=(shape_of((own.shape[0], count * ow...  48.4 us
    dot_general x6, matrix products, dot(): lax.dot_general(a, b, (((ca,), (cb,)), ((), ())), preferred_element_type=...  29.9 us
  transfers between devices with their start and end apart: 2, of which 1 were waited for; matrix products, arithmetic and copies ran while one was open for 4% of the time, Pallas kernels for 27%

profile of v5, /device:TPU:17, one launch (start us, length us, event | category | flops | bytes accessed | tf_op | source)
XLA Modules:
  0.0 444.3 jit_solution(14340468763726216966)
XLA Ops:
  0.6 2.9 collective-permute-start
  9.3 64.8 %front_stage.1 = (bf16[400,512]{1,0:T(8,128)(2,1)}, f32[8,512]{1,0:T(8,128)}, f32[1600,128]{1,0:T(8,128)}, bf16[1600,128]{1,0:T(8,128)(2,1)}, f32[4,8,400]{2,1,0...) custom-call(f32[400,512]{1,0:T(8,128)} %x_ref.3, ...), custom_call_target="tpu_custom_call" | custom-call | flops 10000000000 | bytes 60000000 | tf_op jit(solution)/shard_map/front_stage/pallas_call | solution.py:420
  75.3 2.0 copy.40
  78.0 56.1 %qkv_stage.1 = (bf16[4,128,1200]{2,1,0:T(8,128)(2,1)}, bf16[1600,512]{1,0:T(8,128)(2,1)}) custom-call(bf16[512,400]{1,0:T(8,128)(2,1)} %bitcast.120, bf16[4,400,1200]{2,1,0:T(8,128)(2,1)} %bitcast.143, f32[4,1,1200]{2,1,0:T(1,128)} %concatenate.22.bias_ref, bf16[1600,128]{1,0:T(8,128)(2,1)} %get-tuple-element.75.dy_ref), custom_call_target="tpu_custom_call" | custom-call | flops 30000001024 | bytes 100000000 | tf_op jit(solution)/shard_map/qkv_stage/pallas_call | solution.py:525
  134.2 1.8 copy.41
  136.8 2.2 fusion.9
  139.8 4.3 fusion.59
  145.3 48.4 %pair_stage.1 = (bf16[1600,512]{1,0:T(8,128)(2,1)}, bf16[8,200,1600]{2,1,0:T(8,128)(2,1)}, bf16[8,200,1600]{2,1,0:T(8,128)(2,1)}) custom-call(bf16[1600,128]{1,0:T(8,128)(2,1)} %add_convert_fusion.1.own_ref, bf16[8,200,768]{2,1,0:T(8,128)(2,1)} %get-tuple-element.78.ahead_ref, f32[400,1600]{1,0:T(8,128)} %wf_ref.3, f32[400,1600]{1,0:T(8,128)} %wp_ref.1), custom_call_target="tpu_custom_call" | custom-call | flops 20000000000 | bytes 70000000 | tf_op jit(solution)/shard_map/pair_stage/pallas_call | solution.py:579
  193.8 7.2 %multiply_convert_fusion = (bf16[1600,512]{1,0:T(8,128)(2,1)S(1)}, f32[1600,512]{1,0:T(8,128)S(1)}) fusion(f32[1600]{0:T(1024)S(1)} %copy-done.14, bf16[1600,1600]{1,0:T(8,128)(2,1)} %bitcast.139, bf16[1600,512]{1,0:T(8,128)(2,1)} %get-tuple-element.82.norm_ref), kind=kOutput, calls=%fused_computation.10 | convolution fusion | flops 2629632000 | bytes 11680000 | tf_op jit(solution)/shard_map/dot_general | solution.py:33
  201.0 5.3 %fusion.60 = (f32[1600]{0:T(1024)S(1)}, bf16[1600,512]{1,0:T(8,128)(2,1)S(1)}) fusion(f32[1600,512]{1,0:T(8,128)S(1)} %get-tuple-element.126, bf16[1600,1600]{1,0:T(8,128)(2,1)S(1)} %bitcast.137, bf16[1600,512]{1,0:T(8,128)(2,1)S(1)} %copy-done.18), kind=kOutput, calls=%fused_computation.82 | convolution fusion | flops 2637822464 | bytes 11680000 | tf_op jit(solution)/shard_map/dot_general | solution.py:33
  206.3 4.2 convolution_convert_fusion.1.part_ref
  210.5 4.2 convolution_convert_fusion.out_part_ref
  215.7 73.7 %ffn_back_stage.1 = (f32[1600,128]{1,0:T(8,128)}, f32[1600,128]{1,0:T(8,128)}, bf16[2,200,1600]{2,1,0:T(8,128)(2,1)}, bf16[2,200,1600]{2,1,0:T(8,128)(2,1)}, bf16[4,512,400]{2,1,0:T(8,128)(2,1)}) custom-call(bf16[1600,512]{1,0:T(8,128)(2,1)} %convolution_convert_fusion.1.part_ref, bf16[1600,512]{1,0:T(8,128)(2,1)} %convolution_convert_fusion.out_part_ref, ...), custom_call_target="tpu_custom_call" | custom-call | flops 40000000000 | bytes 100000000 | tf_op jit(solution)/shard_map/ffn_back_stage/pallas_call | solution.py:827
  289.5 1.6 multiply_reduce_fusion.4
  292.4 4.8 %convolution_convert_fusion.2 = bf16[128,1600]{0,1:T(8,128)(2,1)S(1)} fusion(bf16[1600,128]{1,0:T(8,128)(2,1)S(1)} %get-tuple-element.106.resid_ref, bf16[1600,1600]{1,0:T(8,128)(2,1)} %bitcast.98), kind=kOutput, calls=%fused_computation.17 | convolution fusion | flops 655564800 | bytes 5939200 | tf_op jit(solution)/shard_map/dot_general | solution.py:33
  297.2 3.7 bitcast_convert_fusion.2
  301.4 3.6 bitcast_convert_fusion.3
  305.0 3.5 bitcast_convert_fusion.4
  311.4 1.9 maximum_reduce_fusion
  314.6 110.3 %back_stage.1 = (f32[400,512]{1,0:T(8,128)}, f32[3,2,200,400]{3,2,1,0:T(8,128)}, f32[2,200,400]{2,1,0:T(8,128)}, f32[8,1600]{1,0:T(8,128)}, f32[8,512]{1,0:T(8,128)}) custom-call(bf16[4,128,1200]{2,1,0:T(8,128)(2,1)} %copy.52.cot_ref, bf16[400,512]{1,0:T(8,128)(2,1)} %get-tuple-element.72.norm_ref, bf16[4,400,1200]{2,1,0:T(8,128)(2,1)} %bitcast.144, ...), custom_call_target="tpu_custom_call" | custom-call | flops 40000000000 | bytes 100000000 | tf_op jit(solution)/shard_map/back_stage/pallas_call | solution.py:1124
  428.0 3.5 all-to-all-start
  431.5 1.8 bitcast_convert_fusion.1
  433.3 1.8 bitcast_convert_fusion
  439.2 2.1 copy.64
  (88 shorter events, 27.1 us)
Async XLA Ops:
  0.6 136.1 %collective-permute-start = (s32[1,128]{1,0:T(1,128)}, s32[1,128]{1,0:T(1,128)S(1)}, u32[]{:S(2)}, u32[]{:S(2)}) collective-permute-start(s32[1,128]{1,0:T(1,128)} %param.23), channel_id=1, source_target_pairs={{0,0},{4,1},{8,2},{12,3},{1,4},{5,5},{9,6},{13,7},{2,8},{6,9},{10,... | collective-permute-start | bytes 1544 | tf_op jit(solution)/shard_map/ppermute | solution.py:1212
  136.5 2.5 copy-start.3
  145.3 48.4 %copy-start.14 = (f32[1600]{0:T(1024)S(1)}, f32[1600]{0:T(1024)}, u32[]{:S(2)}) copy-start(f32[1600]{0:T(1024)} %param.33) | copy-start | bytes 19204
  193.7 7.2 %copy-start.15 = (bf16[8,200,1600]{2,1,0:T(8,128)(2,1)S(1)}, bf16[8,200,1600]{2,1,0:T(8,128)(2,1)}, u32[]{:S(2)}) copy-start(bf16[8,200,1600]{2,1,0:T(8,128)(2,1)} %get-tuple-element.80) | copy-start | bytes 15360004
  193.8 7.2 %copy-start.18 = (bf16[1600,512]{1,0:T(8,128)(2,1)S(1)}, bf16[1600,512]{1,0:T(8,128)(2,1)}, u32[]{:S(2)}) copy-start(bf16[1600,512]{1,0:T(8,128)(2,1)} %get-tuple-element.81.cot_ref) | copy-start | bytes 4915204
  193.8 12.5 %slice-start = ((s8[5324800]{0:T(1024)(128)(4,1)}), s8[4194304]{0:T(1024)(128)(4,1)S(1)}, s32[]{:S(2)}) async-start(s8[5324800]{0:T(1024)(128)(4,1)} %bitcast.140), calls=%async_computation.1 | async-start | bytes 8388608
  200.9 9.6 %copy-start.16 = (bf16[1600,512]{1,0:T(8,128)(2,1)}, bf16[1600,512]{1,0:T(8,128)(2,1)S(1)}, u32[]{:S(2)}) copy-start(bf16[1600,512]{1,0:T(8,128)(2,1)S(1)} %get-tuple-element.125.hidden_ref) | copy-start | bytes 4915204
  201.0 5.3 %slice-start.1 = ((s8[5324800]{0:T(1024)(128)(4,1)}), s8[1130496]{0:T(1024)(128)(4,1)S(1)}, s32[]{:S(2)}) async-start(s8[5324800]{0:T(1024)(128)(4,1)} %bitcast.140), calls=%async_computation.2 | async-start | bytes 2260992
  206.3 4.2 copy-start.17
  215.7 75.4 %copy-start.10 = (bf16[1600,128]{1,0:T(8,128)(2,1)S(1)}, bf16[1600,128]{1,0:T(8,128)(2,1)}, u32[]{:S(2)}) copy-start(bf16[1600,128]{1,0:T(8,128)(2,1)} %get-tuple-element.75.dy_ref) | copy-start | bytes 1228804
  289.4 1.6 copy-start
  289.5 1.6 copy-start.7
  292.4 4.8 %copy-start.2 = (bf16[1600,128]{1,0:T(8,128)(2,1)}, bf16[1600,128]{1,0:T(8,128)(2,1)S(1)}, u32[]{:S(2)}) copy-start(bf16[1600,128]{1,0:T(8,128)(2,1)S(1)} %get-tuple-element.106.resid_ref) | copy-start | bytes 1228804
  305.0 3.5 copy-start.11
  309.8 1.5 copy-start.8
  309.8 1.6 copy-start.9
  313.9 0.6 copy-start.12
  314.6 116.9 %copy-start.5 = (bf16[2,200,1600]{2,1,0:T(8,128)(2,1)S(1)}, bf16[2,200,1600]{2,1,0:T(8,128)(2,1)}, u32[]{:S(2)}) copy-start(bf16[2,200,1600]{2,1,0:T(8,128)(2,1)} %get-tuple-element.92) | copy-start | bytes 3840004
  428.0 10.2 %all-to-all-start = ((bf16[4,400,128]{2,1,0:T(8,128)(2,1)}), bf16[4,400,128]{2,1,0:T(8,128)(2,1)S(1)}, u32[]{:S(2)}, u32[]{:S(2)}) async-start(bf16[4,400,128]{2,1,0:T(8,128)(2,1)} %bitcast.22), calls=%async_computation | async-start | bytes 819200 | tf_op jit(solution)/shard_map/all_to_all | solution.py:76
  431.5 1.8 copy-start.4
  433.3 4.9 %copy-start.13 = (f32[400]{0:T(512)S(1)}, f32[400]{0:T(512)}, u32[]{:S(2)}) copy-start(f32[400]{0:T(512)} %param.35) | copy-start | bytes 4804
  435.0 6.2 %copy-start.1 = (f32[3,2,200,400]{3,2,1,0:T(8,128)S(1)}, f32[3,2,200,400]{3,2,1,0:T(8,128)}, u32[]{:S(2)}) copy-start(f32[3,2,200,400]{3,2,1,0:T(8,128)} %get-tuple-element.89) | copy-start | bytes 5760004
  441.3 1.7 copy-start.6
